TPU v7x, 128 devices: a whole 4x4x4 slice. The times are simulated.
128 devices in a mesh: grp: 4 (over z), dev: 32 (over y, x, core).
Axes of the slice: x: 4, y: 4, z: 4, core: 2. Of those that a mesh axis runs over, the one named last changes fastest.
Arguments:
- old_state: float32 [32768, 4, 512], P(('grp', 'dev')), may hold values from -6 to 6
- dest_row: int32 [32768], P(('grp', 'dev')), may hold values from -1 to 16383, as said below
- neighbours: int32 [6, 16384], P(None, ('grp', 'dev')), may hold values from 0 to 16383, as said below
- orientation: int32 [6, 16384], P(None, ('grp', 'dev')), may hold values from 0 to 7
- wall_flags: int32 [6, 16384], P(None, ('grp', 'dev')), may hold values from 0 to 1, as said below
- bulk_modulus: float32 [16384], P(('grp', 'dev')), may hold values from 0.5 to 2
- density: float32 [16384], P(('grp', 'dev')), may hold values from 0.5 to 2
Outputs:
- tendency: float32 [16384, 4, 512], P(('grp', 'dev'))
Inputs may be any that keep to these rules, and one draw needn't show every extreme that they name: `dest_row`: each of the 16384 new rows appears exactly once. On half of the devices every slot is used, on the others every slot is -1. The slots of one device whose new rows lie on one device number either 0 or 8. The elements form a grid of 16 x 32 x 32 cubes along x, y, z, cut into blocks of 4 x 4 x 8, faces 0 to 5 looking to -x, +x, -y, +y, -z, +z; a face on the grid's outside has the row itself as neighbour. If neighbours[f, r] = m differs from r then neighbours[f xor 1, m] = r. Each device holds the rows of one whole block, in rows 128 * i to 128 * (i + 1) - 1 for device index i = g * 32 + d (g of grp, d of dev); which block lies on which device is arbitrary. One device's rows and faces have at most 32 neighbours on any one other device. wall_flags[f, r] is 1 exactly where neighbours[f, r] = r.
All inputs are finite; a program needn't handle non-finite values.
Results may differ from a plain program's by a relative error of at most 0.0001.
Values sent between devices are 32-bit elements; how exact they have to be, the bound alone decides.
No kernel may reach another device: no remote copies, remote signals or barrier semaphores. Data moves between devices by JAX's collectives and lax.ppermute only.
A program may use at most 128 MiB of HBM per device.

v0:
```python
import jax
import jax.numpy as jnp
import numpy as np
from jax import lax
from jax.sharding import PartitionSpec as P

NP = 8
PIECES = 16
HCAP = 32


metric_scale = 0.25


def gll_tables(poly_order):
    num_points = poly_order + 1
    points = -np.cos(np.pi * np.arange(num_points) / poly_order)
    legendre = np.zeros((num_points, num_points))
    for sweeps in range(101):
        legendre[:, 0] = 1.0
        legendre[:, 1] = points
        for degree in range(2, num_points):
            legendre[:, degree] = (
                (2 * degree - 1) * points * legendre[:, degree - 1]
                - (degree - 1) * legendre[:, degree - 2]
            ) / degree
        if sweeps < 100:
            points = points - (points * legendre[:, poly_order] - legendre[:, poly_order - 1]) / (
                num_points * legendre[:, poly_order]
            )
    end_values = legendre[:, poly_order]
    weights = 2.0 / (poly_order * num_points * end_values**2)
    distance = points[:, None] - points[None, :] + np.eye(num_points)
    derivative = end_values[:, None] / end_values[None, :] / distance
    derivative = derivative * (1.0 - np.eye(num_points))
    derivative[0, 0] = -poly_order * num_points / 4.0
    derivative[poly_order, poly_order] = poly_order * num_points / 4.0
    return (points, weights, derivative)


def face_index(face_id):
    picked = [slice(None), slice(None), slice(None)]
    picked[face_id // 2] = 0 if face_id % 2 == 0 else NP - 1
    return tuple(picked)


def face_traces(volume):
    return jnp.stack(
        [volume[(slice(None), slice(None)) + face_index(face_id)] for face_id in range(6)]
    )


def orient_trace(values, orient_code):
    shaped = orient_code[:, None, None, None]
    values = jnp.where(shaped % 2 == 1, values[:, :, ::-1, :], values)
    values = jnp.where(shaped // 2 % 2 == 1, values[:, :, :, ::-1], values)
    return jnp.where(shaped >= 4, jnp.swapaxes(values, 2, 3), values)


def derivative_along(scalar_field, matrix, axis_id):
    einsum_forms = ["ai,eijk->eajk", "aj,eijk->eiak", "ak,eijk->eija"]
    return jnp.einsum(einsum_forms[axis_id], matrix, scalar_field, precision=lax.Precision.HIGHEST)


def right_side(
    volume,
    inner_faces,
    outer_faces,
    outer_impedance,
    orientation,
    wall_flags,
    bulk_modulus,
    density,
):
    points, weights, derivative = gll_tables(NP - 1)
    matrix = jnp.asarray(derivative, jnp.float32)
    lift_factor = metric_scale / float(weights[0])
    bulk_vol = bulk_modulus[:, None, None, None]
    dens_vol = density[:, None, None, None]
    divergence = (
        derivative_along(volume[:, 1], matrix, 0)
        + derivative_along(volume[:, 2], matrix, 1)
        + derivative_along(volume[:, 3], matrix, 2)
    )
    pieces_list = [-metric_scale * bulk_vol * divergence]
    for axis_id in range(3):
        pieces_list.append(
            -(metric_scale / dens_vol) * derivative_along(volume[:, 0], matrix, axis_id)
        )
    result = jnp.stack(pieces_list, axis=1)
    inner_impedance = jnp.sqrt(bulk_modulus * density)
    for face_id in range(6):
        axis_id = face_id // 2
        normal_sign = 2.0 * (face_id % 2) - 1.0
        own_face = inner_faces[face_id]
        far_face = orient_trace(outer_faces[face_id], orientation[face_id])
        is_wall = wall_flags[face_id] == 1
        wall_face = is_wall[:, None, None]
        press_in = own_face[:, 0]
        normal_in = normal_sign * own_face[:, 1 + axis_id]
        press_out = jnp.where(wall_face, press_in, far_face[:, 0])
        normal_out = jnp.where(wall_face, -normal_in, normal_sign * far_face[:, 1 + axis_id])
        imped_in = inner_impedance[:, None, None]
        imped_out = jnp.where(is_wall, inner_impedance, outer_impedance[face_id])[:, None, None]
        imped_sum = imped_in + imped_out
        press_star = (
            imped_out * press_in
            + imped_in * press_out
            + imped_in * imped_out * (normal_in - normal_out)
        ) / imped_sum
        normal_star = (
            imped_in * normal_in + imped_out * normal_out + press_in - press_out
        ) / imped_sum
        result = result.at[(slice(None), 0) + face_index(face_id)].add(
            -lift_factor * bulk_modulus[:, None, None] * (normal_star - normal_in)
        )
        result = result.at[(slice(None), 1 + axis_id) + face_index(face_id)].add(
            -(normal_sign * lift_factor) * (press_star - press_in) / density[:, None, None]
        )
    return result.reshape(result.shape[0], 4, -1)


def body(old_state, dest_row, neighbours, orientation, wall_flags, bulk_modulus, density):
    elem_dev = bulk_modulus.shape[0]
    groups = lax.axis_size("grp")
    members = lax.axis_size("dev")
    devices = groups * members
    per_pair = elem_dev // PIECES
    is_used = dest_row >= 0
    dest_dev = jnp.where(is_used, dest_row // elem_dev, -1)
    match_grid = (dest_dev[:, None] == jnp.arange(devices)[None, :]).astype(jnp.int32)
    before = jnp.cumsum(match_grid, axis=0) - match_grid
    within = jnp.sum(before * match_grid, axis=1)
    slot_at = jnp.where(is_used, dest_dev * per_pair + within, devices * per_pair)
    outgoing = (
        jnp.zeros((devices * per_pair, 4, old_state.shape[2]), jnp.float32)
        .at[slot_at]
        .set(old_state, mode="drop")
    )
    labels = (
        jnp.zeros((devices * per_pair,), jnp.int32)
        .at[slot_at]
        .set(dest_row % elem_dev + 1, mode="drop")
    )
    arrived, arrived_lab = (
        lax.all_to_all(outgoing, ("grp", "dev"), split_axis=0, concat_axis=0, tiled=True),
        lax.all_to_all(labels, ("grp", "dev"), split_axis=0, concat_axis=0, tiled=True),
    )
    place_at = jnp.where(arrived_lab > 0, arrived_lab - 1, elem_dev)
    new_state = (
        jnp.zeros((elem_dev, 4, old_state.shape[2]), jnp.float32)
        .at[place_at]
        .set(arrived, mode="drop")
    )
    volume = new_state.reshape(elem_dev, 4, NP, NP, NP)
    inner_faces = face_traces(volume)
    flat_inner = inner_faces.reshape(6, elem_dev, 4 * NP * NP)
    face_width = flat_inner.shape[2]
    impedance = jnp.sqrt(bulk_modulus * density)
    my_index = lax.axis_index("grp") * members + lax.axis_index("dev")
    owner_dev = neighbours // elem_dev
    local_row = neighbours - owner_dev * elem_dev
    remote = (owner_dev != my_index) & (wall_flags == 0)
    near_row = jnp.where(remote, 0, local_row)
    outer_faces = jnp.stack([flat_inner[face_id ^ 1][near_row[face_id]] for face_id in range(6)])
    outer_impedance = impedance[near_row]
    slot_count = HCAP
    remote_flat = remote.reshape(-1)
    owner_flat = owner_dev.reshape(-1)
    match_owner = (
        (owner_flat[:, None] == jnp.arange(devices)[None, :]) & remote_flat[:, None]
    ).astype(jnp.int32)
    owner_before = jnp.cumsum(match_owner, axis=0) - match_owner
    owner_rank = jnp.sum(owner_before * match_owner, axis=1)
    ask_slot = jnp.where(remote_flat, owner_flat * slot_count + owner_rank, devices * slot_count)
    ask_value = ((jnp.arange(6) ^ 1)[:, None] * elem_dev + local_row).reshape(-1) + 1
    requests_out = (
        jnp.zeros((devices * slot_count,), jnp.int32).at[ask_slot].set(ask_value, mode="drop")
    )
    trace_table = flat_inner.reshape(6 * elem_dev, face_width)
    incoming = lax.all_to_all(requests_out, ("grp", "dev"), split_axis=0, concat_axis=0, tiled=True)
    serve_at = jnp.maximum(incoming - 1, 0)
    asked = (incoming > 0).astype(jnp.float32)
    answer = trace_table[serve_at] * asked[:, None]
    answer_imped = impedance[serve_at % elem_dev] * asked
    back_trace, back_imped = (
        lax.all_to_all(answer, ("grp", "dev"), split_axis=0, concat_axis=0, tiled=True),
        lax.all_to_all(answer_imped, ("grp", "dev"), split_axis=0, concat_axis=0, tiled=True),
    )
    take_at = jnp.minimum(ask_slot, devices * slot_count - 1)
    outer_faces = jnp.where(
        remote[:, :, None], back_trace[take_at].reshape(6, elem_dev, face_width), outer_faces
    )
    outer_impedance = jnp.where(remote, back_imped[take_at].reshape(6, elem_dev), outer_impedance)
    outer_shaped = outer_faces.reshape(6, elem_dev, 4, NP, NP)
    return right_side(
        volume,
        inner_faces,
        outer_shaped,
        outer_impedance,
        orientation,
        wall_flags,
        bulk_modulus,
        density,
    )


def solution(mesh):
    in_specs = (
        P(("grp", "dev"), None, None),
        P(("grp", "dev")),
        P(None, ("grp", "dev")),
        P(None, ("grp", "dev")),
        P(None, ("grp", "dev")),
        P(("grp", "dev")),
        P(("grp", "dev")),
    )
    out_specs = P(("grp", "dev"), None, None)
    return jax.shard_map(body, mesh=mesh, in_specs=in_specs, out_specs=out_specs, check_vma=False)
```

profile of v0, /device:TPU:1, one launch (start us, length us, event | category | flops | bytes accessed | tf_op | source)
XLA Modules:
  0.0 374.7 jit_solution(12423309612712494848)
XLA Ops:
  0.0 0.8 add_bitcast_fusion
  1.6 0.4 fusion.10
  2.0 3.4 scatter_custom_fusion.3
  5.4 0.7 all_to_all.30
  6.1 11.5 %all-to-all-start.2 = ((s32[128,32,1]{1,2,0:T(1,128)}), s32[128,32,1]{1,2,0:T(1,128)S(1)}, u32[]{:S(2)}, u32[]{:S(2)}) async-start(s32[128,32,1]{1,2,0:T(1,128)} %bitcast.31), calls=%async_computation.2 | async-start | bytes 131072 | tf_op jit(solution)/shard_map/all_to_all | solution.py:181
  17.6 0.7 fusion.113
  18.3 0.7 fusion.64
  19.7 0.6 broadcast_multiply_fusion.2
  20.2 1.4 scatter_custom_fusion
  21.7 0.7 all_to_all.27
  22.4 4.9 %all-to-all-done.2 = s32[128,32,1]{1,2,0:T(1,128)S(1)} async-done(((s32[128,32,1]{1,2,0:T(1,128)}), s32[128,32,1]{1,2,0:T(1,128)S(1)}, u32[]{:S(2)}, u32[]{:S(2)}) %all-to-all-start.2) | async-done | bytes 16416 | tf_op jit(solution)/shard_map/all_to_all | solution.py:181
  27.3 4.9 %all-to-all-start = ((s32[128,8,1]{1,2,0:T(1,128)}), s32[128,8,1]{1,2,0:T(1,128)S(1)}, u32[]{:S(2)}, u32[]{:S(2)}) async-start(s32[128,8,1]{1,2,0:T(1,128)} %bitcast.4), calls=%async_computation | async-start | bytes 131072 | tf_op jit(solution)/shard_map/all_to_all | solution.py:147
  32.4 24.7 %gather_fusion = f32[4096]{0:T(1024)S(1)} fusion(f32[128]{0:T(128)S(1)} %get-tuple-element.271, s32[4096]{0:T(1024)S(1)} %get-tuple-element.282), kind=kCustom, calls=%fused_computation | custom fusion | bytes 49152 | tf_op jit(solution)/shard_map/gather | solution.py:185
  57.2 0.7 broadcast_select_fusion.12
  57.8 9.8 %all-to-all-start.3 = ((f32[128,32,1]{1,2,0:T(1,128)}), f32[128,32,1]{1,2,0:T(1,128)S(1)}, u32[]{:S(2)}, u32[]{:S(2)}) async-start(f32[128,32,1]{1,2,0:T(1,128)} %bitcast.35), calls=%async_computation.3 | async-start | bytes 131072 | tf_op jit(solution)/shard_map/all_to_all | solution.py:188
  67.6 4.4 %broadcast_in_dim.237 = f32[1024,4,512]{2,1,0:T(4,128)} broadcast(f32[]{:T(128)} %constant.543.clone.1), dimensions={} | broadcast | bytes 8388612 | tf_op jit(solution)/shard_map/broadcast_in_dim | solution.py:136
  72.0 26.5 %scatter_fusion = f32[1024,4,512]{2,1,0:T(4,128)} fusion(f32[1024,4,512]{2,1,0:T(4,128)} %broadcast_in_dim.237, s32[256]{0:T(256)S(1)} %get-tuple-element.259, f32[256,4,512]{2,1,0:T(4,128)S(1)} %copy-done), kind=kCustom, calls=%fused_computation.12 | custom fusion | bytes 6292480 | tf_op jit(solution)/shard_map/scatter | solution.py:138
  98.5 10.0 %all-to-all-start.1 = ((f32[1024,4,512]{2,1,0:T(4,128)}), f32[1024,4,512]{2,1,0:T(4,128)}, u32[]{:S(2)}, u32[]{:S(2)}) async-start(f32[1024,4,512]{2,1,0:T(4,128)} %scatter_fusion), calls=%async_computation.1 | async-start | bytes 16777216 | tf_op jit(solution)/shard_map/all_to_all | solution.py:146
  108.6 0.6 fusion.106
  109.2 1.3 concatenate.34
  110.5 1.3 concatenate.35
  111.8 4.8 %gather_fusion.2 = f32[768]{0:T(1024)S(1)} fusion(f32[128]{0:T(128)S(1)} %get-tuple-element.271, s32[1024]{0:T(1024)S(1)} %pad_clamp_fusion.6), kind=kCustom, calls=%fused_computation.2 | custom fusion | bytes 9216 | tf_op jit(solution)/shard_map/gather | solution.py:166
  116.7 0.6 pad_clamp_fusion.2
  117.3 0.6 pad_clamp_fusion
  117.9 0.7 and_reduce_fusion
  118.6 0.7 and_reduce_fusion.2
  119.3 0.6 fusion.75
  120.0 0.6 fusion.74
  120.5 0.6 fusion.70
  121.1 0.5 fusion.66
  121.7 0.6 compare_bitcast_fusion
  122.6 0.5 broadcast.2028
  123.2 0.8 reduce.53
  124.1 4.5 %gather_fusion.1 = f32[768]{0:T(1024)S(1)} fusion(f32[4096]{0:T(1024)S(1)} %all_to_all.33, s32[1024]{0:T(1024)S(1)} %pad_clamp_fusion.7), kind=kCustom, calls=%fused_computation.1 | custom fusion | bytes 9216 | tf_op jit(solution)/shard_map/gather | solution.py:194
  128.5 79.0 %all-to-all-done.1 = f32[1024,4,512]{2,1,0:T(4,128)} async-done(((f32[1024,4,512]{2,1,0:T(4,128)}), f32[1024,4,512]{2,1,0:T(4,128)}, u32[]{:S(2)}, u32[]{:S(2)}) %all-to-all-start.1) | async-done | bytes 8388640 | tf_op jit(solution)/shard_map/all_to_all | solution.py:146
  207.7 61.2 %scatter_fusion.1 = f32[128,4,512]{2,1,0:T(4,128)S(1)} fusion(f32[128,4,512]{2,1,0:T(4,128)S(1)} %broadcast_in_dim.232, s32[1024]{0:T(1024)S(1)} %bitcast.624, f32[1024,4,512]{2,1,0:T(4,128)} %all-to-all-done.1), kind=kCustom, calls=%fused_computation.13 | custom fusion | bytes 25169920 | tf_op jit(solution)/shard_map/scatter | solution.py:153
  268.9 0.4 copy.306
  269.6 0.5 copy.329
  270.6 16.1 %gather_fusion.3 = f32[4096,256]{1,0:T(8,128)} fusion(f32[768,256]{1,0:T(8,128)S(1)} %copy.330, s32[4096]{0:T(1024)S(1)} %get-tuple-element.281), kind=kCustom, calls=%fused_computation.3 | custom fusion | bytes 8404992 | tf_op jit(solution)/shard_map/gather | solution.py:184
  286.7 3.9 %broadcast_multiply_fusion = f32[128,32,256]{2,1,0:T(8,128)} fusion(f32[128,32,256]{2,1,0:T(8,128)} %bitcast.556, f32[128,32]{1,0:T(8,128)S(1)} %convert_bitcast_fusion), kind=kLoop, calls=%fused_computation.15 | loop fusion | flops 1048576 | bytes 8404992 | tf_op jit(solution)/shard_map/mul | solution.py:184
  290.6 13.0 %all-to-all-start.4 = ((f32[128,32,256]{2,1,0:T(8,128)}), f32[128,32,256]{2,1,0:T(8,128)}, u32[]{:S(2)}, u32[]{:S(2)}) async-start(f32[128,32,256]{2,1,0:T(8,128)} %broadcast_multiply_fusion), calls=%async_computation.4 | async-start | bytes 8388608 | tf_op jit(solution)/shard_map/all_to_all | solution.py:187
  303.7 0.6 fusion.92
  304.3 0.5 copy-done.28
  304.9 0.6 fusion.105
  305.5 0.7 slice_bitcast_fusion.23
  306.4 0.8 slice_bitcast_fusion.21
  307.7 0.5 fusion.2
  308.8 0.8 gather_fusion.5
  309.6 0.8 gather_fusion.6
  310.3 0.9 gather_fusion.7
  311.2 0.9 gather_fusion.8
  312.1 0.9 gather_fusion.9
  313.0 0.9 gather_fusion.10
  314.6 0.5 fusion.14
  315.1 0.4 fusion.4
  315.7 40.5 %all-to-all-done.4 = f32[128,32,256]{2,1,0:T(8,128)} async-done(((f32[128,32,256]{2,1,0:T(8,128)}), f32[128,32,256]{2,1,0:T(8,128)}, u32[]{:S(2)}, u32[]{:S(2)}) %all-to-all-start.4) | async-done | bytes 4194336 | tf_op jit(solution)/shard_map/all_to_all | solution.py:187
  356.2 4.3 %gather_fusion.4 = f32[768,256]{1,0:T(8,128)S(1)} fusion(f32[4096,256]{1,0:T(8,128)} %bitcast.49, s32[1024]{0:T(1024)S(1)} %pad_clamp_fusion.7), kind=kCustom, calls=%fused_computation.4 | custom fusion | bytes 1575936 | tf_op jit(solution)/shard_map/gather | solution.py:192
  362.8 0.7 fusion.49
  363.5 1.9 fusion.29
  365.6 1.3 constant_dynamic-slice_fusion
  367.0 1.9 fusion.31
  369.6 2.0 broadcast_select_fusion.4
  371.6 1.4 scatter-add.56
  373.4 1.4 copy.360
  (247 shorter events, 7.7 us)
Async XLA Ops:
  0.0 19.6 %copy-start.10 = (s32[256]{0:T(256)S(1)}, s32[256]{0:T(256)}, u32[]{:S(2)}) copy-start(s32[256]{0:T(256)} %param.33) | copy-start | bytes 3076
  0.0 19.6 %copy-start.63 = (f32[128]{0:T(128)S(1)}, f32[128]{0:T(128)}, u32[]{:S(2)}) copy-start(f32[128]{0:T(128)} %param.37) | copy-start | bytes 1540
  0.0 19.6 %copy-start.7 = (f32[128]{0:T(128)S(1)}, f32[128]{0:T(128)}, u32[]{:S(2)}) copy-start(f32[128]{0:T(128)} %param.38) | copy-start | bytes 1540
  6.1 21.1 %all-to-all-start.2 = ((s32[128,32,1]{1,2,0:T(1,128)}), s32[128,32,1]{1,2,0:T(1,128)S(1)}, u32[]{:S(2)}, u32[]{:S(2)}) async-start(s32[128,32,1]{1,2,0:T(1,128)} %bitcast.31), calls=%async_computation.2 | async-start | bytes 131072 | tf_op jit(solution)/shard_map/all_to_all | solution.py:181
  20.2 288.1 %copy-start.12 = (f32[128]{0:T(128)}, f32[128]{0:T(128)S(1)}, u32[]{:S(2)}) copy-start(f32[128]{0:T(128)S(1)} %get-tuple-element.272) | copy-start | bytes 1540
  27.3 30.6 %all-to-all-start = ((s32[128,8,1]{1,2,0:T(1,128)}), s32[128,8,1]{1,2,0:T(1,128)S(1)}, u32[]{:S(2)}, u32[]{:S(2)}) async-start(s32[128,8,1]{1,2,0:T(1,128)} %bitcast.4), calls=%async_computation | async-start | bytes 131072 | tf_op jit(solution)/shard_map/all_to_all | solution.py:147
  57.8 40.7 %all-to-all-start.3 = ((f32[128,32,1]{1,2,0:T(1,128)}), f32[128,32,1]{1,2,0:T(1,128)S(1)}, u32[]{:S(2)}, u32[]{:S(2)}) async-start(f32[128,32,1]{1,2,0:T(1,128)} %bitcast.35), calls=%async_computation.3 | async-start | bytes 131072 | tf_op jit(solution)/shard_map/all_to_all | solution.py:188
  67.6 4.4 %copy-start = (f32[256,4,512]{2,1,0:T(4,128)S(1)}, f32[256,4,512]{2,1,0:T(4,128)}, u32[]{:S(2)}) copy-start(f32[256,4,512]{2,1,0:T(4,128)} %param.32) | copy-start | bytes 6291460
  98.5 109.1 %all-to-all-start.1 = ((f32[1024,4,512]{2,1,0:T(4,128)}), f32[1024,4,512]{2,1,0:T(4,128)}, u32[]{:S(2)}, u32[]{:S(2)}) async-start(f32[1024,4,512]{2,1,0:T(4,128)} %scatter_fusion), calls=%async_computation.1 | async-start | bytes 16777216 | tf_op jit(solution)/shard_map/all_to_all | solution.py:146
  108.5 9.4 %copy-start.65 = (s32[5]{0:T(128)S(1)}, s32[5]{0:T(128)}, u32[]{:S(2)}) copy-start(s32[5]{0:T(128)} %constant.567.clone.1) | copy-start | bytes 64
  108.5 9.4 %copy-start.66 = (s32[5]{0:T(128)S(1)}, s32[5]{0:T(128)}, u32[]{:S(2)}) copy-start(s32[5]{0:T(128)} %constant.569.clone.1) | copy-start | bytes 64
  108.5 10.1 %copy-start.64 = (s32[5]{0:T(128)S(1)}, s32[5]{0:T(128)}, u32[]{:S(2)}) copy-start(s32[5]{0:T(128)} %constant.565.clone.1) | copy-start | bytes 64
  108.5 10.8 %copy-start.50 = (s32[6,128]{1,0:T(8,128)S(1)}, s32[6,128]{1,0:T(8,128)}, u32[]{:S(2)}) copy-start(s32[6,128]{1,0:T(8,128)} %param.35) | copy-start | bytes 9220
  108.6 13.1 %copy-start.6 = (s32[6,128]{1,0:T(8,128)S(1)}, s32[6,128]{1,0:T(8,128)}, u32[]{:S(2)}) copy-start(s32[6,128]{1,0:T(8,128)} %param.36) | copy-start | bytes 9220
  290.6 65.6 %all-to-all-start.4 = ((f32[128,32,256]{2,1,0:T(8,128)}), f32[128,32,256]{2,1,0:T(8,128)}, u32[]{:S(2)}, u32[]{:S(2)}) async-start(f32[128,32,256]{2,1,0:T(8,128)} %broadcast_multiply_fusion), calls=%async_computation.4 | async-start | bytes 8388608 | tf_op jit(solution)/shard_map/all_to_all | solution.py:187
  303.7 4.1 %copy-start.5 = (f32[8,8,1,1]{1,0,3,2:T(8,128)S(1)}, f32[8,8,1,1]{1,0,3,2:T(8,128)}, u32[]{:S(2)}) copy-start(f32[8,8,1,1]{1,0,3,2:T(8,128)} %constant.571) | copy-start | bytes 772
  304.3 4.5 %copy-start.20 = (f32[128]{0:T(128)}, f32[128]{0:T(128)S(1)}, u32[]{:S(2)}) copy-start(f32[128]{0:T(128)S(1)} %get-tuple-element.152) | copy-start | bytes 1540
  304.3 4.5 %copy-start.22 = (f32[128]{0:T(128)}, f32[128]{0:T(128)S(1)}, u32[]{:S(2)}) copy-start(f32[128]{0:T(128)S(1)} %get-tuple-element.213) | copy-start | bytes 1540
  304.3 4.5 %copy-start.24 = (f32[128]{0:T(128)}, f32[128]{0:T(128)S(1)}, u32[]{:S(2)}) copy-start(f32[128]{0:T(128)S(1)} %get-tuple-element.215) | copy-start | bytes 1540
  304.3 4.5 %copy-start.26 = (f32[128]{0:T(128)}, f32[128]{0:T(128)S(1)}, u32[]{:S(2)}) copy-start(f32[128]{0:T(128)S(1)} %get-tuple-element.217) | copy-start | bytes 1540
  309.6 4.3 %copy-start.13 = (f32[128]{0:T(128)S(1)}, f32[128]{0:T(128)}, u32[]{:S(2)}) copy-start(f32[128]{0:T(128)} %copy-done.12) | copy-start | bytes 1540
  309.6 5.5 %copy-start.52 = (f32[128]{0:T(128)S(1)}, f32[128]{0:T(128)}, u32[]{:S(2)}) copy-start(f32[128]{0:T(128)} %get-tuple-element.269) | copy-start | bytes 1540
  356.2 4.8 %copy-start.19 = (pred[128]{0:T(512)(128)(4,1)S(1)}, pred[128]{0:T(512)(128)(4,1)}, u32[]{:S(2)}) copy-start(pred[128]{0:T(512)(128)(4,1)} %get-tuple-element.278) | copy-start | bytes 388
  356.2 4.9 %copy-start.43 = (pred[128]{0:T(512)(128)(4,1)S(1)}, pred[128]{0:T(512)(128)(4,1)}, u32[]{:S(2)}) copy-start(pred[128]{0:T(512)(128)(4,1)} %get-tuple-element.153) | copy-start | bytes 388
  360.6 1.5 copy-start.17
  360.6 1.6 copy-start.16
  360.8 1.6 copy-start.15
  360.8 1.7 copy-start.41
  360.9 1.7 copy-start.39
  360.9 1.7 copy-start.54
  361.0 1.6 copy-start.38
  361.1 1.6 copy-start.53
  361.2 1.5 copy-start.4
  361.2 1.5 copy-start.9
  361.2 1.6 copy-start.11
  361.2 1.6 copy-start.31
  361.2 1.6 copy-start.40
  361.2 1.6 copy-start.49
  361.3 1.5 copy-start.8
  361.3 2.2 copy-start.3
  361.3 2.2 copy-start.29
  361.3 2.2 copy-start.37
  361.3 2.2 copy-start.48
  361.4 4.0 %copy-start.2 = (f32[128,4,8,8]{0,3,2,1:T(8,128)S(1)}, f32[128,4,8,8]{0,3,2,1:T(8,128)}, u32[]{:S(2)}) copy-start(f32[128,4,8,8]{0,3,2,1:T(8,128)} %get-tuple-element.183) | copy-start | bytes 393220
  361.5 4.0 %copy-start.27 = (f32[128]{0:T(128)S(1)}, f32[128]{0:T(128)}, u32[]{:S(2)}) copy-start(f32[128]{0:T(128)} %copy-done.26) | copy-start | bytes 1540
  361.5 4.0 %copy-start.36 = (pred[128]{0:T(512)(128)(4,1)S(1)}, pred[128]{0:T(512)(128)(4,1)}, u32[]{:S(2)}) copy-start(pred[128]{0:T(512)(128)(4,1)} %get-tuple-element.224) | copy-start | bytes 388
  361.5 4.0 %copy-start.47 = (f32[128]{0:T(128)S(1)}, f32[128]{0:T(128)}, u32[]{:S(2)}) copy-start(f32[128]{0:T(128)} %get-tuple-element.263) | copy-start | bytes 1540
  361.5 5.3 %copy-start.34 = (pred[128]{0:T(512)(128)(4,1)S(1)}, pred[128]{0:T(512)(128)(4,1)}, u32[]{:S(2)}) copy-start(pred[128]{0:T(512)(128)(4,1)} %get-tuple-element.232) | copy-start | bytes 388
  361.6 5.3 %copy-start.51 = (pred[128]{0:T(512)(128)(4,1)S(1)}, pred[128]{0:T(512)(128)(4,1)}, u32[]{:S(2)}) copy-start(pred[128]{0:T(512)(128)(4,1)} %get-tuple-element.240) | copy-start | bytes 388
  361.7 5.3 %copy-start.1 = (f32[128,4,8,8]{0,3,2,1:T(8,128)S(1)}, f32[128,4,8,8]{0,3,2,1:T(8,128)}, u32[]{:S(2)}) copy-start(f32[128,4,8,8]{0,3,2,1:T(8,128)} %get-tuple-element.182) | copy-start | bytes 393220
  361.7 5.3 %copy-start.25 = (f32[128]{0:T(128)S(1)}, f32[128]{0:T(128)}, u32[]{:S(2)}) copy-start(f32[128]{0:T(128)} %copy-done.24) | copy-start | bytes 1540
  361.7 5.3 %copy-start.35 = (pred[128]{0:T(512)(128)(4,1)S(1)}, pred[128]{0:T(512)(128)(4,1)}, u32[]{:S(2)}) copy-start(pred[128]{0:T(512)(128)(4,1)} %get-tuple-element.223) | copy-start | bytes 388
  361.7 5.3 %copy-start.46 = (f32[128]{0:T(128)S(1)}, f32[128]{0:T(128)}, u32[]{:S(2)}) copy-start(f32[128]{0:T(128)} %get-tuple-element.262) | copy-start | bytes 1540
  361.7 7.2 %copy-start.58 = (f32[128]{0:T(128)S(1)}, f32[128]{0:T(128)}, u32[]{:S(2)}) copy-start(f32[128]{0:T(128)} %get-tuple-element.214) | copy-start | bytes 1540
  361.8 7.2 %copy-start.23 = (f32[128]{0:T(128)S(1)}, f32[128]{0:T(128)}, u32[]{:S(2)}) copy-start(f32[128]{0:T(128)} %copy-done.22) | copy-start | bytes 1540
  361.8 7.2 %copy-start.33 = (pred[128]{0:T(512)(128)(4,1)S(1)}, pred[128]{0:T(512)(128)(4,1)}, u32[]{:S(2)}) copy-start(pred[128]{0:T(512)(128)(4,1)} %get-tuple-element.227) | copy-start | bytes 388
  361.8 7.2 %copy-start.45 = (f32[128]{0:T(128)S(1)}, f32[128]{0:T(128)}, u32[]{:S(2)}) copy-start(f32[128]{0:T(128)} %get-tuple-element.261) | copy-start | bytes 1540
  361.9 7.4 %copy-start.57 = (f32[128]{0:T(128)S(1)}, f32[128]{0:T(128)}, u32[]{:S(2)}) copy-start(f32[128]{0:T(128)} %get-tuple-element.212) | copy-start | bytes 1540
  361.9 3.6 copy-start.61
  361.9 7.7 %copy-start.21 = (f32[128]{0:T(128)S(1)}, f32[128]{0:T(128)}, u32[]{:S(2)}) copy-start(f32[128]{0:T(128)} %copy-done.20) | copy-start | bytes 1540
  361.9 7.7 %copy-start.32 = (pred[128]{0:T(512)(128)(4,1)S(1)}, pred[128]{0:T(512)(128)(4,1)}, u32[]{:S(2)}) copy-start(pred[128]{0:T(512)(128)(4,1)} %get-tuple-element.222) | copy-start | bytes 388
  361.9 7.7 %copy-start.44 = (f32[128]{0:T(128)S(1)}, f32[128]{0:T(128)}, u32[]{:S(2)}) copy-start(f32[128]{0:T(128)} %get-tuple-element.260) | copy-start | bytes 1540
  362.1 11.0 %copy-start.55 = (f32[128]{0:T(128)S(1)}, f32[128]{0:T(128)}, u32[]{:S(2)}) copy-start(f32[128]{0:T(128)} %get-tuple-element.151) | copy-start | bytes 1540
  362.1 3.3 copy-start.62
  (8 other events, 7.4 us)
where the time goes:
time: 378 us; the launch traced here: 375 us
  local copies, waits for them, and re-layouts  173 us (46%)
  waiting for transfers between devices  124 us (33%)
  starting transfers between devices  49.1 us (13%)
  other arithmetic  24.3 us (6%)
    all_to_all x1, waiting for transfers between devices, body(): lax.all_to_all(outgoing, ('grp', 'dev'), split_axis=0, concat_axis=0, til...  79 us
    scatter x2, local copies, waits for them, and re-layouts, body(): new_state = jnp.zeros((elem_dev, 4, old_state.shape[2]), jnp.float32).at[...  61.6 us
    all_to_all x1, waiting for transfers between devices, body(): lax.all_to_all(answer, ('grp', 'dev'), split_axis=0, concat_axis=0, tiled...  40.5 us
    scatter x1, local copies, waits for them, and re-layouts, body(): outgoing = jnp.zeros((devices * per_pair, 4, old_state.shape[2]), jnp.flo...  26.5 us
    gather x2, local copies, waits for them, and re-layouts, body(): answer_imped = impedance[serve_at % elem_dev] * asked  24.8 us
    gather x1, local copies, waits for them, and re-layouts, body(): answer = trace_table[serve_at] * asked[:, None]  16.1 us
    all_to_all x1, starting transfers between devices, body(): lax.all_to_all(answer, ('grp', 'dev'), split_axis=0, concat_axis=0, tiled...  13 us
    all_to_all x1, starting transfers between devices, body(): lax.all_to_all(requests_out, ('grp', 'dev'), split_axis=0, concat_axis=0,...  11.5 us
  transfers between devices with their start and end apart: 5, of which 3 were waited for; matrix products, arithmetic and copies ran while one was open for 24% of the time, Pallas kernels for 0%

commit v1 on v0

v1 whole, which is shorter than its diff:
```python
import jax
import jax.numpy as jnp
import numpy as np
from jax import lax
from jax.experimental import pallas as pl
from jax.experimental.pallas import tpu as pltpu
from jax.sharding import PartitionSpec as P

NP = 8
DEVS = 128
LANES = 128
AXES = ("grp", "dev")
metric_scale = 0.25
F32 = jnp.float32
I32 = jnp.int32
BF16 = jnp.bfloat16
VMEM = pltpu.MemorySpace.VMEM
SMEM = pltpu.MemorySpace.SMEM
ANY = pl.ANY


def gll_tables(poly_order):
    num_points = poly_order + 1
    points = -np.cos(np.pi * np.arange(num_points) / poly_order)
    legendre = np.zeros((num_points, num_points))
    for sweeps in range(101):
        legendre[:, 0] = 1.0
        legendre[:, 1] = points
        for degree in range(2, num_points):
            legendre[:, degree] = (
                (2 * degree - 1) * points * legendre[:, degree - 1]
                - (degree - 1) * legendre[:, degree - 2]
            ) / degree
        if sweeps < 100:
            points = points - (points * legendre[:, poly_order] - legendre[:, poly_order - 1]) / (
                num_points * legendre[:, poly_order]
            )
    end_values = legendre[:, poly_order]
    weights = 2.0 / (poly_order * num_points * end_values**2)
    distance = points[:, None] - points[None, :] + np.eye(num_points)
    derivative = end_values[:, None] / end_values[None, :] / distance
    derivative = derivative * (1.0 - np.eye(num_points))
    derivative[0, 0] = -poly_order * num_points / 4.0
    derivative[poly_order, poly_order] = poly_order * num_points / 4.0
    return (points, weights, derivative)


POINTS, WEIGHTS, DERIV = gll_tables(NP - 1)
DERIV = DERIV.astype(np.float32)
LIFT = metric_scale / float(WEIGHTS[0])


def derivative_tables():
    eye2, eye8 = np.eye(2, dtype=np.float32), np.eye(8, dtype=np.float32)
    along_y = np.kron(eye2, np.kron(DERIV.T, eye8))
    along_z = np.kron(eye2, np.kron(eye8, DERIV.T))
    side = np.concatenate([along_y, along_z], axis=1)
    stacked = np.concatenate([along_y, along_z], axis=0)
    coef = np.zeros((4, 4, 2, LANES), np.float32)
    for out_chunk in range(4):
        for in_chunk in range(4):
            for half in range(2):
                lanes = slice(64 * half, 64 * half + 64)
                coef[out_chunk, in_chunk, 0, lanes] = DERIV[2 * out_chunk + half, 2 * in_chunk + half]
                coef[out_chunk, in_chunk, 1, lanes] = DERIV[
                    2 * out_chunk + half, 2 * in_chunk + 1 - half
                ]
    return side, stacked, coef.reshape(32, LANES)


SIDE, STACKED, COEF = derivative_tables()


def iota(shape, axis):
    return lax.broadcasted_iota(I32, shape, axis)


def small_dot(left, right):
    return jnp.dot(left.astype(BF16), right.astype(BF16), preferred_element_type=F32)


def split3(value):
    high = value.astype(BF16)
    rest = value - high.astype(F32)
    middle = rest.astype(BF16)
    low = (rest - middle.astype(F32)).astype(BF16)
    return high, middle, low


def pick_dot(pick, value):
    pick = pick.astype(BF16)
    high, middle, low = split3(value)
    total = jnp.dot(pick, high, preferred_element_type=F32)
    total = total + jnp.dot(pick, middle, preferred_element_type=F32)
    return total + jnp.dot(pick, low, preferred_element_type=F32)


def order_kernel(dest_ref, info_ref, pos_ref):
    dest = dest_ref[...]
    sub = iota((LANES, LANES), 0)
    lane = iota((LANES, LANES), 1)
    diag = sub == lane
    key_row, key_col, dev_row, dev_col, lab_col = [], [], [], [], []
    for half in range(2):
        row = jnp.broadcast_to(dest[half : half + 1, :], (LANES, LANES))
        owner = (row >> 7).astype(F32)
        local = (row & 127).astype(F32) + 1.0
        key = owner * 256.0 + (lane + 128 * half).astype(F32)
        key_row.append(key)
        dev_row.append(owner)
        key_col.append(jnp.sum(jnp.where(diag, key, 0.0), axis=1, keepdims=True))
        dev_col.append(jnp.sum(jnp.where(diag, owner, 0.0), axis=1, keepdims=True))
        lab_col.append(jnp.sum(jnp.where(diag, local, 0.0), axis=1, keepdims=True))
    labels = jnp.zeros((LANES, LANES), F32)
    targets = jnp.zeros((1, LANES), F32)
    for half in range(2):
        before_col = jnp.zeros((LANES, 1), F32)
        before_row = jnp.zeros((1, LANES), F32)
        for other in range(2):
            before_col = before_col + jnp.sum(
                jnp.where(key_row[other] < key_col[half], 1.0, 0.0), axis=1, keepdims=True
            )
            before_row = before_row + jnp.sum(
                jnp.where(key_col[other] < key_row[half], 1.0, 0.0), axis=0, keepdims=True
            )
        pos_ref[half : half + 1, :] = before_row.astype(I32)
        place = before_col.astype(I32)
        is_target = (place == 8 * lane) & (lane < 32)
        targets = targets + jnp.sum(jnp.where(is_target, dev_col[half], 0.0), axis=0, keepdims=True)
        is_label = (place & 7) == lane - 32
        mine = jnp.where(dev_row[half] == sub.astype(F32), 1.0, 0.0)
        labels = labels + small_dot(mine, jnp.where(is_label, lab_col[half], 0.0))
    info_ref[...] = (labels + targets).astype(I32)


def pack_kernel(pos_ref, dest_ref, state_ref, out_ref):
    @pl.when(dest_ref[0, 0] >= 0)
    def _():
        def one(slot, carry):
            place = pos_ref[slot >> 7, slot & 127]
            start = (place & 7) * 512 + (place >> 3)
            out_ref[pl.ds(start, 16, stride=32), :] = state_ref[pl.ds(pl.multiple_of(slot * 16, 16), 16), :]
            return carry

        lax.fori_loop(0, 256, one, 0, unroll=8)


def table_kernel(me_ref, info_ref, nbr_ref, wall_ref, out_ref, scr):
    sub = iota((LANES, LANES), 0)
    lane = iota((LANES, LANES), 1)
    info = info_ref[...]
    present = jnp.zeros((LANES, LANES), F32)
    for j in range(32):
        present = jnp.where(info[:, j : j + 1] == lane, 1.0, present)
    below = jnp.where(lane < sub, 1.0, 0.0)
    rank = small_dot(below, present)
    target = jnp.clip(info, 0, LANES - 1)
    slot = target * 16 + jnp.take_along_axis(rank.astype(I32), target, axis=1)
    slot = jnp.where(info >= 0, slot, -1)
    out_ref[0:32, :] = slot.astype(F32).T[0:32, :].astype(I32)
    is_source = jnp.broadcast_to(jnp.where(info[:, 32:33] > 0, 1.0, 0.0), (LANES, LANES))
    order = small_dot(below, is_source)
    order_row = jnp.where(is_source > 0.0, order, -1.0).T[0:16, :]
    pick = jnp.where(order_row == iota((16, LANES), 0).astype(F32), 1.0, 0.0)
    out_ref[32:48, :] = small_dot(pick, info.astype(F32)).astype(I32)
    scr[...] = jnp.zeros((8, LANES), F32)
    nbr = nbr_ref[...]
    owner = nbr >> 7
    remote = (owner != me_ref[0]) & (wall_ref[...] == 0)
    scr[0:6, :] = jnp.where(remote, 1.0, 0.0)
    flags = scr[...]
    before = small_dot(flags, jnp.where(sub < lane, 1.0, 0.0))
    out_ref[48:56, :] = jnp.where(flags > 0.0, before, -1.0).astype(I32)
    scr[...] = jnp.full((8, LANES), -1.0, F32)
    scr[0:6, :] = jnp.where(remote, owner, -1).astype(F32)
    out_ref[56:64, :] = jnp.broadcast_to(
        jnp.max(scr[...], axis=1, keepdims=True), (8, LANES)
    ).astype(I32)


def forward_kernel(tab_ref, in_ref, out_ref):
    def one(source, carry):
        @pl.when(tab_ref[0, source] >= 0)
        def _():
            base = pl.multiple_of(source * 32, 32)
            for j in range(32):
                out_ref[pl.ds(tab_ref[j, source], 1), :] = in_ref[pl.ds(base + j, 1), :]

        return carry

    lax.fori_loop(0, DEVS, one, 0)


def half_sign(shape):
    return jnp.where(iota(shape, 1) < 64, -1.0, 1.0)


def arrive_kernel(
    tab_ref, in_ref, rank_ref, bulk_ref, dens_ref, state_ref, press_ref, norm_ref, wave_ref, send_ref, blk, sem
):
    def one(number, carry):
        source = number >> 3
        k = number & 7
        row = tab_ref[32 + source, 32 + k] - 1
        piece = in_ref[pl.ds(k * 256 + source, 16, stride=16), :]
        state_ref[pl.ds(row, 16, stride=128), :] = piece
        return carry

    lax.fori_loop(0, DEVS, one, 0, unroll=8)

    shape = (LANES, LANES)
    lane = iota(shape, 1)
    zed_row = jnp.sqrt(bulk_ref[...] * dens_ref[...])
    diag = iota(shape, 0) == lane
    zed = jnp.sum(jnp.where(diag, jnp.broadcast_to(zed_row, shape), 0.0), axis=1, keepdims=True)
    sign = half_sign(shape)

    def chunk(field, n4):
        start = (n4 * 4 + field) * LANES
        return state_ref[start : start + LANES, :]

    half = lane >> 6
    face_i = (lane >> 3) & 7
    face_b = lane & 7
    from_y = (face_i & 1) * 64 + half * 56 + face_b
    from_z = (face_i & 1) * 64 + face_b * 8 + half * 7
    for axis in range(3):
        values = []
        for field in (0, 1 + axis):
            if axis == 0:
                value = jnp.where(lane < 64, chunk(field, 0), chunk(field, 3))
            else:
                index = from_y if axis == 1 else from_z
                value = jnp.take_along_axis(chunk(field, 0), index, axis=1)
                for n4 in range(1, 4):
                    other = jnp.take_along_axis(chunk(field, n4), index, axis=1)
                    value = jnp.where(face_i >> 1 == n4, other, value)
            values.append(value)
        rows = slice(axis * LANES, axis * LANES + LANES)
        normal = sign * values[1]
        wave = values[0] + zed * normal
        press_ref[rows, :] = values[0]
        norm_ref[rows, :] = normal
        wave_ref[rows, :] = wave
        for side in range(2):
            face = 2 * axis + side
            rank = rank_ref[face : face + 1, :]
            pick = jnp.where(rank == iota((32, LANES), 0), 1.0, 0.0)
            got = pick_dot(pick, wave)
            first, second = got[0:16], got[16:32]
            if side == 0:
                second = pltpu.roll(second, 64, 1)
            else:
                first = pltpu.roll(first, 64, 1)
            block = jnp.where(iota((16, LANES), 1) < 64, first, second)
            for t in range(16):
                blk[face, t] = block[t : t + 1, :]
            rank_col = jnp.sum(
                jnp.where(diag, jnp.broadcast_to(rank, shape).astype(F32), 0.0), axis=1, keepdims=True
            )
            blk[face, 16] = jnp.sum(jnp.where(rank_col == lane.astype(F32), zed, 0.0), axis=0, keepdims=True)
    for face in range(6):
        owner = tab_ref[56 + face, 0]

        @pl.when(owner >= 0)
        def _():
            pltpu.make_async_copy(blk.at[face], send_ref.at[owner], sem.at[face]).start()

    for face in range(6):
        owner = tab_ref[56 + face, 0]

        @pl.when(owner >= 0)
        def _():
            pltpu.make_async_copy(blk.at[face], send_ref.at[owner], sem.at[face]).wait()


def column(row, diag):
    wide = jnp.broadcast_to(row, (LANES, LANES))
    return jnp.sum(jnp.where(diag, wide, 0.0), axis=1, keepdims=True)


def volume_kernel(
    me_ref, state_ref, wave_ref, nbr_ref, wall_ref, orient_ref, bulk_ref, dens_ref, side_ref, stack_ref,
    coef_ref, vol_ref, near_ref, index_ref, zed_ref, pick_ref,
):
    shape = (LANES, LANES)
    lane = iota(shape, 1)
    diag = iota(shape, 0) == lane
    zed_row = jnp.sqrt(bulk_ref[...] * dens_ref[...])
    zed = column(zed_row, diag)
    bulk = column(bulk_ref[...], diag)
    dens = column(dens_ref[...], diag)

    def chunk(field, n4):
        start = (n4 * 4 + field) * LANES
        return state_ref[start : start + LANES, :]

    high = lax.Precision.HIGHEST
    by_bulk = -metric_scale * bulk
    by_dens = -(metric_scale / dens)
    swapped = {}
    for field in (0, 1):
        for n4 in range(4):
            swapped[field, n4] = pltpu.roll(chunk(field, n4), 64, 1)
    for n4 in range(4):
        along = {}
        for field in (0, 1):
            total = None
            for m4 in range(4):
                at = (n4 * 4 + m4) * 2
                term = chunk(field, m4) * coef_ref[at : at + 1, :]
                term = term + swapped[field, m4] * coef_ref[at + 1 : at + 2, :]
                total = term if total is None else total + term
            along[field] = total
        both = jnp.concatenate([chunk(2, n4), chunk(3, n4)], axis=1)
        div = along[1] + jnp.dot(both, stack_ref[...], precision=high, preferred_element_type=F32)
        grad = jnp.dot(chunk(0, n4), side_ref[...], precision=high, preferred_element_type=F32)
        start = n4 * 4 * LANES
        vol_ref[start : start + LANES, :] = by_bulk * div
        vol_ref[start + LANES : start + 2 * LANES, :] = by_dens * along[0]
        vol_ref[start + 2 * LANES : start + 3 * LANES, :] = by_dens * grad[:, 0:LANES]
        vol_ref[start + 3 * LANES : start + 4 * LANES, :] = by_dens * grad[:, LANES:]

    me = me_ref[0]
    low_half = lane < 64
    for axis in range(3):
        rows = slice(axis * LANES, axis * LANES + LANES)
        wave = wave_ref[rows, :]
        parts, zeds, walls, codes = [], [], [], []
        for side in range(2):
            face = 2 * axis + side
            nbr = nbr_ref[face : face + 1, :]
            is_wall = wall_ref[face : face + 1, :] == 1
            remote = ((nbr >> 7) != me) & jnp.logical_not(is_wall)
            local_row = (nbr & 127).astype(F32)
            local_col = column(local_row, diag)
            remote_row = jnp.where(remote, 1.0, 0.0)
            remote_col = column(remote_row, diag) > 0.0
            wall_col = column(jnp.where(is_wall, 1.0, 0.0), diag) > 0.0
            code_col = column(orient_ref[face : face + 1, :].astype(F32), diag).astype(I32)
            near = (local_col == lane.astype(F32)) & jnp.logical_not(remote_col)
            masked = jnp.where(low_half, 0.0, wave) if side == 0 else jnp.where(low_half, wave, 0.0)
            parts.append(pick_dot(jnp.where(near, 1.0, 0.0), masked))
            zed_near = jnp.sum(jnp.where(near, jnp.broadcast_to(zed_row, shape), 0.0), axis=1, keepdims=True)
            zeds.append(jnp.where(wall_col, zed, zed_near))
            walls.append(wall_col)
            codes.append(jnp.where(wall_col, 0, code_col))
            rank = jnp.sum(
                jnp.where((jnp.broadcast_to(local_row, shape) < local_col), remote_row, 0.0),
                axis=1, keepdims=True,
            )
            pick = (rank == lane.astype(F32)) & remote_col & (lane < 32)
            pick_ref[face * LANES : face * LANES + LANES, :] = jnp.where(pick, 1.0, 0.0)
        own = pltpu.roll(wave, 64, 1)
        near_ref[rows, :] = jnp.where(
            jnp.where(low_half, jnp.where(walls[1], 1, 0), jnp.where(walls[0], 1, 0)) == 1, own, parts[0] + parts[1]
        )
        zed_ref[rows, :] = jnp.where(low_half, zeds[0], zeds[1])
        code = jnp.where(low_half, codes[0], codes[1])
        a, b = (lane >> 3) & 7, lane & 7
        swap = code >= 4
        a1, b1 = jnp.where(swap, b, a), jnp.where(swap, a, b)
        a2 = jnp.where((code & 1) == 1, 7 - a1, a1)
        b2 = jnp.where((code & 2) == 2, 7 - b1, b1)
        index_ref[rows, :] = jnp.where(low_half, 64, 0) + a2 * 8 + b2


def flux_kernel(
    tab_ref, recv_ref, vol_ref, near_ref, index_ref, zed_ref, pick_ref, press_ref, norm_ref, bulk_ref,
    dens_ref, out_ref, blk, flat, sem,
):
    for face in range(6):
        owner = tab_ref[56 + face, 0]

        @pl.when(owner >= 0)
        def _():
            pltpu.make_async_copy(recv_ref.at[owner], blk.at[face], sem.at[face]).start()

    shape = (LANES, LANES)
    lane = iota(shape, 1)
    diag = iota(shape, 0) == lane
    zed = column(jnp.sqrt(bulk_ref[...] * dens_ref[...]), diag)
    up = LIFT * column(bulk_ref[...], diag)
    across = -LIFT * zed / column(dens_ref[...], diag)
    for face in range(6):
        owner = tab_ref[56 + face, 0]

        @pl.when(owner >= 0)
        def _():
            pltpu.make_async_copy(recv_ref.at[owner], blk.at[face], sem.at[face]).wait()
            for t in range(17):
                flat[face, t : t + 1, :] = blk[face, t]

        @pl.when(owner < 0)
        def _():
            flat[face] = jnp.zeros((24, LANES), F32)

    low_half = lane < 64
    thin = iota((32, LANES), 1) < 64
    i2 = lane >> 6
    j = (lane >> 3) & 7
    k = lane & 7
    sign = half_sign(shape)
    lifts = []
    for axis in range(3):
        rows = slice(axis * LANES, axis * LANES + LANES)
        far = near_ref[rows, :]
        zeds = []
        for side in range(2):
            face = 2 * axis + side
            block = flat[face, 0:16, :]
            turned = pltpu.roll(block, 64, 1)
            if side == 0:
                table = jnp.where(thin, 0.0, jnp.concatenate([turned, block], axis=0))
            else:
                table = jnp.where(thin, jnp.concatenate([block, turned], axis=0), 0.0)
            pick = pick_ref[face * LANES : face * LANES + LANES, :]
            far = far + pick_dot(pick[:, 0:32], table)
            zeds.append(jnp.sum(jnp.where(pick > 0.0, flat[face, 16:17, :], 0.0), axis=1, keepdims=True))
        far = jnp.take_along_axis(far, index_ref[rows, :], axis=1)
        zed_out = zed_ref[rows, :] + jnp.where(low_half, zeds[0], zeds[1])
        jump = (far - press_ref[rows, :] + zed_out * norm_ref[rows, :]) / (zed + zed_out)
        lifts.append((jump, sign * jump))
    for n4 in range(4):
        face_i = 2 * n4 + i2
        from_y = jnp.where(j == 7, 64, 0) + face_i * 8 + k
        from_z = jnp.where(k == 7, 64, 0) + face_i * 8 + j
        on_y = (j == 0) | (j == 7)
        on_z = (k == 0) | (k == 7)
        total = None
        for axis in range(3):
            jump = lifts[axis][0]
            if axis == 0:
                if n4 == 0:
                    here = jnp.where(low_half, jump, 0.0)
                    turn = -here
                elif n4 == 3:
                    here = jnp.where(low_half, 0.0, jump)
                    turn = here
                else:
                    here = None
            elif axis == 1:
                here = jnp.where(on_y, jnp.take_along_axis(jump, from_y, axis=1), 0.0)
                turn = jnp.where(j == 0, -here, here)
            else:
                here = jnp.where(on_z, jnp.take_along_axis(jump, from_z, axis=1), 0.0)
                turn = jnp.where(k == 0, -here, here)
            at = n4 * 4 + 1 + axis
            value = vol_ref[at * LANES : at * LANES + LANES, :]
            if here is not None:
                value = value + across * turn
                total = here if total is None else total + here
            out_ref[pl.ds(at, LANES, stride=16), :] = value
        at = n4 * 4
        out_ref[pl.ds(at, LANES, stride=16), :] = vol_ref[at * LANES : at * LANES + LANES, :] + up * total


def vm():
    return pl.BlockSpec(memory_space=VMEM)


def sm():
    return pl.BlockSpec(memory_space=SMEM)


def anyspace():
    return pl.BlockSpec(memory_space=ANY)


def shaped(shape, dtype=F32):
    return jax.ShapeDtypeStruct(shape, dtype)


def exchange(value):
    return lax.all_to_all(value, AXES, split_axis=0, concat_axis=0, tiled=True)


def body(old_state, dest_row, neighbours, orientation, wall_flags, bulk_modulus, density):
    me = (lax.axis_index("grp") * lax.axis_size("dev") + lax.axis_index("dev")).astype(I32).reshape(1)
    dest = dest_row.reshape(2, LANES)
    bulk = bulk_modulus.reshape(1, LANES)
    dens = density.reshape(1, LANES)
    state = old_state.reshape(256, 4, 4, LANES).transpose(0, 2, 1, 3).reshape(4096, LANES)

    info, pos = pl.pallas_call(
        order_kernel,
        in_specs=[vm()],
        out_specs=[vm(), vm()],
        out_shape=[shaped((DEVS, LANES), I32), shaped((2, LANES), I32)],
        name="order",
    )(dest)
    heard = exchange(info.reshape(DEVS, 1, LANES)).reshape(DEVS, LANES)
    pieces = pl.pallas_call(
        pack_kernel,
        in_specs=[sm(), sm(), vm()],
        out_specs=vm(),
        out_shape=shaped((4096, LANES)),
        name="pack",
    )(pos, dest, state)
    spread = exchange(pieces.reshape(DEVS, 32, LANES)).reshape(4096, LANES)
    table = pl.pallas_call(
        table_kernel,
        in_specs=[sm(), vm(), vm(), vm()],
        out_specs=vm(),
        out_shape=shaped((64, LANES), I32),
        scratch_shapes=[pltpu.VMEM((8, LANES), F32)],
        name="table",
    )(me, heard, neighbours, wall_flags)
    passed = pl.pallas_call(
        forward_kernel,
        in_specs=[sm(), vm()],
        out_specs=vm(),
        out_shape=shaped((2048, LANES)),
        name="forward",
    )(table, spread)
    arrived = exchange(passed.reshape(DEVS, 16, LANES)).reshape(2048, LANES)
    new_state, press, norm, wave, halo_out = pl.pallas_call(
        arrive_kernel,
        in_specs=[sm(), vm(), vm(), vm(), vm()],
        out_specs=[vm(), vm(), vm(), vm(), anyspace()],
        out_shape=[
            shaped((2048, LANES)),
            shaped((384, LANES)),
            shaped((384, LANES)),
            shaped((384, LANES)),
            shaped((DEVS, 17, 1, LANES)),
        ],
        scratch_shapes=[pltpu.VMEM((6, 17, 1, LANES), F32), pltpu.SemaphoreType.DMA((6,))],
        name="arrive",
    )(table, arrived, table[48:56], bulk, dens)
    halo_in = exchange(halo_out)
    vol, near, index, zed_out, pick = pl.pallas_call(
        volume_kernel,
        in_specs=[sm()] + [vm()] * 10,
        out_specs=[vm()] * 5,
        out_shape=[
            shaped((2048, LANES)),
            shaped((384, LANES)),
            shaped((384, LANES), I32),
            shaped((384, LANES)),
            shaped((768, LANES)),
        ],
        name="volume",
    )(
        me, new_state, wave, neighbours, wall_flags, orientation, bulk, dens,
        jnp.asarray(SIDE), jnp.asarray(STACKED), jnp.asarray(COEF),
    )
    result = pl.pallas_call(
        flux_kernel,
        in_specs=[sm(), anyspace()] + [vm()] * 9,
        out_specs=vm(),
        out_shape=shaped((2048, LANES)),
        scratch_shapes=[
            pltpu.VMEM((6, 17, 1, LANES), F32),
            pltpu.VMEM((6, 24, LANES), F32),
            pltpu.SemaphoreType.DMA((6,)),
        ],
        name="flux",
    )(table, halo_in, vol, near, index, zed_out, pick, press, norm, bulk, dens)
    return result.reshape(128, 4, 4, LANES).transpose(0, 2, 1, 3).reshape(128, 4, 512)


def solution(mesh):
    both = P(AXES)
    faces = P(None, AXES)
    in_specs = (P(AXES, None, None), both, faces, faces, faces, both, both)
    return jax.shard_map(
        body, mesh=mesh, in_specs=in_specs, out_specs=P(AXES, None, None), check_vma=False
    )
```

time: 378 us -> 128 us (0.34)
  local copies, waits for them, and re-layouts: 173 us -> 5.21 us
  waiting for transfers between devices: 124 us -> 68.3 us
  Pallas kernels: 0 us -> 28.2 us
  other arithmetic: 24.3 us -> 0 us
  starting transfers between devices: 49.1 us -> 25.5 us
    scatter x5 -> x0, local copies, waits for them, and re-layouts: 92.9 us -> none  [the longest x2 61.6 us: body(): new_state = jnp.zeros((elem_dev, 4, old_state.shape[2]), jnp.float32).at[...]
    gather x12 -> x0, local copies, waits for them, and re-layouts: 59.5 us -> none  [the longest x2 24.8 us: body(): answer_imped = impedance[serve_at % elem_dev] * asked]
    all_to_all x5 -> x4, waiting for transfers between devices: 124 us -> 68.3 us  [exchange(): return lax.all_to_all(value, AXES, split_axis=0, concat_axis=0, tiled=True)]
    pallas_call x0 -> x7, Pallas kernels: none -> 28.2 us  [the longest x1 6.54 us: body(): pl.pallas_call(forward_kernel, in_specs=[sm(), vm()], out_specs=vm(), out...]
    all_to_all x5 -> x4, starting transfers between devices: 49.1 us -> 25.5 us  [exchange(): return lax.all_to_all(value, AXES, split_axis=0, concat_axis=0, tiled=True)]
    another operation x17 -> x0, local copies, waits for them, and re-layouts: 6.98 us -> none
    mul x5 -> x0, other arithmetic: 5.79 us -> none  [the longest x1 3.93 us: body(): answer = trace_table[serve_at] * asked[:, None]]
    scatter-add x8 -> x0, other arithmetic: 4.63 us -> none  [the longest x4 3.86 us: right_side(): result.at[(slice(None), 0) + face_index(face_id)]]
  transfers between devices with their start and end apart: 5 -> 4, of which waited for: 3 -> 4; matrix products, arithmetic and copies ran while one was open for 24% -> 1% of each run, Pallas kernels for 0% -> 8%
where the time goes in v1:
time: 128 us; the launch traced here: 127 us
  waiting for transfers between devices  68.3 us (53%)
  Pallas kernels  28.2 us (22%)
  starting transfers between devices  25.5 us (20%)
  local copies, waits for them, and re-layouts  5.21 us (4%)
    all_to_all x4, waiting for transfers between devices, exchange(): return lax.all_to_all(value, AXES, split_axis=0, concat_axis=0, tiled=True)  68.3 us
    all_to_all x4, starting transfers between devices, exchange(): return lax.all_to_all(value, AXES, split_axis=0, concat_axis=0, tiled=True)  25.5 us
    pallas_call x1, Pallas kernels, body(): pl.pallas_call(forward_kernel, in_specs=[sm(), vm()], out_specs=vm(), out...  6.54 us
    pallas_call x1, Pallas kernels, body(): pl.pallas_call(arrive_kernel, in_specs=[sm(), vm(), vm(), vm(), vm()], ou...  5.62 us
    pallas_call x1, Pallas kernels, body(): pl.pallas_call(flux_kernel, in_specs=[sm(), anyspace()] + [vm()] * 9, out...  4.52 us
    pallas_call x1, Pallas kernels, body(): pl.pallas_call(volume_kernel, in_specs=[sm()] + [vm()] * 10, out_specs=[v...  4.37 us
    unnamed x8, local copies, waits for them, and re-layouts  3.94 us
    pallas_call x1, Pallas kernels, body(): pl.pallas_call(pack_kernel, in_specs=[sm(), sm(), vm()], out_specs=vm(),...  2.95 us
  transfers between devices with their start and end apart: 4, of which 4 were waited for; matrix products, arithmetic and copies ran while one was open for 1% of the time, Pallas kernels for 8%

profile of v1, /device:TPU:1, one launch (start us, length us, event | category | flops | bytes accessed | tf_op | source)
XLA Modules:
  0.0 127.3 jit_solution(6675738857112708832)
XLA Ops:
  0.0 1.7 %order.1 = (s32[128,128]{1,0:T(8,128)}, s32[2,128]{1,0:T(2,128)}) custom-call(s32[2,128]{1,0:T(2,128)} %bitcast.35), custom_call_target="tpu_custom_call" | custom-call | tf_op jit(solution)/shard_map/order/pallas_call | solution.py:485
  1.7 11.5 %all-to-all-start = ((s32[128,1,128]{2,1,0:T(1,128)}), s32[128,1,128]{2,1,0:T(1,128)S(1)}, u32[]{:S(2)}, u32[]{:S(2)}) async-start(s32[128,1,128]{2,1,0:T(1,128)} %bitcast.28), calls=%async_computation | async-start | bytes 131072 | tf_op jit(solution)/shard_map/all_to_all | solution.py:475
  13.2 3.0 %pack.1 = f32[4096,128]{1,0:T(8,128)} custom-call(s32[2,128]{1,0:T(2,128)} %get-tuple-element.18.pos_ref, s32[2,128]{1,0:T(2,128)} %bitcast.36, f32[4096,128]{1,0:T(8,128)} %bitcast.26), custom_call_target="tpu_custom_call" | custom-call | tf_op jit(solution)/shard_map/pack/pallas_call | solution.py:493
  16.1 6.6 %all-to-all-done = s32[128,1,128]{2,1,0:T(1,128)S(1)} async-done(((s32[128,1,128]{2,1,0:T(1,128)}), s32[128,1,128]{2,1,0:T(1,128)S(1)}, u32[]{:S(2)}, u32[]{:S(2)}) %all-to-all-start) | async-done | bytes 65568 | tf_op jit(solution)/shard_map/all_to_all | solution.py:475
  22.8 0.0 copy-start.3
  22.8 0.6 copy-done.3
  23.4 5.2 %all-to-all-start.1 = ((f32[128,32,128]{2,1,0:T(8,128)}), f32[128,32,128]{2,1,0:T(8,128)S(1)}, u32[]{:S(2)}, u32[]{:S(2)}) async-start(f32[128,32,128]{2,1,0:T(8,128)} %bitcast.22), calls=%async_computation.1 | async-start | bytes 4194304 | tf_op jit(solution)/shard_map/all_to_all | solution.py:475
  28.6 2.5 %table.1.tab_ref = s32[64,128]{1,0:T(8,128)} custom-call(s32[1]{0:T(128)} %bitcast.me_ref, s32[128,128]{1,0:T(8,128)} %bitcast.27, s32[6,128]{1,0:T(8,128)} %nbr_ref.3, s32[6,128]{1,0:T(8,128)} %wall_ref.3), custom_call_target="tpu_custom_call" | custom-call | tf_op jit(solution)/shard_map/table/pallas_call | solution.py:501
  31.1 28.0 %all-to-all-done.1 = f32[128,32,128]{2,1,0:T(8,128)S(1)} async-done(((f32[128,32,128]{2,1,0:T(8,128)}), f32[128,32,128]{2,1,0:T(8,128)S(1)}, u32[]{:S(2)}, u32[]{:S(2)}) %all-to-all-start.1) | async-done | bytes 2097184 | tf_op jit(solution)/shard_map/all_to_all | solution.py:475
  59.0 0.0 copy-start
  59.0 1.3 %copy-done = f32[128,32,128]{2,1,0:T(8,128)} copy-done((f32[128,32,128]{2,1,0:T(8,128)}, f32[128,32,128]{2,1,0:T(8,128)S(1)}, u32[]{:S(2)}) %copy-start) | copy-done | bytes 2097176
  60.4 6.5 %forward.1 = f32[2048,128]{1,0:T(8,128)} custom-call(s32[64,128]{1,0:T(8,128)} %table.1.tab_ref, f32[4096,128]{1,0:T(8,128)} %bitcast.23), custom_call_target="tpu_custom_call" | custom-call | tf_op jit(solution)/shard_map/forward/pallas_call | solution.py:509
  66.9 4.4 %all-to-all-start.2 = ((f32[128,16,128]{2,1,0:T(8,128)}), f32[128,16,128]{2,1,0:T(8,128)S(1)}, u32[]{:S(2)}, u32[]{:S(2)}) async-start(f32[128,16,128]{2,1,0:T(8,128)} %bitcast.24), calls=%async_computation.2 | async-start | bytes 2097152 | tf_op jit(solution)/shard_map/all_to_all | solution.py:475
  71.3 1.3 %slice.4.rank_ref = s32[8,128]{1,0:T(8,128)} slice(s32[64,128]{1,0:T(8,128)} %table.1.tab_ref), slice={[48:56], [0:128]} | slice | bytes 8192 | tf_op jit(solution)/shard_map/slice | solution.py:530
  72.6 18.1 %all-to-all-done.2 = f32[128,16,128]{2,1,0:T(8,128)S(1)} async-done(((f32[128,16,128]{2,1,0:T(8,128)}), f32[128,16,128]{2,1,0:T(8,128)S(1)}, u32[]{:S(2)}, u32[]{:S(2)}) %all-to-all-start.2) | async-done | bytes 1048608 | tf_op jit(solution)/shard_map/all_to_all | solution.py:475
  90.7 0.0 copy-start.2
  90.7 1.0 copy-done.2
  91.7 5.6 %arrive.1 = (f32[2048,128]{1,0:T(8,128)}, f32[384,128]{1,0:T(8,128)}, f32[384,128]{1,0:T(8,128)}, f32[384,128]{1,0:T(8,128)}, f32[128,17,1,128]{3,2,1,0:T(1,128)}) custom-call(s32[64,128]{1,0:T(8,128)} %table.1.tab_ref, f32[2048,128]{1,0:T(8,128)} %bitcast.25, s32[8,128]{1,0:T(8,128)} %slice.4.rank_ref, f32[1,128]{1,0:T(1,128)} %bitcast.29, f32[1,128]{1,0:T(1,128)} %bitcast.32), custom_call_target="tpu_custom_call" | custom-call | tf_op jit(solution)/shard_map/arrive/pallas_call | solution.py:517
  97.3 4.4 %all-to-all-start.3 = ((f32[128,17,1,128]{3,2,1,0:T(1,128)}), f32[128,17,1,128]{3,2,1,0:T(1,128)S(1)}, u32[]{:S(2)}, u32[]{:S(2)}) async-start(f32[128,17,1,128]{3,2,1,0:T(1,128)} %get-tuple-element.19), calls=%async_computation.3 | async-start | bytes 2228224 | tf_op jit(solution)/shard_map/all_to_all | solution.py:475
  101.7 4.4 %volume.1 = (f32[2048,128]{1,0:T(8,128)}, f32[384,128]{1,0:T(8,128)}, s32[384,128]{1,0:T(8,128)}, f32[384,128]{1,0:T(8,128)}, f32[768,128]{1,0:T(8,128)}) custom-call(s32[1]{0:T(128)} %bitcast.me_ref, f32[2048,128]{1,0:T(8,128)} %get-tuple-element.20.state_ref, f32[384,128]{1,0:T(8,128)} %get-tuple-element.21.wave_ref, s32[6,128]{1,0:T(8,128)} %nbr_ref.3, ...), custom_call_target="tpu_custom_call" | custom-call | tf_op jit(solution)/shard_map/volume/pallas_call | solution.py:532
  106.1 15.6 %all-to-all-done.3.recv_ref = f32[128,17,1,128]{3,2,1,0:T(1,128)S(1)} async-done(((f32[128,17,1,128]{3,2,1,0:T(1,128)}), f32[128,17,1,128]{3,2,1,0:T(1,128)S(1)}, u32[]{:S(2)}, u32[]{:S(2)}) %all-to-all-start.3) | async-done | bytes 1114144 | tf_op jit(solution)/shard_map/all_to_all | solution.py:475
  121.7 0.0 copy-start.1
  121.7 1.0 copy-done.1
  122.7 4.5 %flux.1 = f32[2048,128]{1,0:T(8,128)} custom-call(s32[64,128]{1,0:T(8,128)} %table.1.tab_ref, f32[128,17,1,128]{3,2,1,0:T(1,128)} %copy-done.1, f32[2048,128]{1,0:T(8,128)} %get-tuple-element.22.vol_ref, f32[384,128]{1,0:T(8,128)} %get-tuple-element.23.near_ref, s32[384,128]{1,0:T(8,128)} %get-tuple-element.24.index_ref, ...), custom_call_target="tpu_custom_call" | custom-call | tf_op jit(solution)/shard_map/flux/pallas_call | solution.py:548
Async XLA Ops:
  1.7 21.1 %all-to-all-start = ((s32[128,1,128]{2,1,0:T(1,128)}), s32[128,1,128]{2,1,0:T(1,128)S(1)}, u32[]{:S(2)}, u32[]{:S(2)}) async-start(s32[128,1,128]{2,1,0:T(1,128)} %bitcast.28), calls=%async_computation | async-start | bytes 131072 | tf_op jit(solution)/shard_map/all_to_all | solution.py:475
  22.8 0.6 copy-start.3
  23.4 35.7 %all-to-all-start.1 = ((f32[128,32,128]{2,1,0:T(8,128)}), f32[128,32,128]{2,1,0:T(8,128)S(1)}, u32[]{:S(2)}, u32[]{:S(2)}) async-start(f32[128,32,128]{2,1,0:T(8,128)} %bitcast.22), calls=%async_computation.1 | async-start | bytes 4194304 | tf_op jit(solution)/shard_map/all_to_all | solution.py:475
  59.0 1.3 %copy-start = (f32[128,32,128]{2,1,0:T(8,128)}, f32[128,32,128]{2,1,0:T(8,128)S(1)}, u32[]{:S(2)}) copy-start(f32[128,32,128]{2,1,0:T(8,128)S(1)} %all-to-all-done.1) | copy-start | bytes 6291460
  66.9 23.8 %all-to-all-start.2 = ((f32[128,16,128]{2,1,0:T(8,128)}), f32[128,16,128]{2,1,0:T(8,128)S(1)}, u32[]{:S(2)}, u32[]{:S(2)}) async-start(f32[128,16,128]{2,1,0:T(8,128)} %bitcast.24), calls=%async_computation.2 | async-start | bytes 2097152 | tf_op jit(solution)/shard_map/all_to_all | solution.py:475
  90.7 1.0 copy-start.2
  97.3 24.5 %all-to-all-start.3 = ((f32[128,17,1,128]{3,2,1,0:T(1,128)}), f32[128,17,1,128]{3,2,1,0:T(1,128)S(1)}, u32[]{:S(2)}, u32[]{:S(2)}) async-start(f32[128,17,1,128]{3,2,1,0:T(1,128)} %get-tuple-element.19), calls=%async_computation.3 | async-start | bytes 2228224 | tf_op jit(solution)/shard_map/all_to_all | solution.py:475
  121.7 1.0 copy-start.1

commit v2 on v1

--- a/solution.py
+++ b/solution.py
@@ -16,7 +16,7 @@
 BF16 = jnp.bfloat16
 VMEM = pltpu.MemorySpace.VMEM
 SMEM = pltpu.MemorySpace.SMEM
-ANY = pl.ANY
+HBM = pltpu.MemorySpace.HBM
 
 
 def gll_tables(poly_order):
@@ -93,6 +93,35 @@
     total = jnp.dot(pick, high, preferred_element_type=F32)
     total = total + jnp.dot(pick, middle, preferred_element_type=F32)
     return total + jnp.dot(pick, low, preferred_element_type=F32)
+
+
+def column(row, diag):
+    wide = jnp.broadcast_to(row, (LANES, LANES))
+    return jnp.sum(jnp.where(diag, wide, 0.0), axis=1, keepdims=True)
+
+
+def half_sign(shape):
+    return jnp.where(iota(shape, 1) < 64, -1.0, 1.0)
+
+
+def face_pair(chunk, axis, zed):
+    lane = iota((LANES, LANES), 1)
+    half, face_i, face_b = lane >> 6, (lane >> 3) & 7, lane & 7
+    from_y = (face_i & 1) * 64 + half * 56 + face_b
+    from_z = (face_i & 1) * 64 + face_b * 8 + half * 7
+    values = []
+    for field in (0, 1 + axis):
+        if axis == 0:
+            value = jnp.where(lane < 64, chunk(field, 0), chunk(field, 3))
+        else:
+            index = from_y if axis == 1 else from_z
+            value = jnp.take_along_axis(chunk(field, 0), index, axis=1)
+            for n4 in range(1, 4):
+                other = jnp.take_along_axis(chunk(field, n4), index, axis=1)
+                value = jnp.where(face_i >> 1 == n4, other, value)
+        values.append(value)
+    normal = half_sign((LANES, LANES)) * values[1]
+    return values[0], normal, values[0] + zed * normal
 
 
 def order_kernel(dest_ref, info_ref, pos_ref):
@@ -145,9 +174,16 @@
         lax.fori_loop(0, 256, one, 0, unroll=8)
 
 
-def table_kernel(me_ref, info_ref, nbr_ref, wall_ref, out_ref, scr):
+def table_kernel(
+    me_ref, info_ref, nbr_ref, wall_ref, bulk_ref, dens_ref, spot_ref, owner_ref, out_ref, cols_ref, wide, scr
+):
     sub = iota((LANES, LANES), 0)
     lane = iota((LANES, LANES), 1)
+    diag = sub == lane
+    bulk = column(bulk_ref[...], diag)
+    dens = column(dens_ref[...], diag)
+    zed = column(jnp.sqrt(bulk_ref[...] * dens_ref[...]), diag)
+    cols_ref[...] = jnp.where(lane == 0, zed, jnp.where(lane == 1, bulk, dens))
     info = info_ref[...]
     present = jnp.zeros((LANES, LANES), F32)
     for j in range(32):
@@ -157,12 +193,19 @@
     target = jnp.clip(info, 0, LANES - 1)
     slot = target * 16 + jnp.take_along_axis(rank.astype(I32), target, axis=1)
     slot = jnp.where(info >= 0, slot, -1)
-    out_ref[0:32, :] = slot.astype(F32).T[0:32, :].astype(I32)
+    wide[...] = slot
+    quarter = iota((32, LANES), 1) >> 5
+    spots = wide[pl.ds(0, 32, stride=4), :]
+    for part in range(1, 4):
+        moved = pltpu.roll(wide[pl.ds(part, 32, stride=4), :], 32 * part, 1)
+        spots = jnp.where(quarter == part, moved, spots)
+    spot_ref[...] = spots
     is_source = jnp.broadcast_to(jnp.where(info[:, 32:33] > 0, 1.0, 0.0), (LANES, LANES))
     order = small_dot(below, is_source)
-    order_row = jnp.where(is_source > 0.0, order, -1.0).T[0:16, :]
-    pick = jnp.where(order_row == iota((16, LANES), 0).astype(F32), 1.0, 0.0)
-    out_ref[32:48, :] = small_dot(pick, info.astype(F32)).astype(I32)
+    label = jnp.take_along_axis(info, 32 + (lane >> 4), axis=1)
+    chosen = (is_source > 0.0) & (order == (lane & 15).astype(F32))
+    labels = jnp.sum(jnp.where(chosen, label.astype(F32), 0.0), axis=0, keepdims=True)
+    out_ref[0:8, :] = jnp.broadcast_to(labels, (8, LANES)).astype(I32) - 1
     scr[...] = jnp.zeros((8, LANES), F32)
     nbr = nbr_ref[...]
     owner = nbr >> 7
@@ -170,81 +213,57 @@
     scr[0:6, :] = jnp.where(remote, 1.0, 0.0)
     flags = scr[...]
     before = small_dot(flags, jnp.where(sub < lane, 1.0, 0.0))
-    out_ref[48:56, :] = jnp.where(flags > 0.0, before, -1.0).astype(I32)
+    out_ref[8:16, :] = jnp.where(flags > 0.0, before, -1.0).astype(I32)
     scr[...] = jnp.full((8, LANES), -1.0, F32)
     scr[0:6, :] = jnp.where(remote, owner, -1).astype(F32)
-    out_ref[56:64, :] = jnp.broadcast_to(
+    owner_ref[...] = jnp.broadcast_to(
         jnp.max(scr[...], axis=1, keepdims=True), (8, LANES)
     ).astype(I32)
 
 
-def forward_kernel(tab_ref, in_ref, out_ref):
+def forward_kernel(spot_ref, in_ref, out_ref):
     def one(source, carry):
-        @pl.when(tab_ref[0, source] >= 0)
+        base = pl.multiple_of(source * 32, 32)
+
+        @pl.when(spot_ref[base] >= 0)
         def _():
-            base = pl.multiple_of(source * 32, 32)
             for j in range(32):
-                out_ref[pl.ds(tab_ref[j, source], 1), :] = in_ref[pl.ds(base + j, 1), :]
+                out_ref[pl.ds(spot_ref[base + j], 1), :] = in_ref[pl.ds(base + j, 1), :]
 
         return carry
 
     lax.fori_loop(0, DEVS, one, 0)
 
 
-def half_sign(shape):
-    return jnp.where(iota(shape, 1) < 64, -1.0, 1.0)
-
-
 def arrive_kernel(
-    tab_ref, in_ref, rank_ref, bulk_ref, dens_ref, state_ref, press_ref, norm_ref, wave_ref, send_ref, blk, sem
+    owner_ref, in_ref, row_ref, cols_ref, state_ref, send_ref, blk, sem
 ):
-    def one(number, carry):
-        source = number >> 3
-        k = number & 7
-        row = tab_ref[32 + source, 32 + k] - 1
-        piece = in_ref[pl.ds(k * 256 + source, 16, stride=16), :]
-        state_ref[pl.ds(row, 16, stride=128), :] = piece
-        return carry
-
-    lax.fori_loop(0, DEVS, one, 0, unroll=8)
+    place = jnp.where(row_ref[0:1, :] == iota((LANES, LANES), 0), 1.0, 0.0).astype(BF16)
+    place = jnp.concatenate([place, place, place], axis=1)
+    for chunk_id in range(0, 16, 2):
+        pair = []
+        for c in (chunk_id, chunk_id + 1):
+            rows = [in_ref[(k * 16 + c) * 16 : (k * 16 + c) * 16 + 16, :] for k in range(8)]
+            pair.append(jnp.concatenate(rows, axis=0))
+        parts = split3(jnp.concatenate(pair, axis=1))
+        moved = jnp.dot(place, jnp.concatenate(parts, axis=0), preferred_element_type=F32)
+        state_ref[chunk_id * LANES : (chunk_id + 1) * LANES, :] = moved[:, 0:LANES]
+        state_ref[(chunk_id + 1) * LANES : (chunk_id + 2) * LANES, :] = moved[:, LANES:]
 
     shape = (LANES, LANES)
     lane = iota(shape, 1)
-    zed_row = jnp.sqrt(bulk_ref[...] * dens_ref[...])
     diag = iota(shape, 0) == lane
-    zed = jnp.sum(jnp.where(diag, jnp.broadcast_to(zed_row, shape), 0.0), axis=1, keepdims=True)
-    sign = half_sign(shape)
+    zed = cols_ref[:, 0:1]
 
     def chunk(field, n4):
         start = (n4 * 4 + field) * LANES
         return state_ref[start : start + LANES, :]
 
-    half = lane >> 6
-    face_i = (lane >> 3) & 7
-    face_b = lane & 7
-    from_y = (face_i & 1) * 64 + half * 56 + face_b
-    from_z = (face_i & 1) * 64 + face_b * 8 + half * 7
     for axis in range(3):
-        values = []
-        for field in (0, 1 + axis):
-            if axis == 0:
-                value = jnp.where(lane < 64, chunk(field, 0), chunk(field, 3))
-            else:
-                index = from_y if axis == 1 else from_z
-                value = jnp.take_along_axis(chunk(field, 0), index, axis=1)
-                for n4 in range(1, 4):
-                    other = jnp.take_along_axis(chunk(field, n4), index, axis=1)
-                    value = jnp.where(face_i >> 1 == n4, other, value)
-            values.append(value)
-        rows = slice(axis * LANES, axis * LANES + LANES)
-        normal = sign * values[1]
-        wave = values[0] + zed * normal
-        press_ref[rows, :] = values[0]
-        norm_ref[rows, :] = normal
-        wave_ref[rows, :] = wave
+        wave = face_pair(chunk, axis, zed)[2]
         for side in range(2):
             face = 2 * axis + side
-            rank = rank_ref[face : face + 1, :]
+            rank = row_ref[8 + face : 9 + face, :]
             pick = jnp.where(rank == iota((32, LANES), 0), 1.0, 0.0)
             got = pick_dot(pick, wave)
             first, second = got[0:16], got[16:32]
@@ -253,43 +272,36 @@
             else:
                 first = pltpu.roll(first, 64, 1)
             block = jnp.where(iota((16, LANES), 1) < 64, first, second)
-            for t in range(16):
-                blk[face, t] = block[t : t + 1, :]
             rank_col = jnp.sum(
                 jnp.where(diag, jnp.broadcast_to(rank, shape).astype(F32), 0.0), axis=1, keepdims=True
             )
-            blk[face, 16] = jnp.sum(jnp.where(rank_col == lane.astype(F32), zed, 0.0), axis=0, keepdims=True)
+            zeds = jnp.sum(jnp.where(rank_col == lane.astype(F32), zed, 0.0), axis=0, keepdims=True)
+            for t in range(16):
+                blk[face, t] = block[t : t + 1, :]
+            blk[face, 16] = zeds
+            owner = owner_ref[face, 0]
+
+            @pl.when(owner >= 0)
+            def _():
+                pltpu.make_async_copy(blk.at[face], send_ref.at[owner], sem.at[face]).start()
+
     for face in range(6):
-        owner = tab_ref[56 + face, 0]
-
-        @pl.when(owner >= 0)
-        def _():
-            pltpu.make_async_copy(blk.at[face], send_ref.at[owner], sem.at[face]).start()
-
-    for face in range(6):
-        owner = tab_ref[56 + face, 0]
+        owner = owner_ref[face, 0]
 
         @pl.when(owner >= 0)
         def _():
             pltpu.make_async_copy(blk.at[face], send_ref.at[owner], sem.at[face]).wait()
 
 
-def column(row, diag):
-    wide = jnp.broadcast_to(row, (LANES, LANES))
-    return jnp.sum(jnp.where(diag, wide, 0.0), axis=1, keepdims=True)
-
-
 def volume_kernel(
-    me_ref, state_ref, wave_ref, nbr_ref, wall_ref, orient_ref, bulk_ref, dens_ref, side_ref, stack_ref,
-    coef_ref, vol_ref, near_ref, index_ref, zed_ref, pick_ref,
+    me_ref, state_ref, cols_ref, nbr_ref, wall_ref, orient_ref, bulk_ref, dens_ref, side_ref, stack_ref,
+    coef_ref, vol_ref, press_ref, norm_ref, near_ref, index_ref, zed_ref, pick_ref,
 ):
     shape = (LANES, LANES)
     lane = iota(shape, 1)
     diag = iota(shape, 0) == lane
     zed_row = jnp.sqrt(bulk_ref[...] * dens_ref[...])
-    zed = column(zed_row, diag)
-    bulk = column(bulk_ref[...], diag)
-    dens = column(dens_ref[...], diag)
+    zed, bulk, dens = cols_ref[:, 0:1], cols_ref[:, 1:2], cols_ref[:, 2:3]
 
     def chunk(field, n4):
         start = (n4 * 4 + field) * LANES
@@ -323,10 +335,13 @@
 
     me = me_ref[0]
     low_half = lane < 64
+    zed_out = jnp.zeros(shape, F32)
     for axis in range(3):
         rows = slice(axis * LANES, axis * LANES + LANES)
-        wave = wave_ref[rows, :]
-        parts, zeds, walls, codes = [], [], [], []
+        press, norm, wave = face_pair(chunk, axis, zed)
+        press_ref[rows, :] = press
+        norm_ref[rows, :] = norm
+        parts, zeds, walls, codes, picks = [], [], [], [], []
         for side in range(2):
             face = 2 * axis + side
             nbr = nbr_ref[face : face + 1, :]
@@ -350,12 +365,13 @@
                 axis=1, keepdims=True,
             )
             pick = (rank == lane.astype(F32)) & remote_col & (lane < 32)
-            pick_ref[face * LANES : face * LANES + LANES, :] = jnp.where(pick, 1.0, 0.0)
+            picks.append(jnp.where(pick, 1.0, 0.0))
         own = pltpu.roll(wave, 64, 1)
         near_ref[rows, :] = jnp.where(
             jnp.where(low_half, jnp.where(walls[1], 1, 0), jnp.where(walls[0], 1, 0)) == 1, own, parts[0] + parts[1]
         )
-        zed_ref[rows, :] = jnp.where(low_half, zeds[0], zeds[1])
+        zed_out = jnp.where(lane == 2 * axis, zeds[0], jnp.where(lane == 2 * axis + 1, zeds[1], zed_out))
+        pick_ref[rows, :] = picks[0] + pltpu.roll(picks[1], 32, 1)
         code = jnp.where(low_half, codes[0], codes[1])
         a, b = (lane >> 3) & 7, lane & 7
         swap = code >= 4
@@ -363,33 +379,27 @@
         a2 = jnp.where((code & 1) == 1, 7 - a1, a1)
         b2 = jnp.where((code & 2) == 2, 7 - b1, b1)
         index_ref[rows, :] = jnp.where(low_half, 64, 0) + a2 * 8 + b2
+    zed_ref[...] = zed_out
 
 
 def flux_kernel(
-    tab_ref, recv_ref, vol_ref, near_ref, index_ref, zed_ref, pick_ref, press_ref, norm_ref, bulk_ref,
-    dens_ref, out_ref, blk, flat, sem,
+    owner_ref, recv_ref, vol_hbm, near_ref, index_ref, zed_ref, pick_ref, press_ref, norm_ref, cols_ref,
+    out_ref, flat, vol_ref, sem,
 ):
+    load = pltpu.make_async_copy(vol_hbm, vol_ref, sem)
+    load.start()
+    shape = (LANES, LANES)
+    lane = iota(shape, 1)
+    zed = cols_ref[:, 0:1]
+    up = LIFT * cols_ref[:, 1:2]
+    across = -LIFT * zed / cols_ref[:, 2:3]
     for face in range(6):
-        owner = tab_ref[56 + face, 0]
+        owner = owner_ref[face, 0]
 
         @pl.when(owner >= 0)
         def _():
-            pltpu.make_async_copy(recv_ref.at[owner], blk.at[face], sem.at[face]).start()
-
-    shape = (LANES, LANES)
-    lane = iota(shape, 1)
-    diag = iota(shape, 0) == lane
-    zed = column(jnp.sqrt(bulk_ref[...] * dens_ref[...]), diag)
-    up = LIFT * column(bulk_ref[...], diag)
-    across = -LIFT * zed / column(dens_ref[...], diag)
-    for face in range(6):
-        owner = tab_ref[56 + face, 0]
-
-        @pl.when(owner >= 0)
-        def _():
-            pltpu.make_async_copy(recv_ref.at[owner], blk.at[face], sem.at[face]).wait()
             for t in range(17):
-                flat[face, t : t + 1, :] = blk[face, t]
+                flat[face, t : t + 1, :] = recv_ref[owner, t]
 
         @pl.when(owner < 0)
         def _():
@@ -404,23 +414,27 @@
     lifts = []
     for axis in range(3):
         rows = slice(axis * LANES, axis * LANES + LANES)
-        far = near_ref[rows, :]
-        zeds = []
+        pick = pick_ref[rows, :]
+        tables, zeds = [], []
         for side in range(2):
             face = 2 * axis + side
             block = flat[face, 0:16, :]
             turned = pltpu.roll(block, 64, 1)
             if side == 0:
-                table = jnp.where(thin, 0.0, jnp.concatenate([turned, block], axis=0))
+                tables.append(jnp.where(thin, 0.0, jnp.concatenate([turned, block], axis=0)))
             else:
-                table = jnp.where(thin, jnp.concatenate([block, turned], axis=0), 0.0)
-            pick = pick_ref[face * LANES : face * LANES + LANES, :]
-            far = far + pick_dot(pick[:, 0:32], table)
-            zeds.append(jnp.sum(jnp.where(pick > 0.0, flat[face, 16:17, :], 0.0), axis=1, keepdims=True))
+                tables.append(jnp.where(thin, jnp.concatenate([block, turned], axis=0), 0.0))
+            zed_row = flat[face, 16:17, :] if side == 0 else pltpu.roll(flat[face, 16:24, :], 32, 1)[0:1, :]
+            mine = (lane >> 5 == side) & (pick > 0.0)
+            zeds.append(
+                zed_ref[:, face : face + 1] + jnp.sum(jnp.where(mine, zed_row, 0.0), axis=1, keepdims=True)
+            )
+        far = near_ref[rows, :] + pick_dot(pick[:, 0:64], jnp.concatenate(tables, axis=0))
         far = jnp.take_along_axis(far, index_ref[rows, :], axis=1)
-        zed_out = zed_ref[rows, :] + jnp.where(low_half, zeds[0], zeds[1])
+        zed_out = jnp.where(low_half, zeds[0], zeds[1])
         jump = (far - press_ref[rows, :] + zed_out * norm_ref[rows, :]) / (zed + zed_out)
         lifts.append((jump, sign * jump))
+    load.wait()
     for n4 in range(4):
         face_i = 2 * n4 + i2
         from_y = jnp.where(j == 7, 64, 0) + face_i * 8 + k
@@ -463,12 +477,23 @@
     return pl.BlockSpec(memory_space=SMEM)
 
 
-def anyspace():
-    return pl.BlockSpec(memory_space=ANY)
-
-
 def shaped(shape, dtype=F32):
+    return VMEM(shape, dtype)
+
+
+def away(value):
+    return pltpu.with_memory_space_constraint(value, HBM)
+
+
+GRANT = pltpu.CompilerParams(vmem_limit_bytes=24 * 1024 * 1024)
+
+
+def plain(shape, dtype=F32):
     return jax.ShapeDtypeStruct(shape, dtype)
+
+
+def near(value):
+    return pltpu.with_memory_space_constraint(value, VMEM)
 
 
 def exchange(value):
@@ -486,77 +511,88 @@
         order_kernel,
         in_specs=[vm()],
         out_specs=[vm(), vm()],
-        out_shape=[shaped((DEVS, LANES), I32), shaped((2, LANES), I32)],
+        out_shape=[plain((DEVS, LANES), I32), plain((2, LANES), I32)],
         name="order",
+        compiler_params=GRANT,
     )(dest)
     heard = exchange(info.reshape(DEVS, 1, LANES)).reshape(DEVS, LANES)
     pieces = pl.pallas_call(
         pack_kernel,
         in_specs=[sm(), sm(), vm()],
         out_specs=vm(),
-        out_shape=shaped((4096, LANES)),
+        out_shape=plain((4096, LANES)),
         name="pack",
+        compiler_params=GRANT,
     )(pos, dest, state)
     spread = exchange(pieces.reshape(DEVS, 32, LANES)).reshape(4096, LANES)
-    table = pl.pallas_call(
+    spots, owners, rows, cols = pl.pallas_call(
         table_kernel,
-        in_specs=[sm(), vm(), vm(), vm()],
-        out_specs=vm(),
-        out_shape=shaped((64, LANES), I32),
-        scratch_shapes=[pltpu.VMEM((8, LANES), F32)],
+        in_specs=[sm()] + [vm()] * 5,
+        out_specs=[vm()] * 4,
+        out_shape=[
+            shaped((32, LANES), I32),
+            shaped((8, LANES), I32),
+            shaped((16, LANES), I32),
+            shaped((LANES, LANES)),
+        ],
+        scratch_shapes=[pltpu.VMEM((LANES, LANES), I32), pltpu.VMEM((8, LANES), F32)],
         name="table",
-    )(me, heard, neighbours, wall_flags)
+        compiler_params=GRANT,
+    )(me, near(heard), away(neighbours), away(wall_flags), away(bulk), away(dens))
     passed = pl.pallas_call(
         forward_kernel,
         in_specs=[sm(), vm()],
         out_specs=vm(),
         out_shape=shaped((2048, LANES)),
         name="forward",
-    )(table, spread)
+        compiler_params=GRANT,
+    )(spots.reshape(4096), near(spread))
     arrived = exchange(passed.reshape(DEVS, 16, LANES)).reshape(2048, LANES)
-    new_state, press, norm, wave, halo_out = pl.pallas_call(
+    new_state, halo_out = pl.pallas_call(
         arrive_kernel,
-        in_specs=[sm(), vm(), vm(), vm(), vm()],
-        out_specs=[vm(), vm(), vm(), vm(), anyspace()],
+        in_specs=[sm()] + [vm()] * 3,
+        out_specs=[vm(), pl.BlockSpec(memory_space=pl.ANY)],
+        out_shape=[shaped((2048, LANES)), plain((DEVS, 17, 1, LANES))],
+        scratch_shapes=[pltpu.VMEM((6, 17, 1, LANES), F32), pltpu.SemaphoreType.DMA((6,))],
+        name="arrive",
+        compiler_params=GRANT,
+    )(owners, near(arrived), near(rows), near(cols))
+    halo_in = exchange(halo_out)
+    vol, press, norm, here, index, zed_out, pick = pl.pallas_call(
+        volume_kernel,
+        in_specs=[sm()] + [vm()] * 10,
+        out_specs=[vm()] * 7,
         out_shape=[
-            shaped((2048, LANES)),
+            HBM((2048, LANES), F32),
             shaped((384, LANES)),
             shaped((384, LANES)),
             shaped((384, LANES)),
-            shaped((DEVS, 17, 1, LANES)),
-        ],
-        scratch_shapes=[pltpu.VMEM((6, 17, 1, LANES), F32), pltpu.SemaphoreType.DMA((6,))],
-        name="arrive",
-    )(table, arrived, table[48:56], bulk, dens)
-    halo_in = exchange(halo_out)
-    vol, near, index, zed_out, pick = pl.pallas_call(
-        volume_kernel,
-        in_specs=[sm()] + [vm()] * 10,
-        out_specs=[vm()] * 5,
-        out_shape=[
-            shaped((2048, LANES)),
+            shaped((384, LANES), I32),
+            shaped((LANES, LANES)),
             shaped((384, LANES)),
-            shaped((384, LANES), I32),
-            shaped((384, LANES)),
-            shaped((768, LANES)),
         ],
         name="volume",
+        compiler_params=GRANT,
     )(
-        me, new_state, wave, neighbours, wall_flags, orientation, bulk, dens,
-        jnp.asarray(SIDE), jnp.asarray(STACKED), jnp.asarray(COEF),
+        me, near(new_state), near(cols), away(neighbours), away(wall_flags), away(orientation), away(bulk),
+        away(dens), away(jnp.asarray(SIDE)), away(jnp.asarray(STACKED)), away(jnp.asarray(COEF)),
     )
     result = pl.pallas_call(
         flux_kernel,
-        in_specs=[sm(), anyspace()] + [vm()] * 9,
+        in_specs=[sm(), vm(), pl.BlockSpec(memory_space=pl.ANY)] + [vm()] * 7,
         out_specs=vm(),
-        out_shape=shaped((2048, LANES)),
+        out_shape=plain((2048, LANES)),
         scratch_shapes=[
-            pltpu.VMEM((6, 17, 1, LANES), F32),
             pltpu.VMEM((6, 24, LANES), F32),
-            pltpu.SemaphoreType.DMA((6,)),
+            pltpu.VMEM((2048, LANES), F32),
+            pltpu.SemaphoreType.DMA,
         ],
         name="flux",
-    )(table, halo_in, vol, near, index, zed_out, pick, press, norm, bulk, dens)
+        compiler_params=GRANT,
+    )(
+        owners, near(halo_in), away(vol), near(here), near(index), near(zed_out), near(pick), near(press),
+        near(norm), near(cols),
+    )
     return result.reshape(128, 4, 4, LANES).transpose(0, 2, 1, 3).reshape(128, 4, 512)
 
 

time: 128 us -> 117 us (0.914)
  blocking collectives: 0 us -> 23.1 us
  waiting for transfers between devices: 68.3 us -> 47.9 us
  Pallas kernels: 28.2 us -> 20.5 us
  starting transfers between devices: 25.5 us -> 22.3 us
  local copies, waits for them, and re-layouts: 5.21 us -> 2.94 us
    all_to_all x0 -> x1, blocking collectives: none -> 23.1 us  [exchange(): return lax.all_to_all(value, AXES, split_axis=0, concat_axis=0, tiled=True)]
    all_to_all x4 -> x3, waiting for transfers between devices: 68.3 us -> 47.9 us  [exchange(): return lax.all_to_all(value, AXES, split_axis=0, concat_axis=0, tiled=True)]
    pallas_call x3, Pallas kernels: 12.6 us -> 7.3 us  [the longest x1 3.33 us: body(): pl.pallas_call(flux_kernel, in_specs=[sm(), vm(), pl.BlockSpec(memory_spa...]
    all_to_all x4 -> x3, starting transfers between devices: 25.5 us -> 22.3 us  [exchange(): return lax.all_to_all(value, AXES, split_axis=0, concat_axis=0, tiled=True)]
    pallas_call x1, Pallas kernels: 6.54 us -> 4.17 us  [body(): pl.pallas_call(forward_kernel, in_specs=[sm(), vm()], out_specs=vm(), out...]
    unnamed x8 -> x6, local copies, waits for them, and re-layouts: 3.94 us -> 2.94 us
  transfers between devices with their start and end apart: 4 -> 3, of which waited for: 4 -> 3; matrix products, arithmetic and copies ran while one was open for 1% -> 0% of each run, Pallas kernels for 8% -> 8%
where the time goes in v2:
time: 117 us
  waiting for transfers between devices  47.9 us (41%)
  blocking collectives  23.1 us (20%)
  starting transfers between devices  22.3 us (19%)
  Pallas kernels  20.5 us (18%)
  local copies, waits for them, and re-layouts  2.94 us (3%)
    all_to_all x3, waiting for transfers between devices, exchange(): return lax.all_to_all(value, AXES, split_axis=0, concat_axis=0, tiled=True)  47.9 us
    all_to_all x1, blocking collectives, exchange(): return lax.all_to_all(value, AXES, split_axis=0, concat_axis=0, tiled=True)  23.1 us
    all_to_all x3, starting transfers between devices, exchange(): return lax.all_to_all(value, AXES, split_axis=0, concat_axis=0, tiled=True)  22.3 us
    pallas_call x1, Pallas kernels, body(): pl.pallas_call(forward_kernel, in_specs=[sm(), vm()], out_specs=vm(), out...  4.17 us
    pallas_call x1, Pallas kernels, body(): pl.pallas_call(volume_kernel, in_specs=[sm()] + [vm()] * 10, out_specs=[v...  4.11 us
    pallas_call x1, Pallas kernels, body(): pl.pallas_call(pack_kernel, in_specs=[sm(), sm(), vm()], out_specs=vm(),...  3.95 us
    pallas_call x1, Pallas kernels, body(): pl.pallas_call(flux_kernel, in_specs=[sm(), vm(), pl.BlockSpec(memory_spa...  3.33 us
    unnamed x6, local copies, waits for them, and re-layouts  2.94 us
  transfers between devices with their start and end apart: 3, of which 3 were waited for; matrix products, arithmetic and copies ran while one was open for 0% of the time, Pallas kernels for 8%

profile of v2, /device:TPU:1, one launch (start us, length us, event | category | flops | bytes accessed | tf_op | source)
XLA Modules:
  0.0 116.9 jit_solution(10954240731428274644)
XLA Ops:
  0.0 0.0 copy-start.1
  0.0 0.7 copy-done.1
  0.7 1.0 order.1
  1.7 11.5 %all-to-all-start = ((s32[128,1,128]{2,1,0:T(1,128)}), s32[128,1,128]{2,1,0:T(1,128)S(1)}, u32[]{:S(2)}, u32[]{:S(2)}) async-start(s32[128,1,128]{2,1,0:T(1,128)} %bitcast.3), calls=%async_computation | async-start | bytes 131072 | tf_op jit(solution)/shard_map/all_to_all | solution.py:500
  13.2 0.0 copy-start
  13.2 1.6 %copy-done = f32[256,4,512]{2,1,0:T(4,128)S(1)} copy-done((f32[256,4,512]{2,1,0:T(4,128)S(1)}, f32[256,4,512]{2,1,0:T(4,128)}, u32[]{:S(2)}) %copy-start) | copy-done | bytes 2097176
  14.8 0.0 copy-start.2
  14.8 0.7 copy-done.2
  15.5 3.9 %pack.1 = f32[4096,128]{1,0:T(8,128)} custom-call(s32[2,128]{1,0:T(2,128)S(1)} %get-tuple-element.23.pos_ref, s32[2,128]{1,0:T(2,128)S(1)} %bitcast.30, f32[4096,128]{1,0:T(8,128)S(1)} %bitcast.26), custom_call_target="tpu_custom_call" | custom-call | tf_op jit(solution)/shard_map/pack/pallas_call | solution.py:519
  19.4 3.3 %all-to-all-done = s32[128,1,128]{2,1,0:T(1,128)S(1)} async-done(((s32[128,1,128]{2,1,0:T(1,128)}), s32[128,1,128]{2,1,0:T(1,128)S(1)}, u32[]{:S(2)}, u32[]{:S(2)}) %all-to-all-start) | async-done | bytes 65568 | tf_op jit(solution)/shard_map/all_to_all | solution.py:500
  22.8 6.4 %all-to-all-start.1 = ((f32[128,32,128]{2,1,0:T(8,128)}), f32[128,32,128]{2,1,0:T(8,128)S(1)}, u32[]{:S(2)}, u32[]{:S(2)}) async-start(f32[128,32,128]{2,1,0:T(8,128)} %bitcast.11), calls=%async_computation.1 | async-start | bytes 4194304 | tf_op jit(solution)/shard_map/all_to_all | solution.py:500
  29.2 1.8 %table.1 = (s32[32,128]{1,0:T(8,128)S(1)}, s32[8,128]{1,0:T(8,128)S(1)}, s32[16,128]{1,0:T(8,128)S(1)}, f32[128,128]{1,0:T(8,128)S(1)}) custom-call(s32[1]{0:T(128)} %bitcast.me_ref, s32[128,128]{1,0:T(8,128)S(1)} %bitcast.27, s32[6,128]{1,0:T(8,128)} %nbr_ref.3, s32[6,128]{1,0:T(8,128)} %wall_ref.3, f32[1,128]{1,0:T(1,128)} %bitcast.31, f32[1,128]{1,0:T(1,128)} %bitcast.33), custom_call_target="tpu_custom_call" | custom-call | tf_op jit(solution)/shard_map/table/pallas_call | solution.py:528
  31.0 28.6 %all-to-all-done.1 = f32[128,32,128]{2,1,0:T(8,128)S(1)} async-done(((f32[128,32,128]{2,1,0:T(8,128)}), f32[128,32,128]{2,1,0:T(8,128)S(1)}, u32[]{:S(2)}, u32[]{:S(2)}) %all-to-all-start.1) | async-done | bytes 2097184 | tf_op jit(solution)/shard_map/all_to_all | solution.py:500
  59.6 4.2 %forward.1 = f32[2048,128]{1,0:T(8,128)S(1)} custom-call(s32[4096]{0:T(1024)S(1)} %bitcast.28, f32[4096,128]{1,0:T(8,128)S(1)} %bitcast.23), custom_call_target="tpu_custom_call" | custom-call | tf_op jit(solution)/shard_map/forward/pallas_call | solution.py:542
  63.8 23.1 %all_to_all.20 = f32[128,16,128]{2,1,0:T(8,128)S(1)} all-to-all(f32[128,16,128]{2,1,0:T(8,128)S(1)} %bitcast.24), channel_id=1, replica_groups=mesh['grp'=4,'dev'=32] {'grp','dev'}, dimensions={0} | all-to-all | bytes 2097152 | tf_op jit(solution)/shard_map/all_to_all | solution.py:500
  86.9 2.2 %arrive.1 = (f32[2048,128]{1,0:T(8,128)S(1)}, f32[128,17,1,128]{3,2,1,0:T(1,128)}) custom-call(s32[8,128]{1,0:T(8,128)S(1)} %get-tuple-element.21.owner_ref, f32[2048,128]{1,0:T(8,128)S(1)} %bitcast.25, s32[16,128]{1,0:T(8,128)S(1)} %get-tuple-element.24.row_ref, f32[128,128]{1,0:T(8,128)S(1)} %get-tuple-element.25.cols_ref), custom_call_target="tpu_custom_call" | custom-call | tf_op jit(solution)/shard_map/arrive/pallas_call | solution.py:551
  89.1 4.4 %all-to-all-start.3 = ((f32[128,17,1,128]{3,2,1,0:T(1,128)}), f32[128,17,1,128]{3,2,1,0:T(1,128)S(1)}, u32[]{:S(2)}, u32[]{:S(2)}) async-start(f32[128,17,1,128]{3,2,1,0:T(1,128)} %get-tuple-element.26), calls=%async_computation.3 | async-start | bytes 2228224 | tf_op jit(solution)/shard_map/all_to_all | solution.py:500
  93.5 4.1 %volume.1 = (f32[2048,128]{1,0:T(8,128)}, f32[384,128]{1,0:T(8,128)S(1)}, f32[384,128]{1,0:T(8,128)S(1)}, f32[384,128]{1,0:T(8,128)S(1)}, s32[384,128]{1,0:T(8,1...) custom-call(s32[1]{0:T(128)} %bitcast.me_ref, f32[2048,128]{1,0:T(8,128)S(1)} %get-tuple-element.27.state_ref, ...), custom_call_target="tpu_custom_call" | custom-call | tf_op jit(solution)/shard_map/volume/pallas_call | solution.py:561
  97.6 15.9 %all-to-all-done.3.recv_ref = f32[128,17,1,128]{3,2,1,0:T(1,128)S(1)} async-done(((f32[128,17,1,128]{3,2,1,0:T(1,128)}), f32[128,17,1,128]{3,2,1,0:T(1,128)S(1)}, u32[]{:S(2)}, u32[]{:S(2)}) %all-to-all-start.3) | async-done | bytes 1114144 | tf_op jit(solution)/shard_map/all_to_all | solution.py:500
  113.6 3.3 %flux.1 = f32[2048,128]{1,0:T(8,128)} custom-call(s32[8,128]{1,0:T(8,128)S(1)} %get-tuple-element.21.owner_ref, f32[128,17,1,128]{3,2,1,0:T(1,128)S(1)} %all-to-all-done.3.recv_ref, f32[2048,128]{1,0:T(8,128)} %get-tuple-element.28.vol_hbm, f32[384,128]{1,0:T(8,128)S(1)} %get-tuple-element.29.near_ref, s32[384,128]{1,0:T(8,128)S(1)} %get-tuple-element.30.index_ref, ...), custom_call_target="tpu_custom_call" | custom-call | tf_op jit(solution)/shard_map/flux/pallas_call | solution.py:580
Async XLA Ops:
  0.0 0.7 copy-start.1
  1.7 21.1 %all-to-all-start = ((s32[128,1,128]{2,1,0:T(1,128)}), s32[128,1,128]{2,1,0:T(1,128)S(1)}, u32[]{:S(2)}, u32[]{:S(2)}) async-start(s32[128,1,128]{2,1,0:T(1,128)} %bitcast.3), calls=%async_computation | async-start | bytes 131072 | tf_op jit(solution)/shard_map/all_to_all | solution.py:500
  13.2 1.6 %copy-start = (f32[256,4,512]{2,1,0:T(4,128)S(1)}, f32[256,4,512]{2,1,0:T(4,128)}, u32[]{:S(2)}) copy-start(f32[256,4,512]{2,1,0:T(4,128)} %param.10) | copy-start | bytes 6291460
  14.8 0.7 copy-start.2
  22.8 36.9 %all-to-all-start.1 = ((f32[128,32,128]{2,1,0:T(8,128)}), f32[128,32,128]{2,1,0:T(8,128)S(1)}, u32[]{:S(2)}, u32[]{:S(2)}) async-start(f32[128,32,128]{2,1,0:T(8,128)} %bitcast.11), calls=%async_computation.1 | async-start | bytes 4194304 | tf_op jit(solution)/shard_map/all_to_all | solution.py:500
  89.1 24.5 %all-to-all-start.3 = ((f32[128,17,1,128]{3,2,1,0:T(1,128)}), f32[128,17,1,128]{3,2,1,0:T(1,128)S(1)}, u32[]{:S(2)}, u32[]{:S(2)}) async-start(f32[128,17,1,128]{3,2,1,0:T(1,128)} %get-tuple-element.26), calls=%async_computation.3 | async-start | bytes 2228224 | tf_op jit(solution)/shard_map/all_to_all | solution.py:500

commit v3 on v2

v3 whole, which is shorter than its diff:
```python
import jax
import jax.numpy as jnp
import numpy as np
from jax import lax
from jax.experimental import pallas as pl
from jax.experimental.pallas import tpu as pltpu
from jax.sharding import PartitionSpec as P

NP = 8
DEVS = 128
LANES = 128
AXES = ("grp", "dev")
metric_scale = 0.25
F32 = jnp.float32
I32 = jnp.int32
BF16 = jnp.bfloat16
VMEM = pltpu.MemorySpace.VMEM
SMEM = pltpu.MemorySpace.SMEM
HBM = pltpu.MemorySpace.HBM


def gll_tables(poly_order):
    num_points = poly_order + 1
    points = -np.cos(np.pi * np.arange(num_points) / poly_order)
    legendre = np.zeros((num_points, num_points))
    for sweeps in range(101):
        legendre[:, 0] = 1.0
        legendre[:, 1] = points
        for degree in range(2, num_points):
            legendre[:, degree] = (
                (2 * degree - 1) * points * legendre[:, degree - 1]
                - (degree - 1) * legendre[:, degree - 2]
            ) / degree
        if sweeps < 100:
            points = points - (points * legendre[:, poly_order] - legendre[:, poly_order - 1]) / (
                num_points * legendre[:, poly_order]
            )
    end_values = legendre[:, poly_order]
    weights = 2.0 / (poly_order * num_points * end_values**2)
    distance = points[:, None] - points[None, :] + np.eye(num_points)
    derivative = end_values[:, None] / end_values[None, :] / distance
    derivative = derivative * (1.0 - np.eye(num_points))
    derivative[0, 0] = -poly_order * num_points / 4.0
    derivative[poly_order, poly_order] = poly_order * num_points / 4.0
    return (points, weights, derivative)


POINTS, WEIGHTS, DERIV = gll_tables(NP - 1)
DERIV = DERIV.astype(np.float32)
LIFT = metric_scale / float(WEIGHTS[0])


def derivative_tables():
    eye2, eye8 = np.eye(2, dtype=np.float32), np.eye(8, dtype=np.float32)
    along_y = np.kron(eye2, np.kron(DERIV.T, eye8))
    along_z = np.kron(eye2, np.kron(eye8, DERIV.T))
    side = np.concatenate([along_y, along_z], axis=1)
    stacked = np.concatenate([along_y, along_z], axis=0)
    coef = np.zeros((4, 4, 2, LANES), np.float32)
    for out_chunk in range(4):
        for in_chunk in range(4):
            for half in range(2):
                lanes = slice(64 * half, 64 * half + 64)
                coef[out_chunk, in_chunk, 0, lanes] = DERIV[2 * out_chunk + half, 2 * in_chunk + half]
                coef[out_chunk, in_chunk, 1, lanes] = DERIV[
                    2 * out_chunk + half, 2 * in_chunk + 1 - half
                ]
    return side, stacked, coef.reshape(32, LANES)


SIDE, STACKED, COEF = derivative_tables()


def iota(shape, axis):
    return lax.broadcasted_iota(I32, shape, axis)


def small_dot(left, right):
    return jnp.dot(left.astype(BF16), right.astype(BF16), preferred_element_type=F32)


def split3(value):
    high = value.astype(BF16)
    rest = value - high.astype(F32)
    middle = rest.astype(BF16)
    low = (rest - middle.astype(F32)).astype(BF16)
    return high, middle, low


def pick_dot(pick, value):
    pick = pick.astype(BF16)
    high, middle, low = split3(value)
    total = jnp.dot(pick, high, preferred_element_type=F32)
    total = total + jnp.dot(pick, middle, preferred_element_type=F32)
    return total + jnp.dot(pick, low, preferred_element_type=F32)


def column(row, diag):
    wide = jnp.broadcast_to(row, (LANES, LANES))
    return jnp.sum(jnp.where(diag, wide, 0.0), axis=1, keepdims=True)


def half_sign(shape):
    return jnp.where(iota(shape, 1) < 64, -1.0, 1.0)


def face_pair(chunk, axis, zed):
    lane = iota((LANES, LANES), 1)
    half, face_i, face_b = lane >> 6, (lane >> 3) & 7, lane & 7
    from_y = (face_i & 1) * 64 + half * 56 + face_b
    from_z = (face_i & 1) * 64 + face_b * 8 + half * 7
    values = []
    for field in (0, 1 + axis):
        if axis == 0:
            value = jnp.where(lane < 64, chunk(field, 0), chunk(field, 3))
        else:
            index = from_y if axis == 1 else from_z
            value = jnp.take_along_axis(chunk(field, 0), index, axis=1)
            for n4 in range(1, 4):
                other = jnp.take_along_axis(chunk(field, n4), index, axis=1)
                value = jnp.where(face_i >> 1 == n4, other, value)
        values.append(value)
    normal = half_sign((LANES, LANES)) * values[1]
    return values[0], normal, values[0] + zed * normal


def cross(arrays, bit1, bit0):
    first = [jnp.where(bit0, arrays[t ^ 1], arrays[t]) for t in range(4)]
    return [jnp.where(bit1, first[t ^ 2], first[t]) for t in range(4)]


def lane_bit(lane, bit):
    return ((lane >> bit) & 1) == 1


def regroup(arrays, back):
    lane = iota(arrays[0].shape, 1)
    own = (lane >> 3) & 3
    plain = (lane_bit(lane, 1), lane_bit(lane, 0))
    mixed = (lane_bit(lane ^ (lane >> 3), 1), lane_bit(lane ^ (lane >> 3), 0))
    enter, leave = (plain, mixed) if back else (mixed, plain)
    result = [None] * 16
    for top in range(4):
        four = cross(arrays[4 * top : 4 * top + 4], *enter)
        four = [jnp.take_along_axis(four[t], lane ^ t ^ own, axis=1) for t in range(4)]
        result[4 * top : 4 * top + 4] = cross(four, *leave)
    j2, k2 = lane_bit(lane, 5), lane_bit(lane, 2)
    final = [None] * 16
    for t in range(4):
        final[t::4] = cross(result[t::4], j2, k2)
    return final


def order_kernel(me_ref, dest_ref, nbr_ref, wall_ref, info_ref, pos_ref, scr):
    dest = dest_ref[...]
    sub = iota((LANES, LANES), 0)
    lane = iota((LANES, LANES), 1)
    diag = sub == lane
    key_row, key_col, dest_col = [], [], []
    for half in range(2):
        row = jnp.broadcast_to(dest[half : half + 1, :], (LANES, LANES))
        key = (row >> 7).astype(F32) * 256.0 + (lane + 128 * half).astype(F32)
        key_row.append(key)
        key_col.append(jnp.sum(jnp.where(diag, key, 0.0), axis=1, keepdims=True))
        dest_col.append(jnp.sum(jnp.where(diag, row.astype(F32), 0.0), axis=1, keepdims=True))
    lists = [jnp.zeros((1, LANES), F32), jnp.zeros((1, LANES), F32)]
    for half in range(2):
        before_col = jnp.zeros((LANES, 1), F32)
        before_row = jnp.zeros((1, LANES), F32)
        for other in range(2):
            before_col = before_col + jnp.sum(
                jnp.where(key_row[other] < key_col[half], 1.0, 0.0), axis=1, keepdims=True
            )
            before_row = before_row + jnp.sum(
                jnp.where(key_col[other] < key_row[half], 1.0, 0.0), axis=0, keepdims=True
            )
        pos_ref[half : half + 1, :] = before_row.astype(I32)
        place = before_col.astype(I32)
        k = place & 7
        spot = (k & 3) * 32 + (place >> 3)
        for part in range(2):
            hit = (spot == lane) & (k >> 2 == part)
            lists[part] = lists[part] + jnp.sum(jnp.where(hit, dest_col[half], 0.0), axis=0, keepdims=True)
    scr[...] = jnp.full((8, LANES), -1.0, F32)
    owner = nbr_ref[...] >> 7
    remote = (owner != me_ref[0]) & (wall_ref[...] == 0)
    scr[0:6, :] = jnp.where(remote, owner, -1).astype(F32)
    owners = jnp.max(scr[...], axis=1, keepdims=True)
    spread = iota((8, LANES), 0) == iota((8, LANES), 1)
    owner_row = jnp.sum(jnp.where(spread, owners, 0.0), axis=0, keepdims=True)
    for part, row in enumerate((lists[0], lists[1], owner_row)):
        info_ref[pl.ds(part, LANES, stride=3), :] = jnp.broadcast_to(row, (LANES, LANES)).astype(I32)


def pack_kernel(pos_ref, dest_ref, state_ref, bulk_ref, dens_ref, out_ref, scr):
    zed = jnp.sqrt(bulk_ref[...] * dens_ref[...])
    out_ref[pl.ds(32, LANES, stride=33), :] = jnp.broadcast_to(zed, (LANES, LANES))

    @pl.when(dest_ref[0, 0] >= 0)
    def _():
        def one(slot, carry):
            place = pos_ref[slot >> 7, slot & 127]
            start = (place & 7) * 512 + (place >> 3)
            scr[pl.ds(start, 16, stride=32), :] = state_ref[pl.ds(pl.multiple_of(slot * 16, 16), 16), :]
            return carry

        lax.fori_loop(0, 256, one, 0, unroll=8)
        for k in range(8):
            for block in range(4):
                at = [(k * 16 + c) * 32 + block * 8 for c in range(16)]
                groups = regroup([scr[a : a + 8, :] for a in at], False)
                for g in range(16):
                    row = (k * 16 + g) * 33 + block * 8
                    out_ref[row : row + 8, :] = groups[g]


def table_kernel(
    me_ref, info_ref, nbr_ref, wall_ref, orient_ref, bulk_ref, dens_ref,
    spot_ref, owner_ref, row_ref, label_ref, cols_ref, far_ref, near_ref, pick_ref, wide, scr,
):
    shape = (LANES, LANES)
    sub = iota(shape, 0)
    lane = iota(shape, 1)
    diag = sub == lane
    me = me_ref[0]
    bulk = column(bulk_ref[...], diag)
    dens = column(dens_ref[...], diag)
    zed = column(jnp.sqrt(bulk_ref[...] * dens_ref[...]), diag)
    cols_ref[...] = jnp.where(lane == 0, zed, jnp.where(lane == 1, bulk, dens))

    lists = [info_ref[pl.ds(0, LANES, stride=3), :], info_ref[pl.ds(1, LANES, stride=3), :]]
    owners = info_ref[pl.ds(2, LANES, stride=3), :].astype(F32)
    owner_ref[...] = owners.T[0:8, :].astype(I32)
    target = lists[0] >> 7
    my_k = me >> 4
    mine = jnp.where(my_k >= 4, lists[1], lists[0])
    mine = jnp.take_along_axis(mine, (my_k & 3) * 32 + (lane & 31), axis=1) & 127
    present = jnp.zeros(shape, F32)
    label = jnp.zeros(shape, F32)
    mine = mine.astype(F32)
    for j in range(32):
        hit = target[:, j : j + 1] == lane
        present = jnp.where(hit, 1.0, present)
        label = jnp.where(hit, mine[:, j : j + 1], label)
    below = jnp.where(lane < sub, 1.0, 0.0)
    rank = small_dot(below, present)
    safe = jnp.clip(target, 0, LANES - 1)
    slot = safe * 16 + jnp.take_along_axis(rank.astype(I32), safe, axis=1)
    wide[...] = jnp.where(target >= 0, slot, -1)
    quarter = iota((32, LANES), 1) >> 5
    spots = wide[pl.ds(0, 32, stride=4), :]
    for part in range(1, 4):
        moved = pltpu.roll(wide[pl.ds(part, 32, stride=4), :], 32 * part, 1)
        spots = jnp.where(quarter == part, moved, spots)
    spot_ref[...] = spots
    order = jnp.where(present > 0.0, rank, -1.0)
    labels = jnp.zeros(shape, F32)
    for i in range(16):
        row = jnp.sum(jnp.where(order == float(i), label, 0.0), axis=0, keepdims=True)
        labels = jnp.where(sub == i, row, labels)
    label_ref[...] = labels.T.astype(I32)

    gather = [jnp.where((sub >> 5) + 4 * part == lane >> 4, 1.0, 0.0) for part in range(2)]

    def rows_of(block):
        value = jnp.zeros(shape, F32)
        for part in range(2):
            held = jnp.where(lists[part] >> 7 == block, (lists[part] & 127).astype(F32), 0.0)
            value = value + small_dot(held, gather[part])
        source = jnp.sum(jnp.where(lane == block, order, 0.0), axis=1, keepdims=True)
        chosen = source == (lane & 15).astype(F32)
        return jnp.sum(jnp.where(chosen, value, 0.0), axis=0, keepdims=True)

    row_ref[...] = jnp.broadcast_to(rows_of(me), (8, LANES)).astype(I32)
    scr[...] = jnp.full((8, LANES), -1.0, F32)
    nbr_all = nbr_ref[...]
    away_all = ((nbr_all >> 7) != me) & (wall_ref[...] == 0)
    scr[0:6, :] = jnp.where(away_all, nbr_all >> 7, -1).astype(F32)
    neighbour = jnp.max(scr[...], axis=1, keepdims=True).astype(I32)
    low_half = lane < 64
    picks = jnp.zeros(shape, F32)
    for axis in range(3):
        lanes = slice(axis * LANES, axis * LANES + LANES)
        places, codes, walls = [], [], []
        for side in range(2):
            face = 2 * axis + side
            nbr = nbr_ref[face : face + 1, :]
            is_wall = wall_ref[face : face + 1, :] == 1
            remote = ((nbr >> 7) != me) & jnp.logical_not(is_wall)
            wanted = column(jnp.where(remote, nbr & 127, -1).astype(F32), diag)
            hit = rows_of(neighbour[face : face + 1, :]) == wanted
            place = jnp.sum(jnp.where(hit, lane.astype(F32), 0.0), axis=1, keepdims=True).astype(I32)
            places.append(place >> 4)
            chosen = (lane >> 4 == face) & (lane & 15 == place & 15) & (wanted >= 0.0)
            picks = jnp.where(chosen, 1.0, picks)
            codes.append(column(orient_ref[face : face + 1, :].astype(F32), diag).astype(I32))
            walls.append(column(jnp.where(is_wall, 1.0, 0.0), diag))
        code = jnp.where(low_half, codes[0], codes[1])
        code = jnp.where(jnp.where(low_half, walls[0], walls[1]) > 0.0, 0, code)
        a, b = (lane >> 3) & 7, lane & 7
        swap = code >= 4
        a1, b1 = jnp.where(swap, b, a), jnp.where(swap, a, b)
        a2 = jnp.where((code & 1) == 1, 7 - a1, a1)
        b2 = jnp.where((code & 2) == 2, 7 - b1, b1)
        near_ref[lanes, :] = jnp.where(low_half, 64, 0) + a2 * 8 + b2
        h = jnp.where(low_half, 1, 0)
        if axis == 0:
            top = ((a2 >> 2) ^ h) * 8 + ((b2 >> 2) ^ h) * 4
            group, v = top + ((a2 ^ b2) & 3), a2 & 3
        elif axis == 1:
            top = ((a2 >> 2) ^ h) * 8 + (((a2 >> 1) & 1) ^ (b2 >> 2)) * 4
            group, v = top + ((b2 & 3) ^ (h * 3)), (a2 & 1) * 2 + (b2 >> 2)
        else:
            top = ((a2 >> 2) ^ (b2 >> 2)) * 8 + (((a2 >> 1) & 1) ^ h) * 4
            group, v = top + ((b2 & 3) ^ (h * 3)), (a2 & 1) * 2 + (b2 >> 2)
        far_ref[lanes, :] = jnp.where(low_half, places[0], places[1]) * 16 + group + 128 * v
    pick_ref[...] = picks


SHIFT_A, SHIFT_B = (3, 9)


def shift_of(i):
    return (i & 3) ^ ((i >> 2) & 1) * (4 * SHIFT_A) ^ (i >> 3) * (4 * SHIFT_B)


def forward_kernel(me_ref, spot_ref, owner_ref, in_ref, label_ref, out_ref, zed_ref, held, faces):
    def one(source, carry):
        base = pl.multiple_of(source * 32, 32)

        @pl.when(spot_ref[base] >= 0)
        def _():
            for j in range(32):
                held[pl.ds(spot_ref[base + j], 1), :] = in_ref[pl.ds(source * 33 + j, 1), :]

        return carry

    lax.fori_loop(0, DEVS, one, 0)
    shape = (LANES, LANES)
    lane = iota(shape, 1)
    zeds = in_ref[pl.ds(32, LANES, stride=33), :]
    zed_ref[...] = zeds
    zed = jnp.take_along_axis(zeds, label_ref[...], axis=1)
    me = me_ref[0]
    g3, g2, g1, g0 = (me >> 3) & 1, (me >> 2) & 1, (me >> 1) & 1, me & 1
    lane = iota((8, LANES), 1)
    h, v1, v0 = lane >> 6, (lane >> 1) & 1, lane & 1
    nodes = [
        h * 16 + (g3 ^ h) * 8 + v1 * 4 + v0 * 2 + (g2 ^ h),
        v1 * 16 + h * 14 + v0,
        v1 * 16 + v0 * 8 + (g1 ^ h) * 4 + (g0 ^ h) * 2 + h,
    ]
    here = (lane >> 2) & 15
    shift = (here & 3) ^ ((here >> 2) & 1) * (4 * SHIFT_A) ^ (here >> 3) * (4 * SHIFT_B)
    which = []
    for axis in range(3):
        for field in (0, 1 + axis):
            value = jnp.full((8, LANES), -1, I32)
            for i in range(16):
                spot = lane ^ shift_of(i)
                n = spot >> 2
                i0, j2, j1, j0, k2 = (n >> 4) & 1, (n >> 3) & 1, (n >> 2) & 1, (n >> 1) & 1, n & 1
                if axis == 0:
                    hit = (j2 == g3 ^ i0) & (k2 == g2 ^ i0)
                elif axis == 1:
                    hit = (j2 == j1) & (j1 == j0)
                else:
                    hit = (j1 == g1 ^ k2) & (j0 == g0 ^ k2)
                value = jnp.where(hit & (spot & 3 == field), i, value)
            which.append(value)
    sign = half_sign((8, LANES))
    for block in range(16):
        merged = [jnp.zeros((8, LANES), F32)] * 6
        for i in range(16):
            rows = held[pl.ds(block * 128 + i, 8, stride=16), :]
            rows = jnp.take_along_axis(rows, lane ^ shift_of(i), axis=1)
            for m in range(6):
                merged[m] = jnp.where(which[m] == i, rows, merged[m])
        wide = jnp.take_along_axis(zed[block * 8 : block * 8 + 8, :], here, axis=1) * sign
        for axis in range(3):
            press = jnp.take_along_axis(merged[2 * axis], (nodes[axis] * 4) ^ shift, axis=1)
            speed = jnp.take_along_axis(merged[2 * axis + 1], (nodes[axis] * 4 + 1 + axis) ^ shift, axis=1)
            at = axis * LANES + block * 8
            faces[at : at + 8, :] = press + wide * speed
        for target in range(block * 8, block * 8 + 8):
            out_ref[target * 19 : target * 19 + 16, :] = held[target * 16 : target * 16 + 16, :]
    low = iota((1, LANES), 1) < 64

    def two(target, carry):
        for axis in range(3):
            lower = jnp.maximum(owner_ref[2 * axis * LANES + target], 0)
            upper = jnp.maximum(owner_ref[(2 * axis + 1) * LANES + target], 0)
            row = jnp.where(
                low, faces[pl.ds(axis * LANES + upper, 1), :], faces[pl.ds(axis * LANES + lower, 1), :]
            )
            out_ref[pl.ds(target * 19 + 16 + axis, 1), :] = row
        return carry

    lax.fori_loop(0, DEVS, two, 0, unroll=4)


def across_kernel(me_ref, owner_ref, zed_ref, nbr_ref, wall_ref, out_ref):
    shape = (LANES, LANES)
    lane = iota(shape, 1)
    diag = iota(shape, 0) == lane
    me = me_ref[0]
    own = zed_ref[pl.ds(me, 1), :]
    total = jnp.zeros(shape, F32)
    for face in range(6):
        other = zed_ref[pl.ds(jnp.maximum(owner_ref[face * LANES + me], 0), 1), :]
        nbr = nbr_ref[face : face + 1, :]
        remote = ((nbr >> 7) != me) & (wall_ref[face : face + 1, :] == 0)
        far = column(jnp.where(remote, 1.0, 0.0), diag) > 0.0
        spot = column((nbr & 127).astype(F32), diag) == lane.astype(F32)
        value = jnp.where(spot, jnp.where(far, other, own), 0.0)
        total = jnp.where(lane == face, jnp.sum(value, axis=1, keepdims=True), total)
    out_ref[...] = total


def final_kernel(
    me_ref, in_ref, row_ref, cols_ref, zed_ref, far_ref, near_ref, pick_ref, nbr_ref, wall_ref,
    side_ref, stack_ref, coef_ref, out_ref, state, turned,
):
    shape = (LANES, LANES)
    lane = iota(shape, 1)
    diag = iota(shape, 0) == lane
    low_half = lane < 64
    place = jnp.where(row_ref[0:1, :] == iota(shape, 0), 1.0, 0.0).astype(BF16)
    place = jnp.concatenate([place, place, place], axis=1)
    for group in range(0, 16, 2):
        pair = []
        for g in (group, group + 1):
            rows = [in_ref[(k * 16 + g) * 19 : (k * 16 + g) * 19 + 16, :] for k in range(8)]
            pair.append(jnp.concatenate(rows, axis=0))
        parts = split3(jnp.concatenate(pair, axis=1))
        moved = jnp.dot(place, jnp.concatenate(parts, axis=0), preferred_element_type=F32)
        state[group * LANES : (group + 1) * LANES, :] = moved[:, 0:LANES]
        state[(group + 1) * LANES : (group + 2) * LANES, :] = moved[:, LANES:]
    for block in range(16):
        at = [c * LANES + block * 8 for c in range(16)]
        chunks = regroup([state[a : a + 8, :] for a in at], True)
        for c in range(16):
            state[at[c] : at[c] + 8, :] = chunks[c]

    def chunk(field, n4):
        start = (n4 * 4 + field) * LANES
        return state[start : start + LANES, :]

    zed, bulk, dens = cols_ref[:, 0:1], cols_ref[:, 1:2], cols_ref[:, 2:3]
    me = me_ref[0]
    i2, j, k = lane >> 6, (lane >> 3) & 7, lane & 7
    sign = half_sign(shape)
    lifts = []
    for axis in range(3):
        rows = slice(axis * LANES, axis * LANES + LANES)
        press, norm, wave = face_pair(chunk, axis, zed)
        turned[...] = in_ref[pl.ds(16 + axis, LANES, stride=19), :].T
        nears, walls, fars = [], [], []
        for side in range(2):
            face = 2 * axis + side
            nbr = nbr_ref[face : face + 1, :]
            is_wall = wall_ref[face : face + 1, :] == 1
            local = ((nbr >> 7) == me) & jnp.logical_not(is_wall)
            spot = column(jnp.where(local, nbr & 127, -1).astype(F32), diag)
            nears.append(jnp.where(spot == lane.astype(F32), 1.0, 0.0))
            walls.append(column(jnp.where(is_wall, 1.0, 0.0), diag))
            table = [turned[pl.ds((1 - side) * 64 + v, 16, stride=4), :] for v in range(4)]
            pick = pick_ref[:, face * 16 : face * 16 + 16]
            fars.append(pick_dot(pick, jnp.concatenate(table, axis=1)))
        masked = jnp.concatenate([jnp.where(low_half, 0.0, wave), jnp.where(low_half, wave, 0.0)], axis=0)
        near = pick_dot(jnp.concatenate(nears, axis=1), masked)
        own = jnp.where(low_half, walls[1], walls[0]) > 0.0
        near = jnp.where(own, pltpu.roll(wave, 64, 1), near)
        wave_out = jnp.take_along_axis(near, near_ref[rows, :], axis=1)
        code = far_ref[rows, :]
        index, part = code & 127, code >> 7
        far = jnp.zeros(shape, F32)
        for v in range(4):
            below = jnp.take_along_axis(fars[0][:, v * LANES : (v + 1) * LANES], index, axis=1)
            above = jnp.take_along_axis(fars[1][:, v * LANES : (v + 1) * LANES], index, axis=1)
            far = jnp.where(part == v, jnp.where(low_half, below, above), far)
        zed_out = jnp.where(low_half, zed_ref[:, 2 * axis : 2 * axis + 1], zed_ref[:, 2 * axis + 1 : 2 * axis + 2])
        lifts.append((wave_out + far - press + zed_out * norm) / (zed + zed_out))

    high = lax.Precision.HIGHEST
    by_bulk = -metric_scale * bulk
    by_dens = -(metric_scale / dens)
    up = LIFT * bulk
    across = -LIFT * zed / dens
    swapped = {}
    for field in (0, 1):
        for n4 in range(4):
            swapped[field, n4] = pltpu.roll(chunk(field, n4), 64, 1)
    for n4 in range(4):
        along = {}
        for field in (0, 1):
            total = None
            for m4 in range(4):
                at = (n4 * 4 + m4) * 2
                term = chunk(field, m4) * coef_ref[at : at + 1, :]
                term = term + swapped[field, m4] * coef_ref[at + 1 : at + 2, :]
                total = term if total is None else total + term
            along[field] = total
        both = jnp.concatenate([chunk(2, n4), chunk(3, n4)], axis=1)
        div = along[1] + jnp.dot(both, stack_ref[...], precision=high, preferred_element_type=F32)
        grad = jnp.dot(chunk(0, n4), side_ref[...], precision=high, preferred_element_type=F32)
        grads = [along[0], grad[:, 0:LANES], grad[:, LANES:]]
        face_i = 2 * n4 + i2
        from_y = jnp.where(j == 7, 64, 0) + face_i * 8 + k
        from_z = jnp.where(k == 7, 64, 0) + face_i * 8 + j
        on_y = (j == 0) | (j == 7)
        on_z = (k == 0) | (k == 7)
        total = jnp.zeros(shape, F32)
        for axis in range(3):
            jump = lifts[axis]
            value = by_dens * grads[axis]
            here = None
            if axis == 0 and n4 == 0:
                here = jnp.where(low_half, jump, 0.0)
                turn = -here
            elif axis == 0 and n4 == 3:
                here = jnp.where(low_half, 0.0, jump)
                turn = here
            elif axis == 1:
                here = jnp.where(on_y, jnp.take_along_axis(jump, from_y, axis=1), 0.0)
                turn = jnp.where(j == 0, -here, here)
            elif axis == 2:
                here = jnp.where(on_z, jnp.take_along_axis(jump, from_z, axis=1), 0.0)
                turn = jnp.where(k == 0, -here, here)
            if here is not None:
                value = value + across * turn
                total = total + here
            out_ref[pl.ds(n4 * 4 + 1 + axis, LANES, stride=16), :] = value
        out_ref[pl.ds(n4 * 4, LANES, stride=16), :] = by_bulk * div + up * total


def vm():
    return pl.BlockSpec(memory_space=VMEM)


def sm():
    return pl.BlockSpec(memory_space=SMEM)


def shaped(shape, dtype=F32):
    return VMEM(shape, dtype)


def plain(shape, dtype=F32):
    return jax.ShapeDtypeStruct(shape, dtype)


def near(value):
    return pltpu.with_memory_space_constraint(value, VMEM)


def away(value):
    return pltpu.with_memory_space_constraint(value, HBM)


GRANT = pltpu.CompilerParams(vmem_limit_bytes=24 * 1024 * 1024)


def exchange(flat, rows):
    blocks = flat.reshape(DEVS, rows, 1, LANES)
    return lax.all_to_all(blocks, AXES, split_axis=0, concat_axis=0, tiled=True).reshape(flat.shape)


def body(old_state, dest_row, neighbours, orientation, wall_flags, bulk_modulus, density):
    me = (lax.axis_index("grp") * lax.axis_size("dev") + lax.axis_index("dev")).astype(I32).reshape(1)
    dest = dest_row.reshape(2, LANES)
    bulk = away(bulk_modulus.reshape(1, LANES))
    dens = away(density.reshape(1, LANES))
    nbr, wall, orient = away(neighbours), away(wall_flags), away(orientation)
    state = old_state.reshape(256, 4, 4, LANES).transpose(0, 2, 1, 3).reshape(4096, LANES)

    info, pos = pl.pallas_call(
        order_kernel,
        in_specs=[sm()] + [vm()] * 3,
        out_specs=[vm()] * 2,
        out_shape=[shaped((384, LANES), I32), plain((2, LANES), I32)],
        scratch_shapes=[pltpu.VMEM((8, LANES), F32)],
        name="order",
        compiler_params=GRANT,
    )(me, away(dest), nbr, wall)
    heard = exchange(info, 3)
    pieces = pl.pallas_call(
        pack_kernel,
        in_specs=[sm(), sm()] + [vm()] * 3,
        out_specs=vm(),
        out_shape=HBM((4224, LANES), F32),
        scratch_shapes=[pltpu.VMEM((4096, LANES), F32)],
        name="pack",
        compiler_params=GRANT,
    )(pos, dest, away(state), bulk, dens)
    spread = exchange(pieces, 33)
    spots, owners, rows, labels, cols, far, close, pick = pl.pallas_call(
        table_kernel,
        in_specs=[sm()] + [vm()] * 6,
        out_specs=[vm()] * 8,
        out_shape=[
            shaped((32, LANES), I32),
            shaped((8, LANES), I32),
            shaped((8, LANES), I32),
            shaped((LANES, LANES), I32),
            shaped((LANES, LANES)),
            HBM((384, LANES), I32),
            HBM((384, LANES), I32),
            shaped((LANES, LANES)),
        ],
        scratch_shapes=[pltpu.VMEM((LANES, LANES), I32), pltpu.VMEM((8, LANES), F32)],
        name="table",
        compiler_params=GRANT,
    )(me, near(heard), nbr, wall, orient, bulk, dens)
    owners = owners.reshape(1024)
    passed, zeds = pl.pallas_call(
        forward_kernel,
        in_specs=[sm()] * 3 + [vm()] * 2,
        out_specs=[vm()] * 2,
        out_shape=[shaped((2432, LANES)), shaped((LANES, LANES))],
        scratch_shapes=[pltpu.VMEM((2048, LANES), F32), pltpu.VMEM((384, LANES), F32)],
        name="forward",
        compiler_params=GRANT,
    )(me, spots.reshape(4096), owners, near(spread), near(labels))
    arrived = exchange(passed, 19)
    zed_out = pl.pallas_call(
        across_kernel,
        in_specs=[sm()] * 2 + [vm()] * 3,
        out_specs=vm(),
        out_shape=shaped((LANES, LANES)),
        name="across",
        compiler_params=GRANT,
    )(me, owners, near(zeds), nbr, wall)
    result = pl.pallas_call(
        final_kernel,
        in_specs=[sm()] + [vm()] * 12,
        out_specs=vm(),
        out_shape=plain((2048, LANES)),
        scratch_shapes=[pltpu.VMEM((2048, LANES), F32), pltpu.VMEM((LANES, LANES), F32)],
        name="final",
        compiler_params=GRANT,
    )(
        me, near(arrived), near(rows), near(cols), near(zed_out), away(far), away(close), near(pick), nbr, wall,
        away(jnp.asarray(SIDE)), away(jnp.asarray(STACKED)), away(jnp.asarray(COEF)),
    )
    return result.reshape(128, 4, 4, LANES).transpose(0, 2, 1, 3).reshape(128, 4, 512)


def solution(mesh):
    both = P(AXES)
    faces = P(None, AXES)
    in_specs = (P(AXES, None, None), both, faces, faces, faces, both, both)
    return jax.shard_map(
        body, mesh=mesh, in_specs=in_specs, out_specs=P(AXES, None, None), check_vma=False
    )
```

time: 117 us -> 103 us (0.88)
  blocking collectives: 23.1 us -> 0 us
  Pallas kernels: 20.5 us -> 29.5 us
  local copies, waits for them, and re-layouts: 2.94 us -> 0.67 us
  waiting for transfers between devices: 47.9 us -> 50.1 us
    all_to_all x1 -> x0, blocking collectives: 23.1 us -> none  [exchange(): return lax.all_to_all(value, AXES, split_axis=0, concat_axis=0, tiled=True)]
    pallas_call x7 -> x6, Pallas kernels: 20.5 us -> 29.5 us  [the longest x1 8.47 us: body(): pl.pallas_call(forward_kernel, in_specs=[sm()] * 3 + [vm()] * 2, out_spec...]
    unnamed x6 -> x2, local copies, waits for them, and re-layouts: 2.94 us -> 0.67 us
    all_to_all x3, waiting for transfers between devices: 47.9 us -> 50.1 us  [exchange(): lax.all_to_all(blocks, AXES, split_axis=0, concat_axis=0, tiled=True)]
  transfers between devices with their start and end apart: 3 -> 3, of which waited for: 3 -> 3; matrix products, arithmetic and copies ran while one was open for 0% -> 0% of each run, Pallas kernels for 8% -> 12%
where the time goes in v3:
time: 103 us
  waiting for transfers between devices  50.1 us (49%)
  Pallas kernels  29.5 us (29%)
  starting transfers between devices  22.3 us (22%)
    all_to_all x3, waiting for transfers between devices, exchange(): lax.all_to_all(blocks, AXES, split_axis=0, concat_axis=0, tiled=True)  50.1 us
    all_to_all x3, starting transfers between devices, exchange(): lax.all_to_all(blocks, AXES, split_axis=0, concat_axis=0, tiled=True)  22.3 us
    pallas_call x1, Pallas kernels, body(): pl.pallas_call(forward_kernel, in_specs=[sm()] * 3 + [vm()] * 2, out_spec...  8.47 us
    pallas_call x1, Pallas kernels, body(): pl.pallas_call(final_kernel, in_specs=[sm()] + [vm()] * 12, out_specs=vm(...  6.96 us
    pallas_call x1, Pallas kernels, body(): pl.pallas_call(pack_kernel, in_specs=[sm(), sm()] + [vm()] * 3, out_specs...  6.56 us
    pallas_call x1, Pallas kernels, body(): pl.pallas_call(table_kernel, in_specs=[sm()] + [vm()] * 6, out_specs=[vm(...  4.5 us
  transfers between devices with their start and end apart: 3, of which 3 were waited for; matrix products, arithmetic and copies ran while one was open for 0% of the time, Pallas kernels for 12%

profile of v3, /device:TPU:1, one launch (start us, length us, event | category | flops | bytes accessed | tf_op | source)
XLA Modules:
  0.0 102.6 jit_solution(14060748957849343035)
XLA Ops:
  0.0 1.7 %order.1 = (s32[384,128]{1,0:T(8,128)}, s32[2,128]{1,0:T(2,128)S(1)}) custom-call(s32[1]{0:T(128)} %bitcast.me_ref, s32[2,128]{1,0:T(2,128)} %bitcast.28, s32[6,128]{1,0:T(8,128)} %nbr_ref.7, s32[6,128]{1,0:T(8,128)} %wall_ref.7), custom_call_target="tpu_custom_call" | custom-call | tf_op jit(solution)/shard_map/order/pallas_call | solution.py:577
  1.7 11.5 %all-to-all-start = ((s32[128,3,1,128]{3,2,1,0:T(1,128)}), s32[128,3,1,128]{3,2,1,0:T(1,128)S(1)}, u32[]{:S(2)}, u32[]{:S(2)}) async-start(s32[128,3,1,128]{3,2,1,0:T(1,128)} %bitcast.2), calls=%async_computation | async-start | bytes 393216 | tf_op jit(solution)/shard_map/all_to_all | solution.py:566
  13.2 0.0 copy-start
  13.2 0.7 copy-done
  13.8 6.6 %pack.1 = f32[4224,128]{1,0:T(8,128)} custom-call(s32[2,128]{1,0:T(2,128)S(1)} %get-tuple-element.20.pos_ref, s32[2,128]{1,0:T(2,128)S(1)} %bitcast.29, f32[4096,128]{1,0:T(8,128)} %bitcast.31, f32[1,128]{1,0:T(1,128)} %bitcast.32, f32[1,128]{1,0:T(1,128)} %bitcast.34), custom_call_target="tpu_custom_call" | custom-call | tf_op jit(solution)/shard_map/pack/pallas_call | solution.py:587
  20.4 3.3 %all-to-all-done = s32[128,3,1,128]{3,2,1,0:T(1,128)S(1)} async-done(((s32[128,3,1,128]{3,2,1,0:T(1,128)}), s32[128,3,1,128]{3,2,1,0:T(1,128)S(1)}, u32[]{:S(2)}, u32[]{:S(2)}) %all-to-all-start) | async-done | bytes 196640 | tf_op jit(solution)/shard_map/all_to_all | solution.py:566
  23.7 6.5 %all-to-all-start.1 = ((f32[128,33,1,128]{3,2,1,0:T(1,128)}), f32[128,33,1,128]{3,2,1,0:T(1,128)S(1)}, u32[]{:S(2)}, u32[]{:S(2)}) async-start(f32[128,33,1,128]{3,2,1,0:T(1,128)} %bitcast.30), calls=%async_computation.1 | async-start | bytes 4325376 | tf_op jit(solution)/shard_map/all_to_all | solution.py:566
  30.1 4.5 %table.1 = (s32[32,128]{1,0:T(8,128)S(1)}, s32[8,128]{1,0:T(8,128)S(1)}, s32[8,128]{1,0:T(8,128)S(1)}, s32[128,128]{1,0:T(8,128)S(1)}, f32[128,128]{1,0:T(8,128)...) custom-call(s32[1]{0:T(128)} %bitcast.me_ref, s32[384,128]{1,0:T(8,128)S(1)} %bitcast.24, ...), custom_call_target="tpu_custom_call" | custom-call | tf_op jit(solution)/shard_map/table/pallas_call | solution.py:597
  34.7 26.7 %all-to-all-done.1 = f32[128,33,1,128]{3,2,1,0:T(1,128)S(1)} async-done(((f32[128,33,1,128]{3,2,1,0:T(1,128)}), f32[128,33,1,128]{3,2,1,0:T(1,128)S(1)}, u32[]{:S(2)}, u32[]{:S(2)}) %all-to-all-start.1) | async-done | bytes 2162720 | tf_op jit(solution)/shard_map/all_to_all | solution.py:566
  61.3 8.5 %forward.1 = (f32[2432,128]{1,0:T(8,128)}, f32[128,128]{1,0:T(8,128)S(1)}) custom-call(s32[1]{0:T(128)} %bitcast.me_ref, s32[4096]{0:T(1024)S(1)} %bitcast.25, s32[1024]{0:T(1024)S(1)} %bitcast.26, f32[4224,128]{1,0:T(8,128)S(1)} %bitcast.22, s32[128,128]{1,0:T(8,128)S(1)} %get-tuple-element.21.label_ref), custom_call_target="tpu_custom_call" | custom-call | tf_op jit(solution)/shard_map/forward/pallas_call | solution.py:616
  69.8 4.4 %all-to-all-start.2 = ((f32[128,19,1,128]{3,2,1,0:T(1,128)}), f32[128,19,1,128]{3,2,1,0:T(1,128)S(1)}, u32[]{:S(2)}, u32[]{:S(2)}) async-start(f32[128,19,1,128]{3,2,1,0:T(1,128)} %bitcast.13), calls=%async_computation.2 | async-start | bytes 2490368 | tf_op jit(solution)/shard_map/all_to_all | solution.py:566
  74.2 1.3 %across.1.zed_ref = f32[128,128]{1,0:T(8,128)S(1)} custom-call(s32[1]{0:T(128)} %bitcast.me_ref, s32[1024]{0:T(1024)S(1)} %bitcast.27, f32[128,128]{1,0:T(8,128)S(1)} %get-tuple-element.25.zed_ref, s32[6,128]{1,0:T(8,128)} %nbr_ref.7, s32[6,128]{1,0:T(8,128)} %wall_ref.7), custom_call_target="tpu_custom_call" | custom-call | tf_op jit(solution)/shard_map/across/pallas_call | solution.py:626
  75.5 20.1 %all-to-all-done.2 = f32[128,19,1,128]{3,2,1,0:T(1,128)S(1)} async-done(((f32[128,19,1,128]{3,2,1,0:T(1,128)}), f32[128,19,1,128]{3,2,1,0:T(1,128)S(1)}, u32[]{:S(2)}, u32[]{:S(2)}) %all-to-all-start.2) | async-done | bytes 1245216 | tf_op jit(solution)/shard_map/all_to_all | solution.py:566
  95.7 7.0 %final.1 = f32[2048,128]{1,0:T(8,128)} custom-call(s32[1]{0:T(128)} %bitcast.me_ref, f32[2432,128]{1,0:T(8,128)S(1)} %bitcast.23, s32[8,128]{1,0:T(8,128)S(1)} %get-tuple-element.23.row_ref, f32[128,128]{1,0:T(8,128)S(1)} %get-tuple-element.24.cols_ref, f32[128,128]{1,0:T(8,128)S(1)} %across.1.zed_ref, s32[384,128]{1,0:T(8,128)} %get-tuple-element.26.far_ref, ...), custom_call_target="tpu_custom_call" | custom-call | tf_op jit(solution)/shard_map/final/pallas_call | solution.py:634
Async XLA Ops:
  1.7 22.0 %all-to-all-start = ((s32[128,3,1,128]{3,2,1,0:T(1,128)}), s32[128,3,1,128]{3,2,1,0:T(1,128)S(1)}, u32[]{:S(2)}, u32[]{:S(2)}) async-start(s32[128,3,1,128]{3,2,1,0:T(1,128)} %bitcast.2), calls=%async_computation | async-start | bytes 393216 | tf_op jit(solution)/shard_map/all_to_all | solution.py:566
  13.2 0.7 copy-start
  23.7 37.6 %all-to-all-start.1 = ((f32[128,33,1,128]{3,2,1,0:T(1,128)}), f32[128,33,1,128]{3,2,1,0:T(1,128)S(1)}, u32[]{:S(2)}, u32[]{:S(2)}) async-start(f32[128,33,1,128]{3,2,1,0:T(1,128)} %bitcast.30), calls=%async_computation.1 | async-start | bytes 4325376 | tf_op jit(solution)/shard_map/all_to_all | solution.py:566
  69.8 25.9 %all-to-all-start.2 = ((f32[128,19,1,128]{3,2,1,0:T(1,128)}), f32[128,19,1,128]{3,2,1,0:T(1,128)S(1)}, u32[]{:S(2)}, u32[]{:S(2)}) async-start(f32[128,19,1,128]{3,2,1,0:T(1,128)} %bitcast.13), calls=%async_computation.2 | async-start | bytes 2490368 | tf_op jit(solution)/shard_map/all_to_all | solution.py:566

commit v4 on v3

--- a/solution.py
+++ b/solution.py
@@ -69,6 +69,15 @@
 
 
 SIDE, STACKED, COEF = derivative_tables()
+
+
+def three_parts(table):
+    high = table.astype(jnp.bfloat16)
+    low = (table - high.astype(np.float32)).astype(jnp.bfloat16)
+    return np.concatenate([high, high, low], axis=0)
+
+
+SIDE3, STACKED3 = three_parts(SIDE), three_parts(STACKED)
 
 
 def iota(shape, axis):
@@ -216,7 +225,7 @@
 
 def table_kernel(
     me_ref, info_ref, nbr_ref, wall_ref, orient_ref, bulk_ref, dens_ref,
-    spot_ref, owner_ref, row_ref, label_ref, cols_ref, far_ref, near_ref, pick_ref, wide, scr,
+    spot_ref, owner_ref, column_ref, row_ref, label_ref, cols_ref, far_ref, near_ref, pick_ref, wide, scr,
 ):
     shape = (LANES, LANES)
     sub = iota(shape, 0)
@@ -231,6 +240,7 @@
     lists = [info_ref[pl.ds(0, LANES, stride=3), :], info_ref[pl.ds(1, LANES, stride=3), :]]
     owners = info_ref[pl.ds(2, LANES, stride=3), :].astype(F32)
     owner_ref[...] = owners.T[0:8, :].astype(I32)
+    column_ref[...] = owners
     target = lists[0] >> 7
     my_k = me >> 4
     mine = jnp.where(my_k >= 4, lists[1], lists[0])
@@ -246,13 +256,19 @@
     rank = small_dot(below, present)
     safe = jnp.clip(target, 0, LANES - 1)
     slot = safe * 16 + jnp.take_along_axis(rank.astype(I32), safe, axis=1)
-    wide[...] = jnp.where(target >= 0, slot, -1)
-    quarter = iota((32, LANES), 1) >> 5
-    spots = wide[pl.ds(0, 32, stride=4), :]
+    is_source = jnp.broadcast_to(jnp.where(target[:, 0:1] >= 0, 1.0, 0.0), shape)
+    source_rank = jnp.where(is_source > 0.0, small_dot(below, is_source), -1.0)
+    chosen = jnp.where(source_rank.T == sub.astype(F32), 1.0, 0.0)
+    wide[...] = pick_dot(chosen, jnp.where(lane == 32, sub, slot).astype(F32)).astype(I32)
+    quarter = iota((16, LANES), 1) >> 5
+    spots = wide[pl.ds(0, 16, stride=4), :]
     for part in range(1, 4):
-        moved = pltpu.roll(wide[pl.ds(part, 32, stride=4), :], 32 * part, 1)
+        moved = pltpu.roll(wide[pl.ds(part, 16, stride=4), :], 32 * part, 1)
         spots = jnp.where(quarter == part, moved, spots)
-    spot_ref[...] = spots
+    spot_ref[0:16, :] = spots
+    sources = jnp.where(diag, jnp.broadcast_to(wide[:, 32:33], shape).astype(F32), 0.0)
+    sources = jnp.sum(sources, axis=0, keepdims=True).astype(I32)
+    spot_ref[16:24, :] = jnp.broadcast_to(sources, (8, LANES))
     order = jnp.where(present > 0.0, rank, -1.0)
     labels = jnp.zeros(shape, F32)
     for i in range(16):
@@ -324,18 +340,15 @@
     return (i & 3) ^ ((i >> 2) & 1) * (4 * SHIFT_A) ^ (i >> 3) * (4 * SHIFT_B)
 
 
-def forward_kernel(me_ref, spot_ref, owner_ref, in_ref, label_ref, out_ref, zed_ref, held, faces):
-    def one(source, carry):
-        base = pl.multiple_of(source * 32, 32)
-
-        @pl.when(spot_ref[base] >= 0)
-        def _():
-            for j in range(32):
-                held[pl.ds(spot_ref[base + j], 1), :] = in_ref[pl.ds(source * 33 + j, 1), :]
-
+def forward_kernel(me_ref, spot_ref, in_ref, label_ref, column_ref, out_ref, zed_ref, held, made, sem):
+    def one(number, carry):
+        base = number * 32
+        start = spot_ref[2048 + number] * 33
+        for j in range(32):
+            held[pl.ds(spot_ref[base + j], 1), :] = in_ref[pl.ds(start + j, 1), :]
         return carry
 
-    lax.fori_loop(0, DEVS, one, 0)
+    lax.fori_loop(0, DEVS // 2, one, 0, unroll=2)
     shape = (LANES, LANES)
     lane = iota(shape, 1)
     zeds = in_ref[pl.ds(32, LANES, stride=33), :]
@@ -369,6 +382,7 @@
                 value = jnp.where(hit & (spot & 3 == field), i, value)
             which.append(value)
     sign = half_sign((8, LANES))
+    waves = [[], [], []]
     for block in range(16):
         merged = [jnp.zeros((8, LANES), F32)] * 6
         for i in range(16):
@@ -380,52 +394,70 @@
         for axis in range(3):
             press = jnp.take_along_axis(merged[2 * axis], (nodes[axis] * 4) ^ shift, axis=1)
             speed = jnp.take_along_axis(merged[2 * axis + 1], (nodes[axis] * 4 + 1 + axis) ^ shift, axis=1)
-            at = axis * LANES + block * 8
-            faces[at : at + 8, :] = press + wide * speed
-        for target in range(block * 8, block * 8 + 8):
-            out_ref[target * 19 : target * 19 + 16, :] = held[target * 16 : target * 16 + 16, :]
-    low = iota((1, LANES), 1) < 64
-
-    def two(target, carry):
+            waves[axis].append(press + wide * speed)
+    low_half = iota(shape, 1) < 64
+    lane = iota(shape, 1).astype(F32)
+    halos = []
+    for axis in range(3):
+        wave = jnp.concatenate(waves[axis], axis=0)
+        upper = column_ref[:, 2 * axis + 1 : 2 * axis + 2] == lane
+        lower = column_ref[:, 2 * axis : 2 * axis + 1] == lane
+        pick = jnp.concatenate([jnp.where(upper, 1.0, 0.0), jnp.where(lower, 1.0, 0.0)], axis=1)
+        table = jnp.concatenate([jnp.where(low_half, wave, 0.0), jnp.where(low_half, 0.0, wave)], axis=0)
+        halos.append(pick_dot(pick, table))
+    copies = []
+    for part in range(4):
+        base = part * 32
+        for target in range(base, base + 32):
+            made[target * 19 : target * 19 + 16, :] = held[target * 16 : target * 16 + 16, :]
         for axis in range(3):
-            lower = jnp.maximum(owner_ref[2 * axis * LANES + target], 0)
-            upper = jnp.maximum(owner_ref[(2 * axis + 1) * LANES + target], 0)
-            row = jnp.where(
-                low, faces[pl.ds(axis * LANES + upper, 1), :], faces[pl.ds(axis * LANES + lower, 1), :]
-            )
-            out_ref[pl.ds(target * 19 + 16 + axis, 1), :] = row
-        return carry
-
-    lax.fori_loop(0, DEVS, two, 0, unroll=4)
-
-
-def across_kernel(me_ref, owner_ref, zed_ref, nbr_ref, wall_ref, out_ref):
+            made[pl.ds(base * 19 + 16 + axis, 32, stride=19), :] = halos[axis][base : base + 32, :]
+        rows = pl.ds(base * 19, 608)
+        copies.append(pltpu.make_async_copy(made.at[rows], out_ref.at[rows], sem.at[part]))
+        copies[-1].start()
+    for copy in copies:
+        copy.wait()
+
+
+def across_kernel(
+    me_ref, owner_ref, zed_ref, nbr_ref, wall_ref, row_ref, cols_ref, pick_ref, out_ref, near_ref, place_ref, far_ref
+):
     shape = (LANES, LANES)
     lane = iota(shape, 1)
     diag = iota(shape, 0) == lane
     me = me_ref[0]
     own = zed_ref[pl.ds(me, 1), :]
-    total = jnp.zeros(shape, F32)
+    cols = cols_ref[...]
+    total = jnp.where(lane == 16, cols[:, 0:1], jnp.where(lane == 17, cols[:, 1:2], cols[:, 2:3]))
     for face in range(6):
         other = zed_ref[pl.ds(jnp.maximum(owner_ref[face * LANES + me], 0), 1), :]
         nbr = nbr_ref[face : face + 1, :]
-        remote = ((nbr >> 7) != me) & (wall_ref[face : face + 1, :] == 0)
+        is_wall = wall_ref[face : face + 1, :] == 1
+        remote = ((nbr >> 7) != me) & jnp.logical_not(is_wall)
         far = column(jnp.where(remote, 1.0, 0.0), diag) > 0.0
         spot = column((nbr & 127).astype(F32), diag) == lane.astype(F32)
+        wall = column(jnp.where(is_wall, 1.0, 0.0), diag)
         value = jnp.where(spot, jnp.where(far, other, own), 0.0)
         total = jnp.where(lane == face, jnp.sum(value, axis=1, keepdims=True), total)
+        total = jnp.where(lane == 8 + face, wall, total)
+        local = jnp.where(far | (wall > 0.0), 0.0, jnp.where(spot, 1.0, 0.0))
+        rows = slice(face // 2 * LANES, face // 2 * LANES + LANES)
+        near_ref[rows, face % 2 * LANES : (face % 2 + 1) * LANES] = local.astype(BF16)
+        source = face * 16 + (lane & 15)
+        pick = jnp.take_along_axis(pick_ref[...], source, axis=1)
+        far_ref[face * LANES : (face + 1) * LANES, :] = jnp.where(lane < 48, pick, 0.0).astype(BF16)
     out_ref[...] = total
+    place_ref[...] = jnp.where(row_ref[0:1, :] == iota(shape, 0), 1.0, 0.0).astype(BF16)
 
 
 def final_kernel(
-    me_ref, in_ref, row_ref, cols_ref, zed_ref, far_ref, near_ref, pick_ref, nbr_ref, wall_ref,
-    side_ref, stack_ref, coef_ref, out_ref, state, turned,
+    in_ref, place_ref, misc_ref, hot_ref, pick_ref, far_ref, near_ref, side_ref, stack_ref, coef_ref,
+    out_ref, state, turned, lift, loose, made, sem,
 ):
     shape = (LANES, LANES)
     lane = iota(shape, 1)
-    diag = iota(shape, 0) == lane
     low_half = lane < 64
-    place = jnp.where(row_ref[0:1, :] == iota(shape, 0), 1.0, 0.0).astype(BF16)
+    place = place_ref[...]
     place = jnp.concatenate([place, place, place], axis=1)
     for group in range(0, 16, 2):
         pair = []
@@ -446,32 +478,29 @@
         start = (n4 * 4 + field) * LANES
         return state[start : start + LANES, :]
 
-    zed, bulk, dens = cols_ref[:, 0:1], cols_ref[:, 1:2], cols_ref[:, 2:3]
-    me = me_ref[0]
-    i2, j, k = lane >> 6, (lane >> 3) & 7, lane & 7
-    sign = half_sign(shape)
-    lifts = []
+    zed = misc_ref[:, 16:17]
     for axis in range(3):
         rows = slice(axis * LANES, axis * LANES + LANES)
         press, norm, wave = face_pair(chunk, axis, zed)
         turned[...] = in_ref[pl.ds(16 + axis, LANES, stride=19), :].T
-        nears, walls, fars = [], [], []
+        fars = []
         for side in range(2):
             face = 2 * axis + side
-            nbr = nbr_ref[face : face + 1, :]
-            is_wall = wall_ref[face : face + 1, :] == 1
-            local = ((nbr >> 7) == me) & jnp.logical_not(is_wall)
-            spot = column(jnp.where(local, nbr & 127, -1).astype(F32), diag)
-            nears.append(jnp.where(spot == lane.astype(F32), 1.0, 0.0))
-            walls.append(column(jnp.where(is_wall, 1.0, 0.0), diag))
             table = [turned[pl.ds((1 - side) * 64 + v, 16, stride=4), :] for v in range(4)]
-            pick = pick_ref[:, face * 16 : face * 16 + 16]
-            fars.append(pick_dot(pick, jnp.concatenate(table, axis=1)))
+            table = jnp.concatenate(split3(jnp.concatenate(table, axis=1)), axis=0)
+            pick = pick_ref[face * LANES : (face + 1) * LANES, 0:48]
+            fars.append(jnp.dot(pick, table, preferred_element_type=F32))
         masked = jnp.concatenate([jnp.where(low_half, 0.0, wave), jnp.where(low_half, wave, 0.0)], axis=0)
-        near = pick_dot(jnp.concatenate(nears, axis=1), masked)
-        own = jnp.where(low_half, walls[1], walls[0]) > 0.0
-        near = jnp.where(own, pltpu.roll(wave, 64, 1), near)
-        wave_out = jnp.take_along_axis(near, near_ref[rows, :], axis=1)
+        hot = hot_ref[rows, :]
+        near = jnp.dot(
+            jnp.concatenate([hot, hot, hot], axis=1),
+            jnp.concatenate(split3(masked), axis=0),
+            preferred_element_type=F32,
+        )
+        first, second = 2 * axis, 2 * axis + 1
+        wall = jnp.where(low_half, misc_ref[:, 8 + second : 9 + second], misc_ref[:, 8 + first : 9 + first])
+        near = jnp.where(wall > 0.0, pltpu.roll(wave, 64, 1), near)
+        total = jnp.take_along_axis(near, near_ref[rows, :], axis=1)
         code = far_ref[rows, :]
         index, part = code & 127, code >> 7
         far = jnp.zeros(shape, F32)
@@ -479,59 +508,91 @@
             below = jnp.take_along_axis(fars[0][:, v * LANES : (v + 1) * LANES], index, axis=1)
             above = jnp.take_along_axis(fars[1][:, v * LANES : (v + 1) * LANES], index, axis=1)
             far = jnp.where(part == v, jnp.where(low_half, below, above), far)
-        zed_out = jnp.where(low_half, zed_ref[:, 2 * axis : 2 * axis + 1], zed_ref[:, 2 * axis + 1 : 2 * axis + 2])
-        lifts.append((wave_out + far - press + zed_out * norm) / (zed + zed_out))
-
-    high = lax.Precision.HIGHEST
-    by_bulk = -metric_scale * bulk
-    by_dens = -(metric_scale / dens)
-    up = LIFT * bulk
-    across = -LIFT * zed / dens
-    swapped = {}
-    for field in (0, 1):
+        zed_out = jnp.where(low_half, misc_ref[:, first : first + 1], misc_ref[:, second : second + 1])
+        lift[rows, :] = (total + far - press + zed_out * norm) / (zed + zed_out)
+
+    lane = iota((32, LANES), 1)
+    low_half = lane < 64
+    i2, j, k = lane >> 6, (lane >> 3) & 7, lane & 7
+    on_y, on_z = (j == 0) | (j == 7), (k == 0) | (k == 7)
+    copies = []
+    for part in range(4):
+        rows = slice(part * 32, part * 32 + 32)
+        zed, bulk, dens = misc_ref[rows, 16:17], misc_ref[rows, 17:18], misc_ref[rows, 18:19]
+        by_bulk = -metric_scale * bulk
+        by_dens = -(metric_scale / dens)
+        up = LIFT * bulk
+        across = -LIFT * zed / dens
+        piece = {}
+        for field in range(4):
+            for n4 in range(4):
+                start = (n4 * 4 + field) * LANES + part * 32
+                piece[field, n4] = state[start : start + 32, :]
+        cut = []
+        for field in (0, 2, 3):
+            whole = jnp.concatenate([piece[field, n4] for n4 in range(4)], axis=0)
+            high = whole.astype(BF16)
+            cut.append((high, (whole - high.astype(F32)).astype(BF16)))
+        grad = jnp.dot(
+            jnp.concatenate([cut[0][0], cut[0][1], cut[0][0]], axis=1), side_ref[...], preferred_element_type=F32
+        )
+        across_div = jnp.dot(
+            jnp.concatenate([cut[1][0], cut[2][0], cut[1][1], cut[2][1], cut[1][0], cut[2][0]], axis=1),
+            stack_ref[...],
+            preferred_element_type=F32,
+        )
+        swapped = {}
+        for field in (0, 1):
+            for n4 in range(4):
+                swapped[field, n4] = pltpu.roll(piece[field, n4], 64, 1)
+        jumps = [lift[axis * LANES + part * 32 : axis * LANES + part * 32 + 32, :] for axis in range(3)]
+        base = part * 544
         for n4 in range(4):
-            swapped[field, n4] = pltpu.roll(chunk(field, n4), 64, 1)
-    for n4 in range(4):
-        along = {}
-        for field in (0, 1):
+            along = {}
+            for field in (0, 1):
+                total = None
+                for m4 in range(4):
+                    at = (n4 * 4 + m4) * 2
+                    term = piece[field, m4] * coef_ref[at : at + 1, :]
+                    term = term + swapped[field, m4] * coef_ref[at + 1 : at + 2, :]
+                    total = term if total is None else total + term
+                along[field] = total
+            block = slice(n4 * 32, n4 * 32 + 32)
+            div = along[1] + across_div[block, :]
+            grads = [along[0], grad[block, 0:LANES], grad[block, LANES:]]
+            face_i = 2 * n4 + i2
+            from_y = jnp.where(j == 7, 64, 0) + face_i * 8 + k
+            from_z = jnp.where(k == 7, 64, 0) + face_i * 8 + j
             total = None
-            for m4 in range(4):
-                at = (n4 * 4 + m4) * 2
-                term = chunk(field, m4) * coef_ref[at : at + 1, :]
-                term = term + swapped[field, m4] * coef_ref[at + 1 : at + 2, :]
-                total = term if total is None else total + term
-            along[field] = total
-        both = jnp.concatenate([chunk(2, n4), chunk(3, n4)], axis=1)
-        div = along[1] + jnp.dot(both, stack_ref[...], precision=high, preferred_element_type=F32)
-        grad = jnp.dot(chunk(0, n4), side_ref[...], precision=high, preferred_element_type=F32)
-        grads = [along[0], grad[:, 0:LANES], grad[:, LANES:]]
-        face_i = 2 * n4 + i2
-        from_y = jnp.where(j == 7, 64, 0) + face_i * 8 + k
-        from_z = jnp.where(k == 7, 64, 0) + face_i * 8 + j
-        on_y = (j == 0) | (j == 7)
-        on_z = (k == 0) | (k == 7)
-        total = jnp.zeros(shape, F32)
-        for axis in range(3):
-            jump = lifts[axis]
-            value = by_dens * grads[axis]
-            here = None
-            if axis == 0 and n4 == 0:
-                here = jnp.where(low_half, jump, 0.0)
-                turn = -here
-            elif axis == 0 and n4 == 3:
-                here = jnp.where(low_half, 0.0, jump)
-                turn = here
-            elif axis == 1:
-                here = jnp.where(on_y, jnp.take_along_axis(jump, from_y, axis=1), 0.0)
-                turn = jnp.where(j == 0, -here, here)
-            elif axis == 2:
-                here = jnp.where(on_z, jnp.take_along_axis(jump, from_z, axis=1), 0.0)
-                turn = jnp.where(k == 0, -here, here)
-            if here is not None:
-                value = value + across * turn
-                total = total + here
-            out_ref[pl.ds(n4 * 4 + 1 + axis, LANES, stride=16), :] = value
-        out_ref[pl.ds(n4 * 4, LANES, stride=16), :] = by_bulk * div + up * total
+            for axis in range(3):
+                jump = jumps[axis]
+                value = by_dens * grads[axis]
+                here = None
+                if axis == 0 and n4 == 0:
+                    here = jnp.where(low_half, jump, 0.0)
+                    turn = -here
+                elif axis == 0 and n4 == 3:
+                    here = jnp.where(low_half, 0.0, jump)
+                    turn = here
+                elif axis == 1:
+                    here = jnp.where(on_y, jnp.take_along_axis(jump, from_y, axis=1), 0.0)
+                    turn = jnp.where(j == 0, -here, here)
+                elif axis == 2:
+                    here = jnp.where(on_z, jnp.take_along_axis(jump, from_z, axis=1), 0.0)
+                    turn = jnp.where(k == 0, -here, here)
+                if here is not None:
+                    value = value + across * turn
+                    total = here if total is None else total + here
+                loose[pl.ds(base + n4 * 4 + 1 + axis, 32, stride=17), :] = value
+            loose[pl.ds(base + n4 * 4, 32, stride=17), :] = by_bulk * div + up * total
+        for row in range(32):
+            at = (part * 32 + row) * 16
+            made[at : at + 16, :] = loose[base + row * 17 : base + row * 17 + 16, :]
+        window = pl.ds(part * 512, 512)
+        copies.append(pltpu.make_async_copy(made.at[window], out_ref.at[window], sem.at[part]))
+        copies[-1].start()
+    for copy in copies:
+        copy.wait()
 
 
 def vm():
@@ -594,18 +655,19 @@
         compiler_params=GRANT,
     )(pos, dest, away(state), bulk, dens)
     spread = exchange(pieces, 33)
-    spots, owners, rows, labels, cols, far, close, pick = pl.pallas_call(
+    spots, owners, blocks, rows, labels, cols, far, close, pick = pl.pallas_call(
         table_kernel,
         in_specs=[sm()] + [vm()] * 6,
-        out_specs=[vm()] * 8,
+        out_specs=[vm()] * 9,
         out_shape=[
-            shaped((32, LANES), I32),
+            shaped((24, LANES), I32),
             shaped((8, LANES), I32),
+            shaped((LANES, LANES)),
             shaped((8, LANES), I32),
             shaped((LANES, LANES), I32),
             shaped((LANES, LANES)),
-            HBM((384, LANES), I32),
-            HBM((384, LANES), I32),
+            shaped((384, LANES), I32),
+            shaped((384, LANES), I32),
             shaped((LANES, LANES)),
         ],
         scratch_shapes=[pltpu.VMEM((LANES, LANES), I32), pltpu.VMEM((8, LANES), F32)],
@@ -615,33 +677,49 @@
     owners = owners.reshape(1024)
     passed, zeds = pl.pallas_call(
         forward_kernel,
-        in_specs=[sm()] * 3 + [vm()] * 2,
-        out_specs=[vm()] * 2,
-        out_shape=[shaped((2432, LANES)), shaped((LANES, LANES))],
-        scratch_shapes=[pltpu.VMEM((2048, LANES), F32), pltpu.VMEM((384, LANES), F32)],
+        in_specs=[sm()] * 2 + [vm()] * 3,
+        out_specs=[pl.BlockSpec(memory_space=pl.ANY), vm()],
+        out_shape=[HBM((2432, LANES), F32), shaped((LANES, LANES))],
+        scratch_shapes=[
+            pltpu.VMEM((2048, LANES), F32),
+            pltpu.VMEM((2432, LANES), F32),
+            pltpu.SemaphoreType.DMA((4,)),
+        ],
         name="forward",
         compiler_params=GRANT,
-    )(me, spots.reshape(4096), owners, near(spread), near(labels))
+    )(me, spots.reshape(3072), near(spread), near(labels), near(blocks))
     arrived = exchange(passed, 19)
-    zed_out = pl.pallas_call(
+    misc, hot, place, pick = pl.pallas_call(
         across_kernel,
-        in_specs=[sm()] * 2 + [vm()] * 3,
-        out_specs=vm(),
-        out_shape=shaped((LANES, LANES)),
+        in_specs=[sm()] * 2 + [vm()] * 6,
+        out_specs=[vm()] * 4,
+        out_shape=[
+            shaped((LANES, LANES)),
+            shaped((384, 2 * LANES), BF16),
+            shaped((LANES, LANES), BF16),
+            shaped((768, LANES), BF16),
+        ],
         name="across",
         compiler_params=GRANT,
-    )(me, owners, near(zeds), nbr, wall)
+    )(me, owners, near(zeds), nbr, wall, near(rows), near(cols), near(pick))
     result = pl.pallas_call(
         final_kernel,
-        in_specs=[sm()] + [vm()] * 12,
-        out_specs=vm(),
+        in_specs=[vm()] * 10,
+        out_specs=pl.BlockSpec(memory_space=pl.ANY),
         out_shape=plain((2048, LANES)),
-        scratch_shapes=[pltpu.VMEM((2048, LANES), F32), pltpu.VMEM((LANES, LANES), F32)],
+        scratch_shapes=[
+            pltpu.VMEM((2048, LANES), F32),
+            pltpu.VMEM((LANES, LANES), F32),
+            pltpu.VMEM((384, LANES), F32),
+            pltpu.VMEM((2176, LANES), F32),
+            pltpu.VMEM((2048, LANES), F32),
+            pltpu.SemaphoreType.DMA((4,)),
+        ],
         name="final",
         compiler_params=GRANT,
     )(
-        me, near(arrived), near(rows), near(cols), near(zed_out), away(far), away(close), near(pick), nbr, wall,
-        away(jnp.asarray(SIDE)), away(jnp.asarray(STACKED)), away(jnp.asarray(COEF)),
+        near(arrived), near(place), near(misc), near(hot), near(pick), near(far), near(close),
+        jnp.asarray(SIDE3), jnp.asarray(STACKED3), jnp.asarray(COEF),
     )
     return result.reshape(128, 4, 4, LANES).transpose(0, 2, 1, 3).reshape(128, 4, 512)
 

time: 103 us -> 98.8 us (0.959)
  Pallas kernels: 29.5 us -> 21.8 us
  waiting for transfers between devices: 50.1 us -> 53.4 us
    pallas_call x3, Pallas kernels: 16.8 us -> 13 us  [the longest x1 5.91 us: body(): pl.pallas_call(forward_kernel, in_specs=[sm()] * 2 + [vm()] * 3, out_spec...]
    pallas_call x1, Pallas kernels: 6.56 us -> 2.99 us  [body(): pl.pallas_call(pack_kernel, in_specs=[sm(), sm()] + [vm()] * 3, out_specs...]
    all_to_all x3, waiting for transfers between devices: 50.1 us -> 53.4 us  [exchange(): lax.all_to_all(blocks, AXES, split_axis=0, concat_axis=0, tiled=True)]
  transfers between devices with their start and end apart: 3 -> 3, of which waited for: 3 -> 3; matrix products, arithmetic and copies ran while one was open for 0% -> 0% of each run, Pallas kernels for 12% -> 9%
where the time goes in v4:
time: 98.8 us; the launch traced here: 98.3 us
  waiting for transfers between devices  53.4 us (54%)
  starting transfers between devices  22.2 us (22%)
  Pallas kernels  21.8 us (22%)
    all_to_all x3, waiting for transfers between devices, exchange(): lax.all_to_all(blocks, AXES, split_axis=0, concat_axis=0, tiled=True)  53.4 us
    all_to_all x3, starting transfers between devices, exchange(): lax.all_to_all(blocks, AXES, split_axis=0, concat_axis=0, tiled=True)  22.2 us
    pallas_call x1, Pallas kernels, body(): pl.pallas_call(forward_kernel, in_specs=[sm()] * 2 + [vm()] * 3, out_spec...  5.91 us
    pallas_call x1, Pallas kernels, body(): pl.pallas_call(final_kernel, in_specs=[vm()] * 10, out_specs=pl.BlockSpec...  5.17 us
    pallas_call x1, Pallas kernels, body(): pl.pallas_call(table_kernel, in_specs=[sm()] + [vm()] * 6, out_specs=[vm(...  4.13 us
    pallas_call x1, Pallas kernels, body(): pl.pallas_call(pack_kernel, in_specs=[sm(), sm()] + [vm()] * 3, out_specs...  2.99 us
  transfers between devices with their start and end apart: 3, of which 3 were waited for; matrix products, arithmetic and copies ran while one was open for 0% of the time, Pallas kernels for 9%

profile of v4, /device:TPU:1, one launch (start us, length us, event | category | flops | bytes accessed | tf_op | source)
XLA Modules:
  0.0 98.3 jit_solution(10926278527224672264)
XLA Ops:
  0.0 1.7 %order.1 = (s32[384,128]{1,0:T(8,128)}, s32[2,128]{1,0:T(2,128)S(1)}) custom-call(s32[1]{0:T(128)} %bitcast.me_ref, s32[2,128]{1,0:T(2,128)} %bitcast.26, s32[6,128]{1,0:T(8,128)} %nbr_ref.5, s32[6,128]{1,0:T(8,128)} %wall_ref.5), custom_call_target="tpu_custom_call" | custom-call | tf_op jit(solution)/shard_map/order/pallas_call | solution.py:638
  1.7 11.5 %all-to-all-start = ((s32[128,3,1,128]{3,2,1,0:T(1,128)}), s32[128,3,1,128]{3,2,1,0:T(1,128)S(1)}, u32[]{:S(2)}, u32[]{:S(2)}) async-start(s32[128,3,1,128]{3,2,1,0:T(1,128)} %bitcast.2), calls=%async_computation | async-start | bytes 393216 | tf_op jit(solution)/shard_map/all_to_all | solution.py:627
  13.2 0.0 copy-start.3
  13.2 0.7 copy-done.3
  13.8 3.0 %pack.1 = f32[4224,128]{1,0:T(8,128)} custom-call(s32[2,128]{1,0:T(2,128)S(1)} %get-tuple-element.24.pos_ref, s32[2,128]{1,0:T(2,128)S(1)} %bitcast.27, f32[4096,128]{1,0:T(8,128)} %bitcast.30, f32[1,128]{1,0:T(1,128)} %bitcast.32, f32[1,128]{1,0:T(1,128)} %bitcast.34), custom_call_target="tpu_custom_call" | custom-call | tf_op jit(solution)/shard_map/pack/pallas_call | solution.py:648
  16.8 6.8 %all-to-all-done = s32[128,3,1,128]{3,2,1,0:T(1,128)S(1)} async-done(((s32[128,3,1,128]{3,2,1,0:T(1,128)}), s32[128,3,1,128]{3,2,1,0:T(1,128)S(1)}, u32[]{:S(2)}, u32[]{:S(2)}) %all-to-all-start) | async-done | bytes 196640 | tf_op jit(solution)/shard_map/all_to_all | solution.py:627
  23.7 6.3 %all-to-all-start.1 = ((f32[128,33,1,128]{3,2,1,0:T(1,128)}), f32[128,33,1,128]{3,2,1,0:T(1,128)S(1)}, u32[]{:S(2)}, u32[]{:S(2)}) async-start(f32[128,33,1,128]{3,2,1,0:T(1,128)} %bitcast.29), calls=%async_computation.1 | async-start | bytes 4325376 | tf_op jit(solution)/shard_map/all_to_all | solution.py:627
  29.9 4.1 %table.1 = (s32[24,128]{1,0:T(8,128)S(1)}, s32[8,128]{1,0:T(8,128)S(1)}, f32[128,128]{1,0:T(8,128)S(1)}, s32[8,128]{1,0:T(8,128)S(1)}, s32[128,128]{1,0:T(8,128)...) custom-call(s32[1]{0:T(128)} %bitcast.me_ref, ...), custom_call_target="tpu_custom_call" | custom-call | tf_op jit(solution)/shard_map/table/pallas_call | solution.py:658
  34.1 27.0 %all-to-all-done.1 = f32[128,33,1,128]{3,2,1,0:T(1,128)S(1)} async-done(((f32[128,33,1,128]{3,2,1,0:T(1,128)}), f32[128,33,1,128]{3,2,1,0:T(1,128)S(1)}, u32[]{:S(2)}, u32[]{:S(2)}) %all-to-all-start.1) | async-done | bytes 2162720 | tf_op jit(solution)/shard_map/all_to_all | solution.py:627
  61.1 0.0 copy-start
  61.1 0.0 copy-start.1
  61.1 0.0 copy-start.2
  61.1 5.9 %forward.1 = (f32[2432,128]{1,0:T(8,128)}, f32[128,128]{1,0:T(8,128)S(1)}) custom-call(s32[1]{0:T(128)} %bitcast.me_ref, s32[3072]{0:T(1024)S(1)} %bitcast.25, f32[4224,128]{1,0:T(8,128)S(1)} %bitcast.22, s32[128,128]{1,0:T(8,128)S(1)} %get-tuple-element.25.label_ref, f32[128,128]{1,0:T(8,128)S(1)} %get-tuple-element.26.column_ref), custom_call_target="tpu_custom_call" | custom-call | tf_op jit(solution)/shard_map/forward/pallas_call | solution.py:678
  67.0 4.4 %all-to-all-start.2 = ((f32[128,19,1,128]{3,2,1,0:T(1,128)}), f32[128,19,1,128]{3,2,1,0:T(1,128)S(1)}, u32[]{:S(2)}, u32[]{:S(2)}) async-start(f32[128,19,1,128]{3,2,1,0:T(1,128)} %bitcast.31), calls=%async_computation.2 | async-start | bytes 2490368 | tf_op jit(solution)/shard_map/all_to_all | solution.py:627
  71.4 1.9 %across.1 = (f32[128,128]{1,0:T(8,128)S(1)}, bf16[384,256]{1,0:T(8,128)(2,1)S(1)}, bf16[128,128]{1,0:T(8,128)(2,1)S(1)}, bf16[768,128]{1,0:T(8,128)(2,1)S(1)}) custom-call(s32[1]{0:T(128)} %bitcast.me_ref, s32[1024]{0:T(1024)S(1)} %bitcast.28, f32[128,128]{1,0:T(8,128)S(1)} %get-tuple-element.29.zed_ref, s32[6,128]{1,0:T(8,128)} %nbr_ref.5, ...), custom_call_target="tpu_custom_call" | custom-call | tf_op jit(solution)/shard_map/across/pallas_call | solution.py:692
  73.3 19.6 %all-to-all-done.2 = f32[128,19,1,128]{3,2,1,0:T(1,128)S(1)} async-done(((f32[128,19,1,128]{3,2,1,0:T(1,128)}), f32[128,19,1,128]{3,2,1,0:T(1,128)S(1)}, u32[]{:S(2)}, u32[]{:S(2)}) %all-to-all-start.2) | async-done | bytes 1245216 | tf_op jit(solution)/shard_map/all_to_all | solution.py:627
  92.9 0.0 copy-done
  92.9 0.0 copy-done.1
  92.9 0.0 copy-done.2
  92.9 5.2 %final.1 = f32[2048,128]{1,0:T(8,128)} custom-call(f32[2432,128]{1,0:T(8,128)S(1)} %bitcast.23, bf16[128,128]{1,0:T(8,128)(2,1)S(1)} %get-tuple-element.33.place_ref, f32[128,128]{1,0:T(8,128)S(1)} %get-tuple-element.34.misc_ref, bf16[384,256]{1,0:T(8,128)(2,1)S(1)} %get-tuple-element.35.hot_ref, bf16[768,128]{1,0:T(8,128)(2,1)S(1)} %get-tuple-element.36.pick_ref, ...), custom_call_target="tpu_custom_call" | custom-call | tf_op jit(solution)/shard_map/final/pallas_call | solution.py:705
Async XLA Ops:
  1.7 22.0 %all-to-all-start = ((s32[128,3,1,128]{3,2,1,0:T(1,128)}), s32[128,3,1,128]{3,2,1,0:T(1,128)S(1)}, u32[]{:S(2)}, u32[]{:S(2)}) async-start(s32[128,3,1,128]{3,2,1,0:T(1,128)} %bitcast.2), calls=%async_computation | async-start | bytes 393216 | tf_op jit(solution)/shard_map/all_to_all | solution.py:627
  13.2 0.7 copy-start.3
  23.7 37.4 %all-to-all-start.1 = ((f32[128,33,1,128]{3,2,1,0:T(1,128)}), f32[128,33,1,128]{3,2,1,0:T(1,128)S(1)}, u32[]{:S(2)}, u32[]{:S(2)}) async-start(f32[128,33,1,128]{3,2,1,0:T(1,128)} %bitcast.29), calls=%async_computation.1 | async-start | bytes 4325376 | tf_op jit(solution)/shard_map/all_to_all | solution.py:627
  61.1 31.8 %copy-start = (bf16[768,128]{1,0:T(8,128)(2,1)S(1)}, bf16[768,128]{1,0:T(8,128)(2,1)}, u32[]{:S(2)}) copy-start(bf16[768,128]{1,0:T(8,128)(2,1)} %constant.18.clone.stack_ref) | copy-start | bytes 589828
  61.1 31.8 %copy-start.1 = (bf16[384,256]{1,0:T(8,128)(2,1)S(1)}, bf16[384,256]{1,0:T(8,128)(2,1)}, u32[]{:S(2)}) copy-start(bf16[384,256]{1,0:T(8,128)(2,1)} %constant.17.clone.side_ref) | copy-start | bytes 589828
  61.1 31.8 %copy-start.2 = (f32[32,128]{1,0:T(8,128)S(1)}, f32[32,128]{1,0:T(8,128)}, u32[]{:S(2)}) copy-start(f32[32,128]{1,0:T(8,128)} %constant.19.clone.coef_ref) | copy-start | bytes 49156
  67.0 25.9 %all-to-all-start.2 = ((f32[128,19,1,128]{3,2,1,0:T(1,128)}), f32[128,19,1,128]{3,2,1,0:T(1,128)S(1)}, u32[]{:S(2)}, u32[]{:S(2)}) async-start(f32[128,19,1,128]{3,2,1,0:T(1,128)} %bitcast.31), calls=%async_computation.2 | async-start | bytes 2490368 | tf_op jit(solution)/shard_map/all_to_all | solution.py:627

commit v5 on v4

--- a/solution.py
+++ b/solution.py
@@ -225,7 +225,7 @@
 
 def table_kernel(
     me_ref, info_ref, nbr_ref, wall_ref, orient_ref, bulk_ref, dens_ref,
-    spot_ref, owner_ref, column_ref, row_ref, label_ref, cols_ref, far_ref, near_ref, pick_ref, wide, scr,
+    spot_ref, owner_ref, column_ref, row_ref, label_ref, cols_ref, index_ref, hot_ref, wide, scr,
 ):
     shape = (LANES, LANES)
     sub = iota(shape, 0)
@@ -255,7 +255,7 @@
     below = jnp.where(lane < sub, 1.0, 0.0)
     rank = small_dot(below, present)
     safe = jnp.clip(target, 0, LANES - 1)
-    slot = safe * 16 + jnp.take_along_axis(rank.astype(I32), safe, axis=1)
+    slot = safe * 17 + jnp.take_along_axis(rank.astype(I32), safe, axis=1)
     is_source = jnp.broadcast_to(jnp.where(target[:, 0:1] >= 0, 1.0, 0.0), shape)
     source_rank = jnp.where(is_source > 0.0, small_dot(below, is_source), -1.0)
     chosen = jnp.where(source_rank.T == sub.astype(F32), 1.0, 0.0)
@@ -294,10 +294,9 @@
     scr[0:6, :] = jnp.where(away_all, nbr_all >> 7, -1).astype(F32)
     neighbour = jnp.max(scr[...], axis=1, keepdims=True).astype(I32)
     low_half = lane < 64
-    picks = jnp.zeros(shape, F32)
     for axis in range(3):
-        lanes = slice(axis * LANES, axis * LANES + LANES)
-        places, codes, walls = [], [], []
+        rows = slice(axis * LANES, axis * LANES + LANES)
+        codes, aways = [], []
         for side in range(2):
             face = 2 * axis + side
             nbr = nbr_ref[face : face + 1, :]
@@ -305,20 +304,15 @@
             remote = ((nbr >> 7) != me) & jnp.logical_not(is_wall)
             wanted = column(jnp.where(remote, nbr & 127, -1).astype(F32), diag)
             hit = rows_of(neighbour[face : face + 1, :]) == wanted
-            place = jnp.sum(jnp.where(hit, lane.astype(F32), 0.0), axis=1, keepdims=True).astype(I32)
-            places.append(place >> 4)
-            chosen = (lane >> 4 == face) & (lane & 15 == place & 15) & (wanted >= 0.0)
-            picks = jnp.where(chosen, 1.0, picks)
+            hot_ref[rows, side * LANES : (side + 1) * LANES] = jnp.where(hit, 1.0, 0.0).astype(BF16)
             codes.append(column(orient_ref[face : face + 1, :].astype(F32), diag).astype(I32))
-            walls.append(column(jnp.where(is_wall, 1.0, 0.0), diag))
+            aways.append(wanted)
         code = jnp.where(low_half, codes[0], codes[1])
-        code = jnp.where(jnp.where(low_half, walls[0], walls[1]) > 0.0, 0, code)
         a, b = (lane >> 3) & 7, lane & 7
         swap = code >= 4
         a1, b1 = jnp.where(swap, b, a), jnp.where(swap, a, b)
         a2 = jnp.where((code & 1) == 1, 7 - a1, a1)
         b2 = jnp.where((code & 2) == 2, 7 - b1, b1)
-        near_ref[lanes, :] = jnp.where(low_half, 64, 0) + a2 * 8 + b2
         h = jnp.where(low_half, 1, 0)
         if axis == 0:
             top = ((a2 >> 2) ^ h) * 8 + ((b2 >> 2) ^ h) * 4
@@ -329,8 +323,8 @@
         else:
             top = ((a2 >> 2) ^ (b2 >> 2)) * 8 + (((a2 >> 1) & 1) ^ h) * 4
             group, v = top + ((b2 & 3) ^ (h * 3)), (a2 & 1) * 2 + (b2 >> 2)
-        far_ref[lanes, :] = jnp.where(low_half, places[0], places[1]) * 16 + group + 128 * v
-    pick_ref[...] = picks
+        is_far = jnp.where(low_half, aways[0], aways[1]) >= 0.0
+        index_ref[rows, :] = h * 64 + jnp.where(is_far, v * 16 + group, a2 * 8 + b2)
 
 
 SHIFT_A, SHIFT_B = (3, 9)
@@ -341,14 +335,10 @@
 
 
 def forward_kernel(me_ref, spot_ref, in_ref, label_ref, column_ref, out_ref, zed_ref, held, made, sem):
-    def one(number, carry):
-        base = number * 32
+    for number in range(DEVS // 2):
         start = spot_ref[2048 + number] * 33
         for j in range(32):
-            held[pl.ds(spot_ref[base + j], 1), :] = in_ref[pl.ds(start + j, 1), :]
-        return carry
-
-    lax.fori_loop(0, DEVS // 2, one, 0, unroll=2)
+            held[pl.ds(spot_ref[number * 32 + j], 1), :] = in_ref[pl.ds(start + j, 1), :]
     shape = (LANES, LANES)
     lane = iota(shape, 1)
     zeds = in_ref[pl.ds(32, LANES, stride=33), :]
@@ -383,18 +373,24 @@
             which.append(value)
     sign = half_sign((8, LANES))
     waves = [[], [], []]
-    for block in range(16):
-        merged = [jnp.zeros((8, LANES), F32)] * 6
+    for quad in range(4):
+        blocks = range(quad * 4, quad * 4 + 4)
+        merged = [[jnp.zeros((8, LANES), F32)] * 6 for _ in blocks]
         for i in range(16):
-            rows = held[pl.ds(block * 128 + i, 8, stride=16), :]
-            rows = jnp.take_along_axis(rows, lane ^ shift_of(i), axis=1)
-            for m in range(6):
-                merged[m] = jnp.where(which[m] == i, rows, merged[m])
-        wide = jnp.take_along_axis(zed[block * 8 : block * 8 + 8, :], here, axis=1) * sign
+            hits = [which[m] == i for m in range(6)]
+            for b, block in enumerate(blocks):
+                rows = held[pl.ds(block * 136 + i, 8, stride=17), :]
+                rows = jnp.take_along_axis(rows, lane ^ shift_of(i), axis=1)
+                merged[b] = [jnp.where(hits[m], rows, merged[b][m]) for m in range(6)]
+        wide = [
+            jnp.take_along_axis(zed[block * 8 : block * 8 + 8, :], here, axis=1) * sign for block in blocks
+        ]
         for axis in range(3):
-            press = jnp.take_along_axis(merged[2 * axis], (nodes[axis] * 4) ^ shift, axis=1)
-            speed = jnp.take_along_axis(merged[2 * axis + 1], (nodes[axis] * 4 + 1 + axis) ^ shift, axis=1)
-            waves[axis].append(press + wide * speed)
+            at = (nodes[axis] * 4) ^ shift
+            press = [jnp.take_along_axis(merged[b][2 * axis], at, axis=1) for b in range(4)]
+            at = (nodes[axis] * 4 + 1 + axis) ^ shift
+            speed = [jnp.take_along_axis(merged[b][2 * axis + 1], at, axis=1) for b in range(4)]
+            waves[axis] += [press[b] + wide[b] * speed[b] for b in range(4)]
     low_half = iota(shape, 1) < 64
     lane = iota(shape, 1).astype(F32)
     halos = []
@@ -409,7 +405,7 @@
     for part in range(4):
         base = part * 32
         for target in range(base, base + 32):
-            made[target * 19 : target * 19 + 16, :] = held[target * 16 : target * 16 + 16, :]
+            made[target * 19 : target * 19 + 16, :] = held[target * 17 : target * 17 + 16, :]
         for axis in range(3):
             made[pl.ds(base * 19 + 16 + axis, 32, stride=19), :] = halos[axis][base : base + 32, :]
         rows = pl.ds(base * 19, 608)
@@ -419,39 +415,48 @@
         copy.wait()
 
 
-def across_kernel(
-    me_ref, owner_ref, zed_ref, nbr_ref, wall_ref, row_ref, cols_ref, pick_ref, out_ref, near_ref, place_ref, far_ref
-):
+def across_kernel(me_ref, owner_ref, zed_ref, nbr_ref, wall_ref, row_ref, out_ref, near_ref, place_ref):
     shape = (LANES, LANES)
     lane = iota(shape, 1)
     diag = iota(shape, 0) == lane
     me = me_ref[0]
     own = zed_ref[pl.ds(me, 1), :]
-    cols = cols_ref[...]
-    total = jnp.where(lane == 16, cols[:, 0:1], jnp.where(lane == 17, cols[:, 1:2], cols[:, 2:3]))
-    for face in range(6):
-        other = zed_ref[pl.ds(jnp.maximum(owner_ref[face * LANES + me], 0), 1), :]
-        nbr = nbr_ref[face : face + 1, :]
-        is_wall = wall_ref[face : face + 1, :] == 1
-        remote = ((nbr >> 7) != me) & jnp.logical_not(is_wall)
-        far = column(jnp.where(remote, 1.0, 0.0), diag) > 0.0
-        spot = column((nbr & 127).astype(F32), diag) == lane.astype(F32)
-        wall = column(jnp.where(is_wall, 1.0, 0.0), diag)
-        value = jnp.where(spot, jnp.where(far, other, own), 0.0)
-        total = jnp.where(lane == face, jnp.sum(value, axis=1, keepdims=True), total)
-        total = jnp.where(lane == 8 + face, wall, total)
-        local = jnp.where(far | (wall > 0.0), 0.0, jnp.where(spot, 1.0, 0.0))
-        rows = slice(face // 2 * LANES, face // 2 * LANES + LANES)
-        near_ref[rows, face % 2 * LANES : (face % 2 + 1) * LANES] = local.astype(BF16)
-        source = face * 16 + (lane & 15)
-        pick = jnp.take_along_axis(pick_ref[...], source, axis=1)
-        far_ref[face * LANES : (face + 1) * LANES, :] = jnp.where(lane < 48, pick, 0.0).astype(BF16)
-    out_ref[...] = total
+    for axis in range(3):
+        rows = slice(axis * LANES, axis * LANES + LANES)
+        zeds = []
+        for side in range(2):
+            face = 2 * axis + side
+            other = zed_ref[pl.ds(jnp.maximum(owner_ref[face * LANES + me], 0), 1), :]
+            nbr = nbr_ref[face : face + 1, :]
+            is_wall = wall_ref[face : face + 1, :] == 1
+            remote = ((nbr >> 7) != me) & jnp.logical_not(is_wall)
+            far = column(jnp.where(remote, 1.0, 0.0), diag) > 0.0
+            spot = column((nbr & 127).astype(F32), diag) == lane.astype(F32)
+            wall = column(jnp.where(is_wall, 1.0, 0.0), diag) > 0.0
+            value = jnp.where(spot, jnp.where(far, other, own), 0.0)
+            zeds.append(jnp.where(wall, -1.0, jnp.sum(value, axis=1, keepdims=True)))
+            local = jnp.where(far | wall, 0.0, jnp.where(spot, 1.0, 0.0))
+            near_ref[rows, side * LANES : (side + 1) * LANES] = local.astype(BF16)
+        out_ref[rows, :] = jnp.where(lane < 64, zeds[0], zeds[1])
     place_ref[...] = jnp.where(row_ref[0:1, :] == iota(shape, 0), 1.0, 0.0).astype(BF16)
 
 
+def exchange_lanes(arrays):
+    lane = iota(arrays[0].shape, 1)
+    bits = (lane_bit(lane, 6), lane_bit(lane, 5), lane_bit(lane, 4))
+
+    def mix(eight):
+        for step, bit in zip((1, 2, 4), bits[::-1]):
+            eight = [jnp.where(bit, eight[t ^ step], eight[t]) for t in range(8)]
+        return eight
+
+    turned = mix(arrays)
+    turned = [jnp.take_along_axis(turned[t], lane ^ (t * 16), axis=1) for t in range(8)]
+    return mix(turned)
+
+
 def final_kernel(
-    in_ref, place_ref, misc_ref, hot_ref, pick_ref, far_ref, near_ref, side_ref, stack_ref, coef_ref,
+    in_ref, place_ref, cols_ref, zed_ref, near_ref, far_ref, index_ref, side_ref, stack_ref, coef_ref,
     out_ref, state, turned, lift, loose, made, sem,
 ):
     shape = (LANES, LANES)
@@ -478,38 +483,27 @@
         start = (n4 * 4 + field) * LANES
         return state[start : start + LANES, :]
 
-    zed = misc_ref[:, 16:17]
+    zed = cols_ref[:, 0:1]
     for axis in range(3):
         rows = slice(axis * LANES, axis * LANES + LANES)
         press, norm, wave = face_pair(chunk, axis, zed)
         turned[...] = in_ref[pl.ds(16 + axis, LANES, stride=19), :].T
-        fars = []
-        for side in range(2):
-            face = 2 * axis + side
-            table = [turned[pl.ds((1 - side) * 64 + v, 16, stride=4), :] for v in range(4)]
-            table = jnp.concatenate(split3(jnp.concatenate(table, axis=1)), axis=0)
-            pick = pick_ref[face * LANES : (face + 1) * LANES, 0:48]
-            fars.append(jnp.dot(pick, table, preferred_element_type=F32))
-        masked = jnp.concatenate([jnp.where(low_half, 0.0, wave), jnp.where(low_half, wave, 0.0)], axis=0)
-        hot = hot_ref[rows, :]
-        near = jnp.dot(
-            jnp.concatenate([hot, hot, hot], axis=1),
-            jnp.concatenate(split3(masked), axis=0),
+        parts = [turned[pl.ds(h * 64 + v, 16, stride=4), :] for h in range(2) for v in range(4)]
+        far = jnp.concatenate(exchange_lanes(parts), axis=0)
+        masked = []
+        for value in (wave, far):
+            masked.append(jnp.where(low_half, 0.0, value))
+            masked.append(jnp.where(low_half, value, 0.0))
+        hot = [near_ref[rows, :], far_ref[rows, :]]
+        both = jnp.dot(
+            jnp.concatenate(hot * 3, axis=1),
+            jnp.concatenate(split3(jnp.concatenate(masked, axis=0)), axis=0),
             preferred_element_type=F32,
         )
-        first, second = 2 * axis, 2 * axis + 1
-        wall = jnp.where(low_half, misc_ref[:, 8 + second : 9 + second], misc_ref[:, 8 + first : 9 + first])
-        near = jnp.where(wall > 0.0, pltpu.roll(wave, 64, 1), near)
-        total = jnp.take_along_axis(near, near_ref[rows, :], axis=1)
-        code = far_ref[rows, :]
-        index, part = code & 127, code >> 7
-        far = jnp.zeros(shape, F32)
-        for v in range(4):
-            below = jnp.take_along_axis(fars[0][:, v * LANES : (v + 1) * LANES], index, axis=1)
-            above = jnp.take_along_axis(fars[1][:, v * LANES : (v + 1) * LANES], index, axis=1)
-            far = jnp.where(part == v, jnp.where(low_half, below, above), far)
-        zed_out = jnp.where(low_half, misc_ref[:, first : first + 1], misc_ref[:, second : second + 1])
-        lift[rows, :] = (total + far - press + zed_out * norm) / (zed + zed_out)
+        wave_out = jnp.take_along_axis(both, index_ref[rows, :], axis=1)
+        zed_out = zed_ref[rows, :]
+        jump = (wave_out - press + zed_out * norm) / (zed + zed_out)
+        lift[rows, :] = jnp.where(zed_out < 0.0, norm, jump)
 
     lane = iota((32, LANES), 1)
     low_half = lane < 64
@@ -518,7 +512,7 @@
     copies = []
     for part in range(4):
         rows = slice(part * 32, part * 32 + 32)
-        zed, bulk, dens = misc_ref[rows, 16:17], misc_ref[rows, 17:18], misc_ref[rows, 18:19]
+        zed, bulk, dens = cols_ref[rows, 0:1], cols_ref[rows, 1:2], cols_ref[rows, 2:3]
         by_bulk = -metric_scale * bulk
         by_dens = -(metric_scale / dens)
         up = LIFT * bulk
@@ -655,10 +649,10 @@
         compiler_params=GRANT,
     )(pos, dest, away(state), bulk, dens)
     spread = exchange(pieces, 33)
-    spots, owners, blocks, rows, labels, cols, far, close, pick = pl.pallas_call(
+    spots, owners, blocks, rows, labels, cols, index, far = pl.pallas_call(
         table_kernel,
         in_specs=[sm()] + [vm()] * 6,
-        out_specs=[vm()] * 9,
+        out_specs=[vm()] * 8,
         out_shape=[
             shaped((24, LANES), I32),
             shaped((8, LANES), I32),
@@ -667,8 +661,7 @@
             shaped((LANES, LANES), I32),
             shaped((LANES, LANES)),
             shaped((384, LANES), I32),
-            shaped((384, LANES), I32),
-            shaped((LANES, LANES)),
+            shaped((384, 2 * LANES), BF16),
         ],
         scratch_shapes=[pltpu.VMEM((LANES, LANES), I32), pltpu.VMEM((8, LANES), F32)],
         name="table",
@@ -681,7 +674,7 @@
         out_specs=[pl.BlockSpec(memory_space=pl.ANY), vm()],
         out_shape=[HBM((2432, LANES), F32), shaped((LANES, LANES))],
         scratch_shapes=[
-            pltpu.VMEM((2048, LANES), F32),
+            pltpu.VMEM((2176, LANES), F32),
             pltpu.VMEM((2432, LANES), F32),
             pltpu.SemaphoreType.DMA((4,)),
         ],
@@ -689,19 +682,14 @@
         compiler_params=GRANT,
     )(me, spots.reshape(3072), near(spread), near(labels), near(blocks))
     arrived = exchange(passed, 19)
-    misc, hot, place, pick = pl.pallas_call(
+    zed_out, close, place = pl.pallas_call(
         across_kernel,
-        in_specs=[sm()] * 2 + [vm()] * 6,
-        out_specs=[vm()] * 4,
-        out_shape=[
-            shaped((LANES, LANES)),
-            shaped((384, 2 * LANES), BF16),
-            shaped((LANES, LANES), BF16),
-            shaped((768, LANES), BF16),
-        ],
+        in_specs=[sm()] * 2 + [vm()] * 4,
+        out_specs=[vm()] * 3,
+        out_shape=[shaped((384, LANES)), shaped((384, 2 * LANES), BF16), shaped((LANES, LANES), BF16)],
         name="across",
         compiler_params=GRANT,
-    )(me, owners, near(zeds), nbr, wall, near(rows), near(cols), near(pick))
+    )(me, owners, near(zeds), nbr, wall, near(rows))
     result = pl.pallas_call(
         final_kernel,
         in_specs=[vm()] * 10,
@@ -718,7 +706,7 @@
         name="final",
         compiler_params=GRANT,
     )(
-        near(arrived), near(place), near(misc), near(hot), near(pick), near(far), near(close),
+        near(arrived), near(place), near(cols), near(zed_out), near(close), near(far), near(index),
         jnp.asarray(SIDE3), jnp.asarray(STACKED3), jnp.asarray(COEF),
     )
     return result.reshape(128, 4, 4, LANES).transpose(0, 2, 1, 3).reshape(128, 4, 512)

time: 98.8 us -> 95.6 us (0.968)
  waiting for transfers between devices: 53.4 us -> 51 us
    pallas_call x1, Pallas kernels: 2.99 us -> 6.57 us  [body(): pl.pallas_call(pack_kernel, in_specs=[sm(), sm()] + [vm()] * 3, out_specs...]
    all_to_all x3, waiting for transfers between devices: 53.4 us -> 51 us  [exchange(): lax.all_to_all(blocks, AXES, split_axis=0, concat_axis=0, tiled=True)]
    pallas_call x1, Pallas kernels: 5.91 us -> 4.15 us  [body(): pl.pallas_call(forward_kernel, in_specs=[sm()] * 2 + [vm()] * 3, out_spec...]
    pallas_call x1, Pallas kernels: 5.17 us -> 4.02 us  [body(): pl.pallas_call(final_kernel, in_specs=[vm()] * 10, out_specs=pl.BlockSpec...]
  transfers between devices with their start and end apart: 3 -> 3, of which waited for: 3 -> 3; matrix products, arithmetic and copies ran while one was open for 0% -> 0% of each run, Pallas kernels for 9% -> 12%
where the time goes in v5:
time: 95.6 us; the launch traced here: 95.2 us
  waiting for transfers between devices  51 us (53%)
  starting transfers between devices  22.2 us (23%)
  Pallas kernels  21.3 us (22%)
    all_to_all x3, waiting for transfers between devices, exchange(): lax.all_to_all(blocks, AXES, split_axis=0, concat_axis=0, tiled=True)  51 us
    all_to_all x3, starting transfers between devices, exchange(): lax.all_to_all(blocks, AXES, split_axis=0, concat_axis=0, tiled=True)  22.2 us
    pallas_call x1, Pallas kernels, body(): pl.pallas_call(pack_kernel, in_specs=[sm(), sm()] + [vm()] * 3, out_specs...  6.57 us
    pallas_call x1, Pallas kernels, body(): pl.pallas_call(forward_kernel, in_specs=[sm()] * 2 + [vm()] * 3, out_spec...  4.15 us
    pallas_call x1, Pallas kernels, body(): pl.pallas_call(final_kernel, in_specs=[vm()] * 10, out_specs=pl.BlockSpec...  4.02 us
    pallas_call x1, Pallas kernels, body(): pl.pallas_call(table_kernel, in_specs=[sm()] + [vm()] * 6, out_specs=[vm(...  3.45 us
  transfers between devices with their start and end apart: 3, of which 3 were waited for; matrix products, arithmetic and copies ran while one was open for 0% of the time, Pallas kernels for 12%

profile of v5, /device:TPU:1, one launch (start us, length us, event | category | flops | bytes accessed | tf_op | source)
XLA Modules:
  0.0 95.2 jit_solution(8158641585920309177)
XLA Ops:
  0.0 1.7 %order.1 = (s32[384,128]{1,0:T(8,128)}, s32[2,128]{1,0:T(2,128)S(1)}) custom-call(s32[1]{0:T(128)} %bitcast.me_ref, s32[2,128]{1,0:T(2,128)} %bitcast.26, s32[6,128]{1,0:T(8,128)} %nbr_ref.5, s32[6,128]{1,0:T(8,128)} %wall_ref.5), custom_call_target="tpu_custom_call" | custom-call | tf_op jit(solution)/shard_map/order/pallas_call | solution.py:632
  1.7 11.5 %all-to-all-start = ((s32[128,3,1,128]{3,2,1,0:T(1,128)}), s32[128,3,1,128]{3,2,1,0:T(1,128)S(1)}, u32[]{:S(2)}, u32[]{:S(2)}) async-start(s32[128,3,1,128]{3,2,1,0:T(1,128)} %bitcast.2), calls=%async_computation | async-start | bytes 393216 | tf_op jit(solution)/shard_map/all_to_all | solution.py:621
  13.2 0.0 copy-start.3
  13.2 0.7 copy-done.3
  13.8 6.6 %pack.1 = f32[4224,128]{1,0:T(8,128)} custom-call(s32[2,128]{1,0:T(2,128)S(1)} %get-tuple-element.22.pos_ref, s32[2,128]{1,0:T(2,128)S(1)} %bitcast.27, f32[4096,128]{1,0:T(8,128)} %bitcast.30, f32[1,128]{1,0:T(1,128)} %bitcast.32, f32[1,128]{1,0:T(1,128)} %bitcast.34), custom_call_target="tpu_custom_call" | custom-call | tf_op jit(solution)/shard_map/pack/pallas_call | solution.py:642
  20.4 3.3 %all-to-all-done = s32[128,3,1,128]{3,2,1,0:T(1,128)S(1)} async-done(((s32[128,3,1,128]{3,2,1,0:T(1,128)}), s32[128,3,1,128]{3,2,1,0:T(1,128)S(1)}, u32[]{:S(2)}, u32[]{:S(2)}) %all-to-all-start) | async-done | bytes 196640 | tf_op jit(solution)/shard_map/all_to_all | solution.py:621
  23.7 6.3 %all-to-all-start.1 = ((f32[128,33,1,128]{3,2,1,0:T(1,128)}), f32[128,33,1,128]{3,2,1,0:T(1,128)S(1)}, u32[]{:S(2)}, u32[]{:S(2)}) async-start(f32[128,33,1,128]{3,2,1,0:T(1,128)} %bitcast.29), calls=%async_computation.1 | async-start | bytes 4325376 | tf_op jit(solution)/shard_map/all_to_all | solution.py:621
  30.0 3.5 %table.1 = (s32[24,128]{1,0:T(8,128)S(1)}, s32[8,128]{1,0:T(8,128)S(1)}, f32[128,128]{1,0:T(8,128)S(1)}, s32[8,128]{1,0:T(8,128)S(1)}, s32[128,128]{1,0:T(8,128)...) custom-call(s32[1]{0:T(128)} %bitcast.me_ref, s32[384,128]{1,0:T(8,128)S(1)} %bitcast.24, ...), custom_call_target="tpu_custom_call" | custom-call | tf_op jit(solution)/shard_map/table/pallas_call | solution.py:652
  33.4 27.7 %all-to-all-done.1 = f32[128,33,1,128]{3,2,1,0:T(1,128)S(1)} async-done(((f32[128,33,1,128]{3,2,1,0:T(1,128)}), f32[128,33,1,128]{3,2,1,0:T(1,128)S(1)}, u32[]{:S(2)}, u32[]{:S(2)}) %all-to-all-start.1) | async-done | bytes 2162720 | tf_op jit(solution)/shard_map/all_to_all | solution.py:621
  61.1 0.0 copy-start
  61.1 0.0 copy-start.1
  61.1 0.0 copy-start.2
  61.1 4.1 %forward.1 = (f32[2432,128]{1,0:T(8,128)}, f32[128,128]{1,0:T(8,128)S(1)}) custom-call(s32[1]{0:T(128)} %bitcast.me_ref, s32[3072]{0:T(1024)S(1)} %bitcast.25, f32[4224,128]{1,0:T(8,128)S(1)} %bitcast.22, s32[128,128]{1,0:T(8,128)S(1)} %get-tuple-element.23.label_ref, f32[128,128]{1,0:T(8,128)S(1)} %get-tuple-element.24.column_ref), custom_call_target="tpu_custom_call" | custom-call | tf_op jit(solution)/shard_map/forward/pallas_call | solution.py:671
  65.3 4.4 %all-to-all-start.2 = ((f32[128,19,1,128]{3,2,1,0:T(1,128)}), f32[128,19,1,128]{3,2,1,0:T(1,128)S(1)}, u32[]{:S(2)}, u32[]{:S(2)}) async-start(f32[128,19,1,128]{3,2,1,0:T(1,128)} %bitcast.31), calls=%async_computation.2 | async-start | bytes 2490368 | tf_op jit(solution)/shard_map/all_to_all | solution.py:621
  69.7 1.4 %across.1 = (f32[384,128]{1,0:T(8,128)S(1)}, bf16[384,256]{1,0:T(8,128)(2,1)S(1)}, bf16[128,128]{1,0:T(8,128)(2,1)S(1)}) custom-call(s32[1]{0:T(128)} %bitcast.me_ref, s32[1024]{0:T(1024)S(1)} %bitcast.28, f32[128,128]{1,0:T(8,128)S(1)} %get-tuple-element.27.zed_ref, s32[6,128]{1,0:T(8,128)} %nbr_ref.5, s32[6,128]{1,0:T(8,128)} %wall_ref.5, ...), custom_call_target="tpu_custom_call" | custom-call | tf_op jit(solution)/shard_map/across/pallas_call | solution.py:685
  71.2 20.0 %all-to-all-done.2 = f32[128,19,1,128]{3,2,1,0:T(1,128)S(1)} async-done(((f32[128,19,1,128]{3,2,1,0:T(1,128)}), f32[128,19,1,128]{3,2,1,0:T(1,128)S(1)}, u32[]{:S(2)}, u32[]{:S(2)}) %all-to-all-start.2) | async-done | bytes 1245216 | tf_op jit(solution)/shard_map/all_to_all | solution.py:621
  91.2 0.0 copy-done
  91.2 0.0 copy-done.1
  91.2 0.0 copy-done.2
  91.2 4.0 %final.1 = f32[2048,128]{1,0:T(8,128)} custom-call(f32[2432,128]{1,0:T(8,128)S(1)} %bitcast.23, bf16[128,128]{1,0:T(8,128)(2,1)S(1)} %get-tuple-element.29.place_ref, f32[128,128]{1,0:T(8,128)S(1)} %get-tuple-element.30.cols_ref, f32[384,128]{1,0:T(8,128)S(1)} %get-tuple-element.31.zed_ref, bf16[384,256]{1,0:T(8,128)(2,1)S(1)} %get-tuple-element.32.near_ref, ...), custom_call_target="tpu_custom_call" | custom-call | tf_op jit(solution)/shard_map/final/pallas_call | solution.py:693
Async XLA Ops:
  1.7 22.0 %all-to-all-start = ((s32[128,3,1,128]{3,2,1,0:T(1,128)}), s32[128,3,1,128]{3,2,1,0:T(1,128)S(1)}, u32[]{:S(2)}, u32[]{:S(2)}) async-start(s32[128,3,1,128]{3,2,1,0:T(1,128)} %bitcast.2), calls=%async_computation | async-start | bytes 393216 | tf_op jit(solution)/shard_map/all_to_all | solution.py:621
  13.2 0.7 copy-start.3
  23.7 37.5 %all-to-all-start.1 = ((f32[128,33,1,128]{3,2,1,0:T(1,128)}), f32[128,33,1,128]{3,2,1,0:T(1,128)S(1)}, u32[]{:S(2)}, u32[]{:S(2)}) async-start(f32[128,33,1,128]{3,2,1,0:T(1,128)} %bitcast.29), calls=%async_computation.1 | async-start | bytes 4325376 | tf_op jit(solution)/shard_map/all_to_all | solution.py:621
  61.1 30.1 %copy-start = (bf16[768,128]{1,0:T(8,128)(2,1)S(1)}, bf16[768,128]{1,0:T(8,128)(2,1)}, u32[]{:S(2)}) copy-start(bf16[768,128]{1,0:T(8,128)(2,1)} %constant.18.clone.stack_ref) | copy-start | bytes 589828
  61.1 30.1 %copy-start.1 = (bf16[384,256]{1,0:T(8,128)(2,1)S(1)}, bf16[384,256]{1,0:T(8,128)(2,1)}, u32[]{:S(2)}) copy-start(bf16[384,256]{1,0:T(8,128)(2,1)} %constant.17.clone.side_ref) | copy-start | bytes 589828
  61.1 30.1 %copy-start.2 = (f32[32,128]{1,0:T(8,128)S(1)}, f32[32,128]{1,0:T(8,128)}, u32[]{:S(2)}) copy-start(f32[32,128]{1,0:T(8,128)} %constant.19.clone.coef_ref) | copy-start | bytes 49156
  65.3 25.9 %all-to-all-start.2 = ((f32[128,19,1,128]{3,2,1,0:T(1,128)}), f32[128,19,1,128]{3,2,1,0:T(1,128)S(1)}, u32[]{:S(2)}, u32[]{:S(2)}) async-start(f32[128,19,1,128]{3,2,1,0:T(1,128)} %bitcast.31), calls=%async_computation.2 | async-start | bytes 2490368 | tf_op jit(solution)/shard_map/all_to_all | solution.py:621

commit v6 on v5

--- a/solution.py
+++ b/solution.py
@@ -183,7 +183,7 @@
             before_row = before_row + jnp.sum(
                 jnp.where(key_col[other] < key_row[half], 1.0, 0.0), axis=0, keepdims=True
             )
-        pos_ref[half : half + 1, :] = before_row.astype(I32)
+        pos_ref[half : half + 1, :] = jnp.where(dest[half : half + 1, :] >= 0, before_row.astype(I32), -1)
         place = before_col.astype(I32)
         k = place & 7
         spot = (k & 3) * 32 + (place >> 3)
@@ -201,26 +201,51 @@
         info_ref[pl.ds(part, LANES, stride=3), :] = jnp.broadcast_to(row, (LANES, LANES)).astype(I32)
 
 
-def pack_kernel(pos_ref, dest_ref, state_ref, bulk_ref, dens_ref, out_ref, scr):
+def pack_kernel(pos_ref, state_ref, bulk_ref, dens_ref, out_ref, rows, made, in_sem, out_sem):
+    full = pos_ref[0, 0] >= 0
+    loads = []
+    for part in range(4):
+        window = pl.ds(part * 1024, 1024)
+        loads.append(pltpu.make_async_copy(state_ref.at[window], rows.at[window], in_sem.at[part]))
+
+    @pl.when(full)
+    def _():
+        for load in loads:
+            load.start()
+
     zed = jnp.sqrt(bulk_ref[...] * dens_ref[...])
-    out_ref[pl.ds(32, LANES, stride=33), :] = jnp.broadcast_to(zed, (LANES, LANES))
-
-    @pl.when(dest_ref[0, 0] >= 0)
+    made[pl.ds(32, LANES, stride=33), :] = jnp.broadcast_to(zed, (LANES, LANES))
+
+    @pl.when(full)
     def _():
-        def one(slot, carry):
-            place = pos_ref[slot >> 7, slot & 127]
-            start = (place & 7) * 512 + (place >> 3)
-            scr[pl.ds(start, 16, stride=32), :] = state_ref[pl.ds(pl.multiple_of(slot * 16, 16), 16), :]
-            return carry
-
-        lax.fori_loop(0, 256, one, 0, unroll=8)
-        for k in range(8):
+        for part in range(4):
+            loads[part].wait()
+
+            def one(step, carry):
+                slot = part * 64 + step
+                place = pos_ref[slot >> 7, slot & 127]
+                start = (place & 7) * 528 + (place >> 3)
+                made[pl.ds(start, 16, stride=33), :] = rows[pl.ds(pl.multiple_of(slot * 16, 16), 16), :]
+                return carry
+
+            lax.fori_loop(0, 64, one, 0, unroll=8)
+
+    stores = []
+    for k in range(8):
+
+        @pl.when(full)
+        def _():
             for block in range(4):
-                at = [(k * 16 + c) * 32 + block * 8 for c in range(16)]
-                groups = regroup([scr[a : a + 8, :] for a in at], False)
+                at = [(k * 16 + c) * 33 + block * 8 for c in range(16)]
+                groups = regroup([made[a : a + 8, :] for a in at], False)
                 for g in range(16):
-                    row = (k * 16 + g) * 33 + block * 8
-                    out_ref[row : row + 8, :] = groups[g]
+                    made[at[g] : at[g] + 8, :] = groups[g]
+
+        window = pl.ds(k * 528, 528)
+        stores.append(pltpu.make_async_copy(made.at[window], out_ref.at[window], out_sem.at[k]))
+        stores[-1].start()
+    for store in stores:
+        store.wait()
 
 
 def table_kernel(
@@ -641,13 +666,18 @@
     heard = exchange(info, 3)
     pieces = pl.pallas_call(
         pack_kernel,
-        in_specs=[sm(), sm()] + [vm()] * 3,
-        out_specs=vm(),
+        in_specs=[sm(), pl.BlockSpec(memory_space=pl.ANY), vm(), vm()],
+        out_specs=pl.BlockSpec(memory_space=pl.ANY),
         out_shape=HBM((4224, LANES), F32),
-        scratch_shapes=[pltpu.VMEM((4096, LANES), F32)],
+        scratch_shapes=[
+            pltpu.VMEM((4096, LANES), F32),
+            pltpu.VMEM((4224, LANES), F32),
+            pltpu.SemaphoreType.DMA((4,)),
+            pltpu.SemaphoreType.DMA((8,)),
+        ],
         name="pack",
         compiler_params=GRANT,
-    )(pos, dest, away(state), bulk, dens)
+    )(pos, away(state), bulk, dens)
     spread = exchange(pieces, 33)
     spots, owners, blocks, rows, labels, cols, index, far = pl.pallas_call(
         table_kernel,

time: 95.6 us -> 94.2 us (0.985)
  waiting for transfers between devices: 51 us -> 56.1 us
  Pallas kernels: 21.3 us -> 16.9 us
  starting transfers between devices: 22.2 us -> 20.6 us
    all_to_all x3, waiting for transfers between devices: 51 us -> 56.1 us  [exchange(): lax.all_to_all(blocks, AXES, split_axis=0, concat_axis=0, tiled=True)]
    pallas_call x1, Pallas kernels: 6.57 us -> 2.15 us  [body(): pl.pallas_call(pack_kernel, in_specs=[sm(), pl.BlockSpec(memory_space=pl....]
    all_to_all x3, starting transfers between devices: 22.2 us -> 20.6 us  [exchange(): lax.all_to_all(blocks, AXES, split_axis=0, concat_axis=0, tiled=True)]
  transfers between devices with their start and end apart: 3 -> 3, of which waited for: 3 -> 3; matrix products, arithmetic and copies ran while one was open for 0% -> 0% of each run, Pallas kernels for 12% -> 8%
where the time goes in v6:
time: 94.2 us; the launch traced here: 93.6 us
  waiting for transfers between devices  56.1 us (60%)
  starting transfers between devices  20.6 us (22%)
  Pallas kernels  16.9 us (18%)
    all_to_all x3, waiting for transfers between devices, exchange(): lax.all_to_all(blocks, AXES, split_axis=0, concat_axis=0, tiled=True)  56.1 us
    all_to_all x3, starting transfers between devices, exchange(): lax.all_to_all(blocks, AXES, split_axis=0, concat_axis=0, tiled=True)  20.6 us
    pallas_call x1, Pallas kernels, body(): pl.pallas_call(forward_kernel, in_specs=[sm()] * 2 + [vm()] * 3, out_spec...  4.14 us
    pallas_call x1, Pallas kernels, body(): pl.pallas_call(final_kernel, in_specs=[vm()] * 10, out_specs=pl.BlockSpec...  4.03 us
    pallas_call x1, Pallas kernels, body(): pl.pallas_call(table_kernel, in_specs=[sm()] + [vm()] * 6, out_specs=[vm(...  3.45 us
    pallas_call x1, Pallas kernels, body(): pl.pallas_call(pack_kernel, in_specs=[sm(), pl.BlockSpec(memory_space=pl....  2.15 us
  transfers between devices with their start and end apart: 3, of which 3 were waited for; matrix products, arithmetic and copies ran while one was open for 0% of the time, Pallas kernels for 8%

profile of v6, /device:TPU:1, one launch (start us, length us, event | category | flops | bytes accessed | tf_op | source)
XLA Modules:
  0.0 93.6 jit_solution(8603429498354280666)
XLA Ops:
  0.0 1.7 %order.1 = (s32[384,128]{1,0:T(8,128)}, s32[2,128]{1,0:T(2,128)S(1)}) custom-call(s32[1]{0:T(128)} %bitcast.me_ref, s32[2,128]{1,0:T(2,128)} %bitcast.34, s32[6,128]{1,0:T(8,128)} %nbr_ref.5, s32[6,128]{1,0:T(8,128)} %wall_ref.5), custom_call_target="tpu_custom_call" | custom-call | tf_op jit(solution)/shard_map/order/pallas_call | solution.py:657
  1.7 11.5 %all-to-all-start = ((s32[128,3,1,128]{3,2,1,0:T(1,128)}), s32[128,3,1,128]{3,2,1,0:T(1,128)S(1)}, u32[]{:S(2)}, u32[]{:S(2)}) async-start(s32[128,3,1,128]{3,2,1,0:T(1,128)} %bitcast.2), calls=%async_computation | async-start | bytes 393216 | tf_op jit(solution)/shard_map/all_to_all | solution.py:646
  13.2 2.2 %pack.1 = f32[4224,128]{1,0:T(8,128)} custom-call(s32[2,128]{1,0:T(2,128)S(1)} %get-tuple-element.22.pos_ref, f32[4096,128]{1,0:T(8,128)} %bitcast.28, f32[1,128]{1,0:T(1,128)} %bitcast.30, f32[1,128]{1,0:T(1,128)} %bitcast.32), custom_call_target="tpu_custom_call" | custom-call | tf_op jit(solution)/shard_map/pack/pallas_call | solution.py:667
  15.3 8.3 %all-to-all-done = s32[128,3,1,128]{3,2,1,0:T(1,128)S(1)} async-done(((s32[128,3,1,128]{3,2,1,0:T(1,128)}), s32[128,3,1,128]{3,2,1,0:T(1,128)S(1)}, u32[]{:S(2)}, u32[]{:S(2)}) %all-to-all-start) | async-done | bytes 196640 | tf_op jit(solution)/shard_map/all_to_all | solution.py:646
  23.7 4.7 %all-to-all-start.1 = ((f32[128,33,1,128]{3,2,1,0:T(1,128)}), f32[128,33,1,128]{3,2,1,0:T(1,128)S(1)}, u32[]{:S(2)}, u32[]{:S(2)}) async-start(f32[128,33,1,128]{3,2,1,0:T(1,128)} %bitcast.27), calls=%async_computation.1 | async-start | bytes 4325376 | tf_op jit(solution)/shard_map/all_to_all | solution.py:646
  28.4 3.5 %table.1 = (s32[24,128]{1,0:T(8,128)S(1)}, s32[8,128]{1,0:T(8,128)S(1)}, f32[128,128]{1,0:T(8,128)S(1)}, s32[8,128]{1,0:T(8,128)S(1)}, s32[128,128]{1,0:T(8,128)...) custom-call(s32[1]{0:T(128)} %bitcast.me_ref, s32[384,128]{1,0:T(8,128)S(1)} %bitcast.24, ...), custom_call_target="tpu_custom_call" | custom-call | tf_op jit(solution)/shard_map/table/pallas_call | solution.py:682
  31.9 27.7 %all-to-all-done.1 = f32[128,33,1,128]{3,2,1,0:T(1,128)S(1)} async-done(((f32[128,33,1,128]{3,2,1,0:T(1,128)}), f32[128,33,1,128]{3,2,1,0:T(1,128)S(1)}, u32[]{:S(2)}, u32[]{:S(2)}) %all-to-all-start.1) | async-done | bytes 2162720 | tf_op jit(solution)/shard_map/all_to_all | solution.py:646
  59.6 0.0 copy-start
  59.6 0.0 copy-start.1
  59.6 0.0 copy-start.2
  59.6 4.1 %forward.1 = (f32[2432,128]{1,0:T(8,128)}, f32[128,128]{1,0:T(8,128)S(1)}) custom-call(s32[1]{0:T(128)} %bitcast.me_ref, s32[3072]{0:T(1024)S(1)} %bitcast.25, f32[4224,128]{1,0:T(8,128)S(1)} %bitcast.22, s32[128,128]{1,0:T(8,128)S(1)} %get-tuple-element.23.label_ref, f32[128,128]{1,0:T(8,128)S(1)} %get-tuple-element.24.column_ref), custom_call_target="tpu_custom_call" | custom-call | tf_op jit(solution)/shard_map/forward/pallas_call | solution.py:701
  63.7 4.4 %all-to-all-start.2 = ((f32[128,19,1,128]{3,2,1,0:T(1,128)}), f32[128,19,1,128]{3,2,1,0:T(1,128)S(1)}, u32[]{:S(2)}, u32[]{:S(2)}) async-start(f32[128,19,1,128]{3,2,1,0:T(1,128)} %bitcast.29), calls=%async_computation.2 | async-start | bytes 2490368 | tf_op jit(solution)/shard_map/all_to_all | solution.py:646
  68.1 1.4 %across.1 = (f32[384,128]{1,0:T(8,128)S(1)}, bf16[384,256]{1,0:T(8,128)(2,1)S(1)}, bf16[128,128]{1,0:T(8,128)(2,1)S(1)}) custom-call(s32[1]{0:T(128)} %bitcast.me_ref, s32[1024]{0:T(1024)S(1)} %bitcast.26, f32[128,128]{1,0:T(8,128)S(1)} %get-tuple-element.27.zed_ref, s32[6,128]{1,0:T(8,128)} %nbr_ref.5, s32[6,128]{1,0:T(8,128)} %wall_ref.5, ...), custom_call_target="tpu_custom_call" | custom-call | tf_op jit(solution)/shard_map/across/pallas_call | solution.py:715
  69.6 20.0 %all-to-all-done.2 = f32[128,19,1,128]{3,2,1,0:T(1,128)S(1)} async-done(((f32[128,19,1,128]{3,2,1,0:T(1,128)}), f32[128,19,1,128]{3,2,1,0:T(1,128)S(1)}, u32[]{:S(2)}, u32[]{:S(2)}) %all-to-all-start.2) | async-done | bytes 1245216 | tf_op jit(solution)/shard_map/all_to_all | solution.py:646
  89.6 0.0 copy-done
  89.6 0.0 copy-done.1
  89.6 0.0 copy-done.2
  89.6 4.0 %final.1 = f32[2048,128]{1,0:T(8,128)} custom-call(f32[2432,128]{1,0:T(8,128)S(1)} %bitcast.23, bf16[128,128]{1,0:T(8,128)(2,1)S(1)} %get-tuple-element.29.place_ref, f32[128,128]{1,0:T(8,128)S(1)} %get-tuple-element.30.cols_ref, f32[384,128]{1,0:T(8,128)S(1)} %get-tuple-element.31.zed_ref, bf16[384,256]{1,0:T(8,128)(2,1)S(1)} %get-tuple-element.32.near_ref, ...), custom_call_target="tpu_custom_call" | custom-call | tf_op jit(solution)/shard_map/final/pallas_call | solution.py:723
Async XLA Ops:
  1.7 22.0 %all-to-all-start = ((s32[128,3,1,128]{3,2,1,0:T(1,128)}), s32[128,3,1,128]{3,2,1,0:T(1,128)S(1)}, u32[]{:S(2)}, u32[]{:S(2)}) async-start(s32[128,3,1,128]{3,2,1,0:T(1,128)} %bitcast.2), calls=%async_computation | async-start | bytes 393216 | tf_op jit(solution)/shard_map/all_to_all | solution.py:646
  23.7 35.9 %all-to-all-start.1 = ((f32[128,33,1,128]{3,2,1,0:T(1,128)}), f32[128,33,1,128]{3,2,1,0:T(1,128)S(1)}, u32[]{:S(2)}, u32[]{:S(2)}) async-start(f32[128,33,1,128]{3,2,1,0:T(1,128)} %bitcast.27), calls=%async_computation.1 | async-start | bytes 4325376 | tf_op jit(solution)/shard_map/all_to_all | solution.py:646
  59.6 30.0 %copy-start = (bf16[768,128]{1,0:T(8,128)(2,1)S(1)}, bf16[768,128]{1,0:T(8,128)(2,1)}, u32[]{:S(2)}) copy-start(bf16[768,128]{1,0:T(8,128)(2,1)} %constant.18.clone.stack_ref) | copy-start | bytes 589828
  59.6 30.0 %copy-start.1 = (bf16[384,256]{1,0:T(8,128)(2,1)S(1)}, bf16[384,256]{1,0:T(8,128)(2,1)}, u32[]{:S(2)}) copy-start(bf16[384,256]{1,0:T(8,128)(2,1)} %constant.17.clone.side_ref) | copy-start | bytes 589828
  59.6 30.0 %copy-start.2 = (f32[32,128]{1,0:T(8,128)S(1)}, f32[32,128]{1,0:T(8,128)}, u32[]{:S(2)}) copy-start(f32[32,128]{1,0:T(8,128)} %constant.19.clone.coef_ref) | copy-start | bytes 49156
  63.7 25.9 %all-to-all-start.2 = ((f32[128,19,1,128]{3,2,1,0:T(1,128)}), f32[128,19,1,128]{3,2,1,0:T(1,128)S(1)}, u32[]{:S(2)}, u32[]{:S(2)}) async-start(f32[128,19,1,128]{3,2,1,0:T(1,128)} %bitcast.29), calls=%async_computation.2 | async-start | bytes 2490368 | tf_op jit(solution)/shard_map/all_to_all | solution.py:646

commit v7 on v6

--- a/solution.py
+++ b/solution.py
@@ -160,7 +160,10 @@
     return final
 
 
-def order_kernel(me_ref, dest_ref, nbr_ref, wall_ref, info_ref, pos_ref, scr):
+def order_kernel(
+    me_ref, dest_ref, nbr_ref, wall_ref, bulk_ref, dens_ref, info_ref, pos_ref, zed_ref, scr
+):
+    zed_ref[...] = jnp.broadcast_to(jnp.sqrt(bulk_ref[...] * dens_ref[...]), (8, LANES))
     dest = dest_ref[...]
     sub = iota((LANES, LANES), 0)
     lane = iota((LANES, LANES), 1)
@@ -183,7 +186,9 @@
             before_row = before_row + jnp.sum(
                 jnp.where(key_col[other] < key_row[half], 1.0, 0.0), axis=0, keepdims=True
             )
-        pos_ref[half : half + 1, :] = jnp.where(dest[half : half + 1, :] >= 0, before_row.astype(I32), -1)
+        spot = before_row.astype(I32)
+        spot = (spot & 7) * 528 + (spot >> 3)
+        pos_ref[half : half + 1, :] = jnp.where(dest[half : half + 1, :] >= 0, spot, -1)
         place = before_col.astype(I32)
         k = place & 7
         spot = (k & 3) * 32 + (place >> 3)
@@ -201,8 +206,8 @@
         info_ref[pl.ds(part, LANES, stride=3), :] = jnp.broadcast_to(row, (LANES, LANES)).astype(I32)
 
 
-def pack_kernel(pos_ref, state_ref, bulk_ref, dens_ref, out_ref, rows, made, in_sem, out_sem):
-    full = pos_ref[0, 0] >= 0
+def pack_kernel(pos_ref, state_ref, zed_ref, out_ref, rows, made, in_sem, out_sem):
+    full = pos_ref[0] >= 0
     loads = []
     for part in range(4):
         window = pl.ds(part * 1024, 1024)
@@ -213,22 +218,17 @@
         for load in loads:
             load.start()
 
-    zed = jnp.sqrt(bulk_ref[...] * dens_ref[...])
-    made[pl.ds(32, LANES, stride=33), :] = jnp.broadcast_to(zed, (LANES, LANES))
+    made[pl.ds(32, LANES, stride=33), :] = jnp.broadcast_to(zed_ref[0:1, :], (LANES, LANES))
 
     @pl.when(full)
     def _():
+        def one(slot, carry):
+            made[pl.ds(pos_ref[slot], 16, stride=33), :] = rows[pl.ds(pl.multiple_of(slot * 16, 16), 16), :]
+            return carry
+
         for part in range(4):
             loads[part].wait()
-
-            def one(step, carry):
-                slot = part * 64 + step
-                place = pos_ref[slot >> 7, slot & 127]
-                start = (place & 7) * 528 + (place >> 3)
-                made[pl.ds(start, 16, stride=33), :] = rows[pl.ds(pl.multiple_of(slot * 16, 16), 16), :]
-                return carry
-
-            lax.fori_loop(0, 64, one, 0, unroll=8)
+            lax.fori_loop(part * 64, part * 64 + 64, one, 0, unroll=16)
 
     stores = []
     for k in range(8):
@@ -250,7 +250,7 @@
 
 def table_kernel(
     me_ref, info_ref, nbr_ref, wall_ref, orient_ref, bulk_ref, dens_ref,
-    spot_ref, owner_ref, column_ref, row_ref, label_ref, cols_ref, index_ref, hot_ref, wide, scr,
+    spot_ref, owner_ref, column_ref, label_ref, cols_ref, index_ref, hot_ref, near_ref, place_ref, wide, scr,
 ):
     shape = (LANES, LANES)
     sub = iota(shape, 0)
@@ -260,7 +260,7 @@
     bulk = column(bulk_ref[...], diag)
     dens = column(dens_ref[...], diag)
     zed = column(jnp.sqrt(bulk_ref[...] * dens_ref[...]), diag)
-    cols_ref[...] = jnp.where(lane == 0, zed, jnp.where(lane == 1, bulk, dens))
+    cols = jnp.where(lane == 0, zed, jnp.where(lane == 1, bulk, dens))
 
     lists = [info_ref[pl.ds(0, LANES, stride=3), :], info_ref[pl.ds(1, LANES, stride=3), :]]
     owners = info_ref[pl.ds(2, LANES, stride=3), :].astype(F32)
@@ -312,7 +312,7 @@
         chosen = source == (lane & 15).astype(F32)
         return jnp.sum(jnp.where(chosen, value, 0.0), axis=0, keepdims=True)
 
-    row_ref[...] = jnp.broadcast_to(rows_of(me), (8, LANES)).astype(I32)
+    place_ref[...] = jnp.where(rows_of(me) == sub.astype(F32), 1.0, 0.0).astype(BF16)
     scr[...] = jnp.full((8, LANES), -1.0, F32)
     nbr_all = nbr_ref[...]
     away_all = ((nbr_all >> 7) != me) & (wall_ref[...] == 0)
@@ -332,6 +332,13 @@
             hot_ref[rows, side * LANES : (side + 1) * LANES] = jnp.where(hit, 1.0, 0.0).astype(BF16)
             codes.append(column(orient_ref[face : face + 1, :].astype(F32), diag).astype(I32))
             aways.append(wanted)
+            wall = column(jnp.where(is_wall, 1.0, 0.0), diag) > 0.0
+            spot = column((nbr & 127).astype(F32), diag)
+            far = wanted >= 0.0
+            local = jnp.where(far | wall, 0.0, jnp.where(spot == lane.astype(F32), 1.0, 0.0))
+            near_ref[rows, side * LANES : (side + 1) * LANES] = local.astype(BF16)
+            cols = jnp.where(lane == 8 + face, spot, cols)
+            cols = jnp.where(lane == 16 + face, jnp.where(wall, -1.0, jnp.where(far, 1.0, 0.0)), cols)
         code = jnp.where(low_half, codes[0], codes[1])
         a, b = (lane >> 3) & 7, lane & 7
         swap = code >= 4
@@ -350,6 +357,7 @@
             group, v = top + ((b2 & 3) ^ (h * 3)), (a2 & 1) * 2 + (b2 >> 2)
         is_far = jnp.where(low_half, aways[0], aways[1]) >= 0.0
         index_ref[rows, :] = h * 64 + jnp.where(is_far, v * 16 + group, a2 * 8 + b2)
+    cols_ref[...] = cols
 
 
 SHIFT_A, SHIFT_B = (3, 9)
@@ -359,7 +367,7 @@
     return (i & 3) ^ ((i >> 2) & 1) * (4 * SHIFT_A) ^ (i >> 3) * (4 * SHIFT_B)
 
 
-def forward_kernel(me_ref, spot_ref, in_ref, label_ref, column_ref, out_ref, zed_ref, held, made, sem):
+def forward_kernel(me_ref, spot_ref, owner_ref, in_ref, label_ref, column_ref, cols_ref, out_ref, zed_ref, held):
     for number in range(DEVS // 2):
         start = spot_ref[2048 + number] * 33
         for j in range(32):
@@ -367,7 +375,17 @@
     shape = (LANES, LANES)
     lane = iota(shape, 1)
     zeds = in_ref[pl.ds(32, LANES, stride=33), :]
-    zed_ref[...] = zeds
+    me = me_ref[0]
+    own = in_ref[pl.ds(me * 33 + 32, 1), :]
+    for axis in range(3):
+        values = []
+        for face in (2 * axis, 2 * axis + 1):
+            other = in_ref[pl.ds(jnp.maximum(owner_ref[face * LANES + me], 0) * 33 + 32, 1), :]
+            kind = cols_ref[:, 16 + face : 17 + face]
+            hit = cols_ref[:, 8 + face : 9 + face] == lane.astype(F32)
+            value = jnp.where(hit, jnp.where(kind > 0.0, other, own), 0.0)
+            values.append(jnp.where(kind < 0.0, -1.0, jnp.sum(value, axis=1, keepdims=True)))
+        zed_ref[axis * LANES : axis * LANES + LANES, :] = jnp.where(lane < 64, values[0], values[1])
     zed = jnp.take_along_axis(zeds, label_ref[...], axis=1)
     me = me_ref[0]
     g3, g2, g1, g0 = (me >> 3) & 1, (me >> 2) & 1, (me >> 1) & 1, me & 1
@@ -426,44 +444,10 @@
         pick = jnp.concatenate([jnp.where(upper, 1.0, 0.0), jnp.where(lower, 1.0, 0.0)], axis=1)
         table = jnp.concatenate([jnp.where(low_half, wave, 0.0), jnp.where(low_half, 0.0, wave)], axis=0)
         halos.append(pick_dot(pick, table))
-    copies = []
-    for part in range(4):
-        base = part * 32
-        for target in range(base, base + 32):
-            made[target * 19 : target * 19 + 16, :] = held[target * 17 : target * 17 + 16, :]
-        for axis in range(3):
-            made[pl.ds(base * 19 + 16 + axis, 32, stride=19), :] = halos[axis][base : base + 32, :]
-        rows = pl.ds(base * 19, 608)
-        copies.append(pltpu.make_async_copy(made.at[rows], out_ref.at[rows], sem.at[part]))
-        copies[-1].start()
-    for copy in copies:
-        copy.wait()
-
-
-def across_kernel(me_ref, owner_ref, zed_ref, nbr_ref, wall_ref, row_ref, out_ref, near_ref, place_ref):
-    shape = (LANES, LANES)
-    lane = iota(shape, 1)
-    diag = iota(shape, 0) == lane
-    me = me_ref[0]
-    own = zed_ref[pl.ds(me, 1), :]
+    for target in range(DEVS):
+        out_ref[target * 19 : target * 19 + 16, :] = held[target * 17 : target * 17 + 16, :]
     for axis in range(3):
-        rows = slice(axis * LANES, axis * LANES + LANES)
-        zeds = []
-        for side in range(2):
-            face = 2 * axis + side
-            other = zed_ref[pl.ds(jnp.maximum(owner_ref[face * LANES + me], 0), 1), :]
-            nbr = nbr_ref[face : face + 1, :]
-            is_wall = wall_ref[face : face + 1, :] == 1
-            remote = ((nbr >> 7) != me) & jnp.logical_not(is_wall)
-            far = column(jnp.where(remote, 1.0, 0.0), diag) > 0.0
-            spot = column((nbr & 127).astype(F32), diag) == lane.astype(F32)
-            wall = column(jnp.where(is_wall, 1.0, 0.0), diag) > 0.0
-            value = jnp.where(spot, jnp.where(far, other, own), 0.0)
-            zeds.append(jnp.where(wall, -1.0, jnp.sum(value, axis=1, keepdims=True)))
-            local = jnp.where(far | wall, 0.0, jnp.where(spot, 1.0, 0.0))
-            near_ref[rows, side * LANES : (side + 1) * LANES] = local.astype(BF16)
-        out_ref[rows, :] = jnp.where(lane < 64, zeds[0], zeds[1])
-    place_ref[...] = jnp.where(row_ref[0:1, :] == iota(shape, 0), 1.0, 0.0).astype(BF16)
+        out_ref[pl.ds(16 + axis, LANES, stride=19), :] = halos[axis]
 
 
 def exchange_lanes(arrays):
@@ -654,19 +638,23 @@
     nbr, wall, orient = away(neighbours), away(wall_flags), away(orientation)
     state = old_state.reshape(256, 4, 4, LANES).transpose(0, 2, 1, 3).reshape(4096, LANES)
 
-    info, pos = pl.pallas_call(
+    info, pos, zed = pl.pallas_call(
         order_kernel,
-        in_specs=[sm()] + [vm()] * 3,
-        out_specs=[vm()] * 2,
-        out_shape=[shaped((384, LANES), I32), plain((2, LANES), I32)],
+        in_specs=[sm()] + [vm()] * 5,
+        out_specs=[vm()] * 3,
+        out_shape=[
+            shaped((384, LANES), I32),
+            shaped((2, LANES), I32),
+            shaped((8, LANES)),
+        ],
         scratch_shapes=[pltpu.VMEM((8, LANES), F32)],
         name="order",
         compiler_params=GRANT,
-    )(me, away(dest), nbr, wall)
+    )(me, away(dest), nbr, wall, bulk, dens)
     heard = exchange(info, 3)
     pieces = pl.pallas_call(
         pack_kernel,
-        in_specs=[sm(), pl.BlockSpec(memory_space=pl.ANY), vm(), vm()],
+        in_specs=[sm(), pl.BlockSpec(memory_space=pl.ANY), vm()],
         out_specs=pl.BlockSpec(memory_space=pl.ANY),
         out_shape=HBM((4224, LANES), F32),
         scratch_shapes=[
@@ -677,49 +665,38 @@
         ],
         name="pack",
         compiler_params=GRANT,
-    )(pos, away(state), bulk, dens)
+    )(pos.reshape(256), away(state), near(zed))
     spread = exchange(pieces, 33)
-    spots, owners, blocks, rows, labels, cols, index, far = pl.pallas_call(
+    spots, owners, blocks, labels, cols, index, far, close, place = pl.pallas_call(
         table_kernel,
         in_specs=[sm()] + [vm()] * 6,
-        out_specs=[vm()] * 8,
+        out_specs=[vm()] * 9,
         out_shape=[
             shaped((24, LANES), I32),
             shaped((8, LANES), I32),
             shaped((LANES, LANES)),
-            shaped((8, LANES), I32),
             shaped((LANES, LANES), I32),
             shaped((LANES, LANES)),
             shaped((384, LANES), I32),
             shaped((384, 2 * LANES), BF16),
+            shaped((384, 2 * LANES), BF16),
+            shaped((LANES, LANES), BF16),
         ],
         scratch_shapes=[pltpu.VMEM((LANES, LANES), I32), pltpu.VMEM((8, LANES), F32)],
         name="table",
         compiler_params=GRANT,
     )(me, near(heard), nbr, wall, orient, bulk, dens)
     owners = owners.reshape(1024)
-    passed, zeds = pl.pallas_call(
+    passed, zed_out = pl.pallas_call(
         forward_kernel,
-        in_specs=[sm()] * 2 + [vm()] * 3,
-        out_specs=[pl.BlockSpec(memory_space=pl.ANY), vm()],
-        out_shape=[HBM((2432, LANES), F32), shaped((LANES, LANES))],
-        scratch_shapes=[
-            pltpu.VMEM((2176, LANES), F32),
-            pltpu.VMEM((2432, LANES), F32),
-            pltpu.SemaphoreType.DMA((4,)),
-        ],
+        in_specs=[sm()] * 3 + [vm()] * 4,
+        out_specs=[vm()] * 2,
+        out_shape=[shaped((2432, LANES)), shaped((384, LANES))],
+        scratch_shapes=[pltpu.VMEM((2176, LANES), F32)],
         name="forward",
         compiler_params=GRANT,
-    )(me, spots.reshape(3072), near(spread), near(labels), near(blocks))
+    )(me, spots.reshape(3072), owners, near(spread), near(labels), near(blocks), near(cols))
     arrived = exchange(passed, 19)
-    zed_out, close, place = pl.pallas_call(
-        across_kernel,
-        in_specs=[sm()] * 2 + [vm()] * 4,
-        out_specs=[vm()] * 3,
-        out_shape=[shaped((384, LANES)), shaped((384, 2 * LANES), BF16), shaped((LANES, LANES), BF16)],
-        name="across",
-        compiler_params=GRANT,
-    )(me, owners, near(zeds), nbr, wall, near(rows))
     result = pl.pallas_call(
         final_kernel,
         in_specs=[vm()] * 10,

time: 94.2 us -> 92 us (0.977)
  blocking collectives: 0 us -> 25.2 us
  waiting for transfers between devices: 56.1 us -> 33 us
  starting transfers between devices: 20.6 us -> 15.8 us
    all_to_all x0 -> x1, blocking collectives: none -> 25.2 us  [exchange(): lax.all_to_all(blocks, AXES, split_axis=0, concat_axis=0, tiled=True)]
    all_to_all x3 -> x2, waiting for transfers between devices: 56.1 us -> 33 us  [exchange(): lax.all_to_all(blocks, AXES, split_axis=0, concat_axis=0, tiled=True)]
    all_to_all x3 -> x2, starting transfers between devices: 20.6 us -> 15.8 us  [exchange(): lax.all_to_all(blocks, AXES, split_axis=0, concat_axis=0, tiled=True)]
    pallas_call x1, Pallas kernels: 2.15 us -> 5.02 us  [body(): pl.pallas_call(pack_kernel, in_specs=[sm(), pl.BlockSpec(memory_space=pl....]
    pallas_call x3 -> x2, Pallas kernels: 7.23 us -> 4.91 us  [the longest x1 3.21 us: body(): pl.pallas_call(forward_kernel, in_specs=[sm()] * 3 + [vm()] * 4, out_spec...]
  transfers between devices with their start and end apart: 3 -> 2, of which waited for: 3 -> 2; matrix products, arithmetic and copies ran while one was open for 0% -> 0% of each run, Pallas kernels for 8% -> 9%
where the time goes in v7:
time: 92 us; the launch traced here: 91.6 us
  waiting for transfers between devices  33 us (36%)
  blocking collectives  25.2 us (27%)
  Pallas kernels  17.6 us (19%)
  starting transfers between devices  15.8 us (17%)
    all_to_all x2, waiting for transfers between devices, exchange(): lax.all_to_all(blocks, AXES, split_axis=0, concat_axis=0, tiled=True)  33 us
    all_to_all x1, blocking collectives, exchange(): lax.all_to_all(blocks, AXES, split_axis=0, concat_axis=0, tiled=True)  25.2 us
    all_to_all x2, starting transfers between devices, exchange(): lax.all_to_all(blocks, AXES, split_axis=0, concat_axis=0, tiled=True)  15.8 us
    pallas_call x1, Pallas kernels, body(): pl.pallas_call(pack_kernel, in_specs=[sm(), pl.BlockSpec(memory_space=pl....  5.02 us
    pallas_call x1, Pallas kernels, body(): pl.pallas_call(final_kernel, in_specs=[vm()] * 10, out_specs=pl.BlockSpec...  4.02 us
    pallas_call x1, Pallas kernels, body(): pl.pallas_call(table_kernel, in_specs=[sm()] + [vm()] * 6, out_specs=[vm(...  3.67 us
    pallas_call x1, Pallas kernels, body(): pl.pallas_call(forward_kernel, in_specs=[sm()] * 3 + [vm()] * 4, out_spec...  3.21 us
  transfers between devices with their start and end apart: 2, of which 2 were waited for; matrix products, arithmetic and copies ran while one was open for 0% of the time, Pallas kernels for 9%

profile of v7, /device:TPU:1, one launch (start us, length us, event | category | flops | bytes accessed | tf_op | source)
XLA Modules:
  0.0 91.6 jit_solution(9620300256578882836)
XLA Ops:
  0.0 1.7 %order.1 = (s32[384,128]{1,0:T(8,128)}, s32[2,128]{1,0:T(2,128)S(1)}, f32[8,128]{1,0:T(8,128)S(1)}) custom-call(s32[1]{0:T(128)} %bitcast.me_ref, s32[2,128]{1,0:T(2,128)} %bitcast.36, s32[6,128]{1,0:T(8,128)} %nbr_ref.3, s32[6,128]{1,0:T(8,128)} %wall_ref.3, f32[1,128]{1,0:T(1,128)} %bitcast.32, f32[1,128]{1,0:T(1,128)} %bitcast.34), custom_call_target="tpu_custom_call" | custom-call | tf_op jit(solution)/shard_map/order/pallas_call | solution.py:641
  1.7 11.5 %all-to-all-start = ((s32[128,3,1,128]{3,2,1,0:T(1,128)}), s32[128,3,1,128]{3,2,1,0:T(1,128)S(1)}, u32[]{:S(2)}, u32[]{:S(2)}) async-start(s32[128,3,1,128]{3,2,1,0:T(1,128)} %bitcast.4), calls=%async_computation | async-start | bytes 393216 | tf_op jit(solution)/shard_map/all_to_all | solution.py:630
  13.2 5.0 %pack.1 = f32[4224,128]{1,0:T(8,128)} custom-call(s32[256]{0:T(256)S(1)} %bitcast.29, f32[4096,128]{1,0:T(8,128)} %bitcast.31, f32[8,128]{1,0:T(8,128)S(1)} %get-tuple-element.23.zed_ref), custom_call_target="tpu_custom_call" | custom-call | tf_op jit(solution)/shard_map/pack/pallas_call | solution.py:655
  18.2 5.5 %all-to-all-done = s32[128,3,1,128]{3,2,1,0:T(1,128)S(1)} async-done(((s32[128,3,1,128]{3,2,1,0:T(1,128)}), s32[128,3,1,128]{3,2,1,0:T(1,128)S(1)}, u32[]{:S(2)}, u32[]{:S(2)}) %all-to-all-start) | async-done | bytes 196640 | tf_op jit(solution)/shard_map/all_to_all | solution.py:630
  23.7 4.3 %all-to-all-start.1 = ((f32[128,33,1,128]{3,2,1,0:T(1,128)}), f32[128,33,1,128]{3,2,1,0:T(1,128)S(1)}, u32[]{:S(2)}, u32[]{:S(2)}) async-start(f32[128,33,1,128]{3,2,1,0:T(1,128)} %bitcast.30), calls=%async_computation.1 | async-start | bytes 4325376 | tf_op jit(solution)/shard_map/all_to_all | solution.py:630
  28.0 3.7 %table.1 = (s32[24,128]{1,0:T(8,128)S(1)}, s32[8,128]{1,0:T(8,128)S(1)}, f32[128,128]{1,0:T(8,128)S(1)}, s32[128,128]{1,0:T(8,128)S(1)}, f32[128,128]{1,0:T(8,12...) custom-call(s32[1]{0:T(128)} %bitcast.me_ref, ...), custom_call_target="tpu_custom_call" | custom-call | tf_op jit(solution)/shard_map/table/pallas_call | solution.py:670
  31.7 27.5 %all-to-all-done.1 = f32[128,33,1,128]{3,2,1,0:T(1,128)S(1)} async-done(((f32[128,33,1,128]{3,2,1,0:T(1,128)}), f32[128,33,1,128]{3,2,1,0:T(1,128)S(1)}, u32[]{:S(2)}, u32[]{:S(2)}) %all-to-all-start.1) | async-done | bytes 2162720 | tf_op jit(solution)/shard_map/all_to_all | solution.py:630
  59.2 0.0 copy-start
  59.2 0.0 copy-start.1
  59.2 0.0 copy-start.2
  59.2 3.2 %forward.1 = (f32[2432,128]{1,0:T(8,128)S(1)}, f32[384,128]{1,0:T(8,128)S(1)}) custom-call(s32[1]{0:T(128)} %bitcast.me_ref, s32[3072]{0:T(1024)S(1)} %bitcast.27, s32[1024]{0:T(1024)S(1)} %bitcast.28, f32[4224,128]{1,0:T(8,128)S(1)} %bitcast.23, s32[128,128]{1,0:T(8,128)S(1)} %get-tuple-element.24.label_ref, f32[128,128]{1,0:T(8,128)S(1)} %get-tuple-element.25.column_ref, ...), custom_call_target="tpu_custom_call" | custom-call | tf_op jit(solution)/shard_map/forward/pallas_call | solution.py:690
  62.4 25.2 %all_to_all.15 = f32[128,19,1,128]{3,2,1,0:T(1,128)S(1)} all-to-all(f32[128,19,1,128]{3,2,1,0:T(1,128)S(1)} %bitcast.25), channel_id=1, replica_groups=mesh['grp'=4,'dev'=32] {'grp','dev'}, dimensions={0} | all-to-all | bytes 2490368 | tf_op jit(solution)/shard_map/all_to_all | solution.py:630
  87.6 0.0 copy-done
  87.6 0.0 copy-done.1
  87.6 0.0 copy-done.2
  87.6 4.0 %final.1 = f32[2048,128]{1,0:T(8,128)} custom-call(f32[2432,128]{1,0:T(8,128)S(1)} %bitcast.24, bf16[128,128]{1,0:T(8,128)(2,1)S(1)} %get-tuple-element.28.place_ref, f32[128,128]{1,0:T(8,128)S(1)} %get-tuple-element.26.cols_ref, f32[384,128]{1,0:T(8,128)S(1)} %get-tuple-element.29.zed_ref, bf16[384,256]{1,0:T(8,128)(2,1)S(1)} %get-tuple-element.30.near_ref, ...), custom_call_target="tpu_custom_call" | custom-call | tf_op jit(solution)/shard_map/final/pallas_call | solution.py:700
Async XLA Ops:
  1.7 22.0 %all-to-all-start = ((s32[128,3,1,128]{3,2,1,0:T(1,128)}), s32[128,3,1,128]{3,2,1,0:T(1,128)S(1)}, u32[]{:S(2)}, u32[]{:S(2)}) async-start(s32[128,3,1,128]{3,2,1,0:T(1,128)} %bitcast.4), calls=%async_computation | async-start | bytes 393216 | tf_op jit(solution)/shard_map/all_to_all | solution.py:630
  23.7 35.5 %all-to-all-start.1 = ((f32[128,33,1,128]{3,2,1,0:T(1,128)}), f32[128,33,1,128]{3,2,1,0:T(1,128)S(1)}, u32[]{:S(2)}, u32[]{:S(2)}) async-start(f32[128,33,1,128]{3,2,1,0:T(1,128)} %bitcast.30), calls=%async_computation.1 | async-start | bytes 4325376 | tf_op jit(solution)/shard_map/all_to_all | solution.py:630
  59.2 28.4 %copy-start = (bf16[768,128]{1,0:T(8,128)(2,1)S(1)}, bf16[768,128]{1,0:T(8,128)(2,1)}, u32[]{:S(2)}) copy-start(bf16[768,128]{1,0:T(8,128)(2,1)} %constant.18.clone.stack_ref) | copy-start | bytes 589828
  59.2 28.4 %copy-start.1 = (bf16[384,256]{1,0:T(8,128)(2,1)S(1)}, bf16[384,256]{1,0:T(8,128)(2,1)}, u32[]{:S(2)}) copy-start(bf16[384,256]{1,0:T(8,128)(2,1)} %constant.17.clone.side_ref) | copy-start | bytes 589828
  59.2 28.4 %copy-start.2 = (f32[32,128]{1,0:T(8,128)S(1)}, f32[32,128]{1,0:T(8,128)}, u32[]{:S(2)}) copy-start(f32[32,128]{1,0:T(8,128)} %constant.19.clone.coef_ref) | copy-start | bytes 49156

commit v8 on v7

--- a/solution.py
+++ b/solution.py
@@ -71,13 +71,15 @@
 SIDE, STACKED, COEF = derivative_tables()
 
 
-def three_parts(table):
+def six_parts(table):
     high = table.astype(jnp.bfloat16)
-    low = (table - high.astype(np.float32)).astype(jnp.bfloat16)
-    return np.concatenate([high, high, low], axis=0)
-
-
-SIDE3, STACKED3 = three_parts(SIDE), three_parts(STACKED)
+    rest = table - high.astype(np.float32)
+    middle = rest.astype(jnp.bfloat16)
+    low = (rest - middle.astype(np.float32)).astype(jnp.bfloat16)
+    return np.concatenate([high, high, high, middle, middle, low], axis=0)
+
+
+SIDE6, STACKED6 = six_parts(SIDE), six_parts(STACKED)
 
 
 def iota(shape, axis):
@@ -514,13 +516,13 @@
         jump = (wave_out - press + zed_out * norm) / (zed + zed_out)
         lift[rows, :] = jnp.where(zed_out < 0.0, norm, jump)
 
-    lane = iota((32, LANES), 1)
+    lane = iota((64, LANES), 1)
     low_half = lane < 64
     i2, j, k = lane >> 6, (lane >> 3) & 7, lane & 7
     on_y, on_z = (j == 0) | (j == 7), (k == 0) | (k == 7)
     copies = []
-    for part in range(4):
-        rows = slice(part * 32, part * 32 + 32)
+    for part in range(2):
+        rows = slice(part * 64, part * 64 + 64)
         zed, bulk, dens = cols_ref[rows, 0:1], cols_ref[rows, 1:2], cols_ref[rows, 2:3]
         by_bulk = -metric_scale * bulk
         by_dens = -(metric_scale / dens)
@@ -529,27 +531,21 @@
         piece = {}
         for field in range(4):
             for n4 in range(4):
-                start = (n4 * 4 + field) * LANES + part * 32
-                piece[field, n4] = state[start : start + 32, :]
+                start = (n4 * 4 + field) * LANES + part * 64
+                piece[field, n4] = state[start : start + 64, :]
         cut = []
-        for field in (0, 2, 3):
-            whole = jnp.concatenate([piece[field, n4] for n4 in range(4)], axis=0)
-            high = whole.astype(BF16)
-            cut.append((high, (whole - high.astype(F32)).astype(BF16)))
-        grad = jnp.dot(
-            jnp.concatenate([cut[0][0], cut[0][1], cut[0][0]], axis=1), side_ref[...], preferred_element_type=F32
-        )
-        across_div = jnp.dot(
-            jnp.concatenate([cut[1][0], cut[2][0], cut[1][1], cut[2][1], cut[1][0], cut[2][0]], axis=1),
-            stack_ref[...],
-            preferred_element_type=F32,
-        )
+        for fields in ((0,), (2, 3)):
+            whole = [jnp.concatenate([piece[field, n4] for n4 in range(4)], axis=0) for field in fields]
+            high, middle, low = split3(jnp.concatenate(whole, axis=1))
+            cut.append(jnp.concatenate([high, middle, low, high, middle, high], axis=1))
+        grad = jnp.dot(cut[0], side_ref[...], preferred_element_type=F32)
+        across_div = jnp.dot(cut[1], stack_ref[...], preferred_element_type=F32)
         swapped = {}
         for field in (0, 1):
             for n4 in range(4):
                 swapped[field, n4] = pltpu.roll(piece[field, n4], 64, 1)
-        jumps = [lift[axis * LANES + part * 32 : axis * LANES + part * 32 + 32, :] for axis in range(3)]
-        base = part * 544
+        jumps = [lift[axis * LANES + part * 64 : axis * LANES + part * 64 + 64, :] for axis in range(3)]
+        base = part * 1088
         for n4 in range(4):
             along = {}
             for field in (0, 1):
@@ -560,7 +556,7 @@
                     term = term + swapped[field, m4] * coef_ref[at + 1 : at + 2, :]
                     total = term if total is None else total + term
                 along[field] = total
-            block = slice(n4 * 32, n4 * 32 + 32)
+            block = slice(n4 * 64, n4 * 64 + 64)
             div = along[1] + across_div[block, :]
             grads = [along[0], grad[block, 0:LANES], grad[block, LANES:]]
             face_i = 2 * n4 + i2
@@ -586,12 +582,12 @@
                 if here is not None:
                     value = value + across * turn
                     total = here if total is None else total + here
-                loose[pl.ds(base + n4 * 4 + 1 + axis, 32, stride=17), :] = value
-            loose[pl.ds(base + n4 * 4, 32, stride=17), :] = by_bulk * div + up * total
-        for row in range(32):
-            at = (part * 32 + row) * 16
+                loose[pl.ds(base + n4 * 4 + 1 + axis, 64, stride=17), :] = value
+            loose[pl.ds(base + n4 * 4, 64, stride=17), :] = by_bulk * div + up * total
+        for row in range(64):
+            at = (part * 64 + row) * 16
             made[at : at + 16, :] = loose[base + row * 17 : base + row * 17 + 16, :]
-        window = pl.ds(part * 512, 512)
+        window = pl.ds(part * 1024, 1024)
         copies.append(pltpu.make_async_copy(made.at[window], out_ref.at[window], sem.at[part]))
         copies[-1].start()
     for copy in copies:
@@ -708,13 +704,13 @@
             pltpu.VMEM((384, LANES), F32),
             pltpu.VMEM((2176, LANES), F32),
             pltpu.VMEM((2048, LANES), F32),
-            pltpu.SemaphoreType.DMA((4,)),
+            pltpu.SemaphoreType.DMA((2,)),
         ],
         name="final",
         compiler_params=GRANT,
     )(
         near(arrived), near(place), near(cols), near(zed_out), near(close), near(far), near(index),
-        jnp.asarray(SIDE3), jnp.asarray(STACKED3), jnp.asarray(COEF),
+        jnp.asarray(SIDE6), jnp.asarray(STACKED6), jnp.asarray(COEF),
     )
     return result.reshape(128, 4, 4, LANES).transpose(0, 2, 1, 3).reshape(128, 4, 512)
 

time: 92 us -> 92 us (level)
  Pallas kernels: 17.6 us -> 14.6 us
  waiting for transfers between devices: 33 us -> 36 us
    pallas_call x1, Pallas kernels: 5.02 us -> 2.01 us  [body(): pl.pallas_call(pack_kernel, in_specs=[sm(), pl.BlockSpec(memory_space=pl....]
    all_to_all x2, waiting for transfers between devices: 33 us -> 36 us  [exchange(): lax.all_to_all(blocks, AXES, split_axis=0, concat_axis=0, tiled=True)]
  transfers between devices with their start and end apart: 2 -> 2, of which waited for: 2 -> 2; matrix products, arithmetic and copies ran while one was open for 0% -> 0% of each run, Pallas kernels for 9% -> 6%
where the time goes in v8:
time: 92 us; the launch traced here: 91.7 us
  waiting for transfers between devices  36 us (39%)
  blocking collectives  25.2 us (27%)
  starting transfers between devices  15.8 us (17%)
  Pallas kernels  14.6 us (16%)
    all_to_all x2, waiting for transfers between devices, exchange(): lax.all_to_all(blocks, AXES, split_axis=0, concat_axis=0, tiled=True)  36 us
    all_to_all x1, blocking collectives, exchange(): lax.all_to_all(blocks, AXES, split_axis=0, concat_axis=0, tiled=True)  25.2 us
    all_to_all x2, starting transfers between devices, exchange(): lax.all_to_all(blocks, AXES, split_axis=0, concat_axis=0, tiled=True)  15.8 us
    pallas_call x1, Pallas kernels, body(): pl.pallas_call(final_kernel, in_specs=[vm()] * 10, out_specs=pl.BlockSpec...  4.03 us
    pallas_call x1, Pallas kernels, body(): pl.pallas_call(table_kernel, in_specs=[sm()] + [vm()] * 6, out_specs=[vm(...  3.67 us
    pallas_call x1, Pallas kernels, body(): pl.pallas_call(forward_kernel, in_specs=[sm()] * 3 + [vm()] * 4, out_spec...  3.21 us
    pallas_call x1, Pallas kernels, body(): pl.pallas_call(pack_kernel, in_specs=[sm(), pl.BlockSpec(memory_space=pl....  2.01 us
  transfers between devices with their start and end apart: 2, of which 2 were waited for; matrix products, arithmetic and copies ran while one was open for 0% of the time, Pallas kernels for 6%

profile of v8, /device:TPU:1, one launch (start us, length us, event | category | flops | bytes accessed | tf_op | source)
XLA Modules:
  0.0 91.7 jit_solution(4477826658391308543)
XLA Ops:
  0.0 1.7 %order.1 = (s32[384,128]{1,0:T(8,128)}, s32[2,128]{1,0:T(2,128)S(1)}, f32[8,128]{1,0:T(8,128)S(1)}) custom-call(s32[1]{0:T(128)} %bitcast.me_ref, s32[2,128]{1,0:T(2,128)} %bitcast.36, s32[6,128]{1,0:T(8,128)} %nbr_ref.3, s32[6,128]{1,0:T(8,128)} %wall_ref.3, f32[1,128]{1,0:T(1,128)} %bitcast.32, f32[1,128]{1,0:T(1,128)} %bitcast.34), custom_call_target="tpu_custom_call" | custom-call | tf_op jit(solution)/shard_map/order/pallas_call | solution.py:637
  1.7 11.5 %all-to-all-start = ((s32[128,3,1,128]{3,2,1,0:T(1,128)}), s32[128,3,1,128]{3,2,1,0:T(1,128)S(1)}, u32[]{:S(2)}, u32[]{:S(2)}) async-start(s32[128,3,1,128]{3,2,1,0:T(1,128)} %bitcast.4), calls=%async_computation | async-start | bytes 393216 | tf_op jit(solution)/shard_map/all_to_all | solution.py:626
  13.2 2.0 %pack.1 = f32[4224,128]{1,0:T(8,128)} custom-call(s32[256]{0:T(256)S(1)} %bitcast.29, f32[4096,128]{1,0:T(8,128)} %bitcast.31, f32[8,128]{1,0:T(8,128)S(1)} %get-tuple-element.23.zed_ref), custom_call_target="tpu_custom_call" | custom-call | tf_op jit(solution)/shard_map/pack/pallas_call | solution.py:651
  15.2 8.5 %all-to-all-done = s32[128,3,1,128]{3,2,1,0:T(1,128)S(1)} async-done(((s32[128,3,1,128]{3,2,1,0:T(1,128)}), s32[128,3,1,128]{3,2,1,0:T(1,128)S(1)}, u32[]{:S(2)}, u32[]{:S(2)}) %all-to-all-start) | async-done | bytes 196640 | tf_op jit(solution)/shard_map/all_to_all | solution.py:626
  23.7 4.3 %all-to-all-start.1 = ((f32[128,33,1,128]{3,2,1,0:T(1,128)}), f32[128,33,1,128]{3,2,1,0:T(1,128)S(1)}, u32[]{:S(2)}, u32[]{:S(2)}) async-start(f32[128,33,1,128]{3,2,1,0:T(1,128)} %bitcast.30), calls=%async_computation.1 | async-start | bytes 4325376 | tf_op jit(solution)/shard_map/all_to_all | solution.py:626
  28.0 3.7 %table.1 = (s32[24,128]{1,0:T(8,128)S(1)}, s32[8,128]{1,0:T(8,128)S(1)}, f32[128,128]{1,0:T(8,128)S(1)}, s32[128,128]{1,0:T(8,128)S(1)}, f32[128,128]{1,0:T(8,12...) custom-call(s32[1]{0:T(128)} %bitcast.me_ref, ...), custom_call_target="tpu_custom_call" | custom-call | tf_op jit(solution)/shard_map/table/pallas_call | solution.py:666
  31.7 27.5 %all-to-all-done.1 = f32[128,33,1,128]{3,2,1,0:T(1,128)S(1)} async-done(((f32[128,33,1,128]{3,2,1,0:T(1,128)}), f32[128,33,1,128]{3,2,1,0:T(1,128)S(1)}, u32[]{:S(2)}, u32[]{:S(2)}) %all-to-all-start.1) | async-done | bytes 2162720 | tf_op jit(solution)/shard_map/all_to_all | solution.py:626
  59.2 0.0 copy-start
  59.2 0.0 copy-start.1
  59.2 0.0 copy-start.2
  59.2 3.2 %forward.1 = (f32[2432,128]{1,0:T(8,128)S(1)}, f32[384,128]{1,0:T(8,128)S(1)}) custom-call(s32[1]{0:T(128)} %bitcast.me_ref, s32[3072]{0:T(1024)S(1)} %bitcast.27, s32[1024]{0:T(1024)S(1)} %bitcast.28, f32[4224,128]{1,0:T(8,128)S(1)} %bitcast.23, s32[128,128]{1,0:T(8,128)S(1)} %get-tuple-element.24.label_ref, f32[128,128]{1,0:T(8,128)S(1)} %get-tuple-element.25.column_ref, ...), custom_call_target="tpu_custom_call" | custom-call | tf_op jit(solution)/shard_map/forward/pallas_call | solution.py:686
  62.4 25.2 %all_to_all.15 = f32[128,19,1,128]{3,2,1,0:T(1,128)S(1)} all-to-all(f32[128,19,1,128]{3,2,1,0:T(1,128)S(1)} %bitcast.25), channel_id=1, replica_groups=mesh['grp'=4,'dev'=32] {'grp','dev'}, dimensions={0} | all-to-all | bytes 2490368 | tf_op jit(solution)/shard_map/all_to_all | solution.py:626
  87.6 0.0 copy-done
  87.6 0.0 copy-done.1
  87.6 0.0 copy-done.2
  87.6 4.0 %final.1 = f32[2048,128]{1,0:T(8,128)} custom-call(f32[2432,128]{1,0:T(8,128)S(1)} %bitcast.24, bf16[128,128]{1,0:T(8,128)(2,1)S(1)} %get-tuple-element.28.place_ref, f32[128,128]{1,0:T(8,128)S(1)} %get-tuple-element.26.cols_ref, f32[384,128]{1,0:T(8,128)S(1)} %get-tuple-element.29.zed_ref, bf16[384,256]{1,0:T(8,128)(2,1)S(1)} %get-tuple-element.30.near_ref, ...), custom_call_target="tpu_custom_call" | custom-call | tf_op jit(solution)/shard_map/final/pallas_call | solution.py:696
Async XLA Ops:
  1.7 22.0 %all-to-all-start = ((s32[128,3,1,128]{3,2,1,0:T(1,128)}), s32[128,3,1,128]{3,2,1,0:T(1,128)S(1)}, u32[]{:S(2)}, u32[]{:S(2)}) async-start(s32[128,3,1,128]{3,2,1,0:T(1,128)} %bitcast.4), calls=%async_computation | async-start | bytes 393216 | tf_op jit(solution)/shard_map/all_to_all | solution.py:626
  23.7 35.5 %all-to-all-start.1 = ((f32[128,33,1,128]{3,2,1,0:T(1,128)}), f32[128,33,1,128]{3,2,1,0:T(1,128)S(1)}, u32[]{:S(2)}, u32[]{:S(2)}) async-start(f32[128,33,1,128]{3,2,1,0:T(1,128)} %bitcast.30), calls=%async_computation.1 | async-start | bytes 4325376 | tf_op jit(solution)/shard_map/all_to_all | solution.py:626
  59.2 28.4 %copy-start = (bf16[1536,128]{1,0:T(8,128)(2,1)S(1)}, bf16[1536,128]{1,0:T(8,128)(2,1)}, u32[]{:S(2)}) copy-start(bf16[1536,128]{1,0:T(8,128)(2,1)} %constant.18.clone.stack_ref) | copy-start | bytes 1179652
  59.2 28.4 %copy-start.1 = (bf16[768,256]{1,0:T(8,128)(2,1)S(1)}, bf16[768,256]{1,0:T(8,128)(2,1)}, u32[]{:S(2)}) copy-start(bf16[768,256]{1,0:T(8,128)(2,1)} %constant.17.clone.side_ref) | copy-start | bytes 1179652
  59.2 28.4 %copy-start.2 = (f32[32,128]{1,0:T(8,128)S(1)}, f32[32,128]{1,0:T(8,128)}, u32[]{:S(2)}) copy-start(f32[32,128]{1,0:T(8,128)} %constant.19.clone.coef_ref) | copy-start | bytes 49156
